TPU v7x, 32 devices: a whole 2x2x4 slice. The times are simulated.
32 devices in a mesh: dp: 8 (over y, x, core), tensor: 4 (over z).
Axes of the slice: x: 2, y: 2, z: 4, core: 2. Of those that a mesh axis runs over, the one named last changes fastest.
Arguments:
- frames: bfloat16 [1024, 4, 84, 84], P(('dp', 'tensor')), may hold values from 0 to 1
- counts: int32 [4, 8], replicated, may hold values from 1 to 32, 128 in all within a row
- slot_ids: int32 [8, 64], P('dp'), may hold values from 0 to 127, as said below
- reset_flags: int32 [8, 128], P('dp'), may hold values 0 or 1
- hidden_state: float32 [2048, 1024], P('tensor', 'dp'), may hold values from -1 to 1
- cell_state: float32 [2048, 1024], P('tensor', 'dp'), may hold values from -6 to 6
- conv_first: bfloat16 [16, 4, 3, 3], replicated, may hold values from -1.5 to 1.5
- conv_second: bfloat16 [32, 16, 3, 3], replicated, may hold values from -0.75 to 0.75
- conv_third: bfloat16 [32, 32, 3, 3], replicated, may hold values from -0.5 to 0.5
- res_first: bfloat16 [32, 32, 3, 3], replicated, may hold values from -0.5 to 0.5
- res_second: bfloat16 [32, 32, 3, 3], replicated, may hold values from -0.5 to 0.5
- projection: bfloat16 [256, 3872], replicated, may hold values from -0.125 to 0.125
- input_weight: bfloat16 [4, 2048, 256], P(None, 'tensor'), may hold values from -0.375 to 0.375
- recur_weight: bfloat16 [4, 2048, 2048], P(None, 'tensor'), may hold values from -0.125 to 0.125
- gate_bias: float32 [4, 2048], P(None, 'tensor'), may hold values from -3 to 3
- head_weight: bfloat16 [19, 2048], P(None, 'tensor'), may hold values from -0.125 to 0.125
Outputs:
- policy_out: float32 [19, 1024], P(None, ('dp', 'tensor'))
- hidden_after: float32 [2048, 1024], P('tensor', 'dp')
- cell_after: float32 [2048, 1024], P('tensor', 'dp')
Inputs may be any that keep to these rules, and one draw needn't show every extreme that they name: Arrival rows fill the first counts[t, a] slots of their device; each row of counts sums to 128. `slot_ids`: the entries of one dp index are distinct.
All inputs are finite; a program needn't handle non-finite values. No bound on the sum of `reset_flags` on one device may be relied on, other than what follows from the above.
Results may differ from a plain program's by a relative error of at most 0.008.
Values may be sent and summed in bfloat16 or wider, within the bound.
No kernel may reach another device: no remote copies, remote signals or barrier semaphores. Data moves between devices by JAX's collectives and lax.ppermute only.
A program may use at most 128 MiB of HBM per device.

v0:
```python
import jax
import jax.numpy as jnp
from jax import lax
from jax.sharding import PartitionSpec as P


def conv_same(inputs, kernel):
    return lax.conv_general_dilated(
        inputs,
        kernel,
        (1, 1),
        "SAME",
        dimension_numbers=("NCHW", "OIHW", "NCHW"),
        preferred_element_type=jnp.float32,
    )


def pooled(inputs):
    return lax.reduce_window(inputs, -jnp.inf, lax.max, (1, 1, 3, 3), (1, 1, 2, 2), "SAME")


def encode(images, kernels, projection):
    conv_first, conv_second, conv_third, res_first, res_second = kernels
    section_one = jax.nn.relu(pooled(conv_same(images, conv_first))).astype(jnp.bfloat16)
    section_two = jax.nn.relu(pooled(conv_same(section_one, conv_second))).astype(jnp.bfloat16)
    section_three = pooled(conv_same(section_two, conv_third)).astype(jnp.bfloat16)
    residual_in = jax.nn.relu(conv_same(jax.nn.relu(section_three), res_first)).astype(jnp.bfloat16)
    encoded_map = jax.nn.relu(
        section_three.astype(jnp.float32) + conv_same(residual_in, res_second)
    ).astype(jnp.bfloat16)
    flattened = encoded_map.reshape(encoded_map.shape[0], -1)
    product = lax.dot_general(
        projection, flattened, (((1,), (1,)), ((), ())), preferred_element_type=jnp.float32
    )
    return jax.nn.relu(product).astype(jnp.bfloat16)


def body(
    frames,
    counts,
    slot_ids,
    reset_flags,
    hidden_state,
    cell_state,
    conv_first,
    conv_second,
    conv_third,
    res_first,
    res_second,
    projection,
    input_weight,
    recur_weight,
    gate_bias,
    head_weight,
):
    dp_count = lax.axis_size("dp")
    tensor_count = lax.axis_size("tensor")
    dp_index = lax.axis_index("dp")
    tensor_index = lax.axis_index("tensor")
    kernels = (conv_first, conv_second, conv_third, res_first, res_second)
    capacity = frames.shape[0]
    pair_depth = capacity // dp_count
    per_device = slot_ids.shape[1] // tensor_count
    tallies = lax.dynamic_index_in_dim(counts, tensor_index, 0, keepdims=False)
    starts = jnp.cumsum(tallies, dtype=jnp.int32) - tallies
    range_ends = starts + tallies
    own_start = lax.dynamic_index_in_dim(starts, dp_index, 0, keepdims=False)
    own_count = lax.dynamic_index_in_dim(tallies, dp_index, 0, keepdims=False)
    peer_index = jnp.arange(dp_count, dtype=jnp.int32)
    levels = jnp.arange(pair_depth, dtype=jnp.int32)
    send_rows = ((peer_index[:, None] - own_start) % dp_count + levels[None, :] * dp_count).reshape(
        -1
    )
    send_live = send_rows < own_count
    send_safe = jnp.minimum(send_rows, capacity - 1)
    balanced_ranks = jnp.arange(per_device, dtype=jnp.int32) * dp_count + dp_index
    source = jnp.sum((range_ends[:, None] <= balanced_ranks[None, :]).astype(jnp.int32), axis=0)
    offset = balanced_ranks - jnp.take(starts, source)
    take_slots = source * pair_depth + offset // dp_count
    outgoing = jnp.where(
        send_live[:, None, None, None],
        jnp.take(frames, send_safe, axis=0),
        jnp.zeros((), jnp.bfloat16),
    )
    incoming = lax.all_to_all(outgoing, "dp", split_axis=0, concat_axis=0, tiled=True)
    features = encode(jnp.take(incoming, take_slots, axis=0), kernels, projection)
    chosen = slot_ids[0]
    keep_state = (1 - jnp.take(reset_flags[0], chosen)).astype(jnp.float32)
    prev_hidden = jnp.take(hidden_state, chosen, axis=1) * keep_state[None, :]
    prev_cell = jnp.take(cell_state, chosen, axis=1) * keep_state[None, :]
    all_features, all_hidden = (
        lax.all_gather(features, "tensor", axis=1, tiled=True),
        lax.all_gather(prev_hidden.astype(jnp.bfloat16), "tensor", axis=0, tiled=True),
    )
    hidden_share = hidden_state.shape[0]
    gate_sums = jnp.dot(
        input_weight.reshape(4 * hidden_share, -1), all_features, preferred_element_type=jnp.float32
    )
    gate_sums = gate_sums + jnp.dot(
        recur_weight.reshape(4 * hidden_share, -1), all_hidden, preferred_element_type=jnp.float32
    )
    gate_sums = (gate_sums + gate_bias.reshape(4 * hidden_share, 1)).reshape(4, hidden_share, -1)
    next_cell = jax.nn.sigmoid(gate_sums[1]) * prev_cell + jax.nn.sigmoid(gate_sums[0]) * jnp.tanh(
        gate_sums[2]
    )
    next_hidden = jax.nn.sigmoid(gate_sums[3]) * jnp.tanh(next_cell)
    hidden_after = hidden_state.at[:, chosen].set(next_hidden)
    cell_after = cell_state.at[:, chosen].set(next_cell)
    partial_heads = jnp.dot(
        head_weight, next_hidden.astype(jnp.bfloat16), preferred_element_type=jnp.float32
    )
    totals = lax.psum(partial_heads, "tensor")
    own_heads = lax.dynamic_slice_in_dim(totals, tensor_index * per_device, per_device, 1)
    back_rows = (dp_index - starts[:, None]) % dp_count + levels[None, :] * dp_count
    back_live = (back_rows < tallies[:, None]).reshape(-1)
    back_place = jnp.minimum((starts[:, None] + back_rows) // dp_count, per_device - 1).reshape(-1)
    outgoing_heads = jnp.where(back_live[None, :], jnp.take(own_heads, back_place, axis=1), 0.0)
    returned = lax.all_to_all(outgoing_heads, "dp", split_axis=1, concat_axis=1, tiled=True)
    arrivals = jnp.arange(capacity, dtype=jnp.int32)
    home_slots = (own_start + arrivals) % dp_count * pair_depth + arrivals // dp_count
    policy_out = jnp.where(
        (arrivals < own_count)[None, :], jnp.take(returned, home_slots, axis=1), 0.0
    )
    return (policy_out, hidden_after, cell_after)


def solution(mesh):
    return jax.shard_map(
        body,
        mesh=mesh,
        in_specs=(
            P(("dp", "tensor"), None, None, None),
            P(),
            P("dp", None),
            P("dp", None),
            P("tensor", "dp"),
            P("tensor", "dp"),
            P(),
            P(),
            P(),
            P(),
            P(),
            P(),
            P(None, "tensor", None),
            P(None, "tensor", None),
            P(None, "tensor"),
            P(None, "tensor"),
        ),
        out_specs=(P(None, ("dp", "tensor")), P("tensor", "dp"), P("tensor", "dp")),
        check_vma=False,
    )
```

profile of v0, /device:TPU:0, one launch (start us, length us, event | category | flops | bytes accessed | tf_op | source)
XLA Modules:
  0.0 190.8 jit_solution(4338175990484992727)
XLA Ops:
  0.6 0.0 copy-start
  0.7 0.8 fusion.61
  1.5 0.2 reduce-window.7
  1.7 0.7 and_select_fusion.9
  2.4 0.6 dynamic_slice.16
  3.0 0.7 and_select_fusion.6
  3.6 0.1 add_add_fusion
  3.7 0.1 min.44
  3.8 0.1 min.43
  3.9 1.3 dynamic_slice.14
  5.2 0.7 add_compare_fusion.1
  5.9 0.1 lt.199
  6.0 4.3 %gather_fusion.1 = bf16[32,4,84,84]{3,1,2,0:T(4,128)(2,1)} fusion(bf16[32,4,84,84]{3,1,2,0:T(4,128)(2,1)S(1)} %copy-done, s32[1024]{0:T(1024)S(1)} %pad_clamp_fusion.5), kind=kCustom, calls=%fused_computation.3 | custom fusion | bytes 3612800 | tf_op jit(solution)/shard_map/jit(_take)/gather | solution.py:82
  10.3 4.8 %select_select_fusion = bf16[32,4,84,84]{3,1,2,0:T(4,128)(2,1)} fusion(bf16[32,4,84,84]{3,1,2,0:T(4,128)(2,1)} %gather_fusion.1, pred[32]{0:T(512)(128)(4,1)S(1)} %compare_and_fusion.2, pred[32]{0:T(512)(128)(4,1)S(1)} %lt.199), kind=kLoop, calls=%fused_computation.14 | loop fusion | flops 1806336 | bytes 3612736 | tf_op jit(solution)/shard_map/jit(_where)/select_n | solution.py:80
  15.2 5.3 %all-to-all-start = ((bf16[32,4,84,84]{3,1,2,0:T(4,128)(2,1)}), bf16[32,4,84,84]{3,1,2,0:T(4,128)(2,1)}, u32[]{:S(2)}, u32[]{:S(2)}) async-start(bf16[32,4,84,84]{3,1,2,0:T(4,128)(2,1)} %select_select_fusion), calls=%async_computation | async-start | bytes 5505024 | tf_op jit(solution)/shard_map/all_to_all | solution.py:85
  20.6 0.1 convert_reduce_fusion
  20.7 0.7 gather_fusion
  21.3 0.8 gather_fusion.3
  22.1 0.0 copy-start.8
  22.1 0.1 copy.40
  22.3 0.1 copy.41
  22.5 0.7 gather_fusion.6
  23.1 0.7 gather_fusion.7
  23.8 0.1 add.441
  23.9 0.1 fusion.33
  24.0 15.7 %all_gather.7 = bf16[2048,64]{0,1:T(8,128)(2,1)} all-gather(bf16[512,64]{0,1:T(8,128)(2,1)S(1)} %fusion.33), channel_id=1, replica_groups=mesh['dp'=8,'tensor'=4] {'tensor'}, dimensions={0}, use_global_device_ids=true | all-gather | bytes 327680 | tf_op jit(solution)/shard_map/all_gather | solution.py:93
  39.7 0.7 fusion.57
  40.5 13.7 %all-to-all-done = bf16[32,4,84,84]{3,1,2,0:T(4,128)(2,1)} async-done(((bf16[32,4,84,84]{3,1,2,0:T(4,128)(2,1)}), bf16[32,4,84,84]{3,1,2,0:T(4,128)(2,1)}, u32[]{:S(2)}, u32[]{:S(2)}) %all-to-all-start) | async-done | bytes 1806368 | tf_op jit(solution)/shard_map/all_to_all | solution.py:85
  54.2 3.5 %gather_fusion.2 = bf16[16,4,84,84]{3,1,2,0:T(4,128)(2,1)S(1)} fusion(bf16[32,4,84,84]{3,1,2,0:T(4,128)(2,1)} %all-to-all-done, s32[1024]{0:T(1024)S(1)} %pad_clamp_fusion.4), kind=kCustom, calls=%fused_computation.4 | custom fusion | bytes 1806400 | tf_op jit(solution)/shard_map/jit(_take)/gather | solution.py:86
  57.8 0.7 broadcast_select_fusion
  58.4 0.0 copy-start.18
  58.4 7.6 %copy.38 = bf16[16,4,84,84]{0,1,3,2:T(4,128)(2,1)} copy(bf16[16,4,84,84]{3,1,2,0:T(4,128)(2,1)S(1)} %broadcast_select_fusion) | data formatting | bytes 1806336 | tf_op jit(solution)/shard_map/jit(_take)/select_n | solution.py:86
  66.0 28.2 %fusion.70 = bf16[16,16,84,84]{1,0,3,2:T(8,128)(2,1)} fusion(bf16[16,4,84,84]{0,1,3,2:T(4,128)(2,1)} %copy.38, bf16[16,4,3,3]{0,1,3,2:T(4,128)(2,1)S(1)} %copy-done.18), kind=kOutput, calls=%fused_computation.169 | convolution fusion | flops 128000000 | bytes 4516992 | tf_op jit(solution)/shard_map/conv_general_dilated | solution.py:8
  94.2 16.0 %fusion.71 = bf16[16,16,42,42]{1,0,3,2:T(8,128)(2,1)} fusion(bf16[16,16,84,84]{1,0,3,2:T(8,128)(2,1)} %fusion.70), kind=kOutput, calls=%fused_computation.170 | output fusion | flops 3612672 | bytes 4515840 | tf_op jit(solution)/shard_map/reduce_window_max | solution.py:19
  110.2 11.7 %fusion = bf16[16,32,42,42]{1,0,3,2:T(8,128)(2,1)S(1)} fusion(bf16[32,16,3,3]{0,1,3,2:T(8,128)(2,1)S(1)} %copy-done.16, bf16[16,16,42,42]{1,0,3,2:T(8,128)(2,1)} %fusion.71), kind=kOutput, calls=%fused_computation.11 | convolution fusion | flops 253275136 | bytes 2718720 | tf_op jit(solution)/shard_map/conv_general_dilated | solution.py:8
  121.9 1.6 fusion.72
  123.5 0.0 copy-start.14
  123.5 0.0 copy-start.15
  123.5 2.6 %fusion.4 = bf16[16,32,21,21]{1,0,3,2:T(8,128)(2,1)S(1)} fusion(bf16[32,32,3,3]{1,0,3,2:T(8,128)(2,1)S(1)} %copy-done.13, bf16[16,32,21,21]{1,0,3,2:T(8,128)(2,1)S(1)} %fusion.72), kind=kOutput, calls=%fused_computation.18 | convolution fusion | flops 122607104 | bytes 921600 | tf_op jit(solution)/shard_map/conv_general_dilated | solution.py:8
  126.1 1.2 reduce-window_convert_fusion
  127.3 4.7 %fusion.8 = bf16[16,32,11,11]{1,0,3,2:T(8,128)(2,1)S(1)} fusion(bf16[32,32,3,3]{1,0,3,2:T(8,128)(2,1)S(1)} %copy-done.14, bf16[32,32,3,3]{1,0,3,2:T(8,128)(2,1)S(1)} %copy-done.15, bf16[16,32,11,11]{1,0,3,2:T(8,128)(2,1)} %reduce-window_convert_fusion), kind=kOutput, calls=%fused_computation.26 | convolution fusion | flops 63599616 | bytes 284672 | tf_op jit(solution)/shard_map/conv_general_dilated | solution.py:8
  131.9 2.1 %copy.39 = bf16[16,32,11,11]{3,2,1,0:T(8,128)(2,1)S(1)} copy(bf16[16,32,11,11]{1,0,3,2:T(8,128)(2,1)S(1)} %fusion.8) | data formatting | bytes 247808 | tf_op jit(solution)/shard_map/convert_element_type | solution.py:30
  134.0 1.6 reshape.554
  135.7 1.9 %fusion.10 = bf16[256,16]{0,1:T(8,128)(2,1)S(1)} fusion(bf16[16,3872]{1,0:T(8,128)(2,1)S(1)} %reshape.554, bf16[256,3872]{0,1:T(8,128)(2,1)} %param.29), kind=kOutput, calls=%fused_computation.30 | convolution fusion | flops 31727616 | bytes 2114560 | tf_op jit(solution)/shard_map/dot_general | solution.py:32
  137.6 14.0 %all_gather.6 = bf16[256,64]{0,1:T(8,128)(2,1)S(1)} all-gather(bf16[256,16]{0,1:T(8,128)(2,1)S(1)} %fusion.10), channel_id=1, replica_groups=mesh['dp'=8,'tensor'=4] {'tensor'}, dimensions={1}, use_global_device_ids=true | all-gather | bytes 40960 | tf_op jit(solution)/shard_map/all_gather | solution.py:92
  151.6 1.7 fusion.73
  153.3 6.2 %fusion.3 = f32[2048,64]{0,1:T(8,128)S(1)} fusion(f32[64,2048]{1,0:T(8,128)S(1)} %fusion.73, bf16[2048,64]{0,1:T(8,128)(2,1)S(1)} %copy-done.4, bf16[2048,2048]{1,0:T(8,128)(2,1)} %bitcast.97, f32[2048]{0:T(1024)S(1)} %bitcast.101), kind=kOutput, calls=%fused_computation.17 | convolution fusion | flops 537133056 | bytes 9707520 | tf_op jit(solution)/shard_map/dot_general | solution.py:99
  159.6 0.1 fusion.17
  159.7 0.7 copy-done.3
  160.3 0.2 convolution_bitcast_fusion
  160.5 18.7 %psum.7 = f32[19,64]{1,0:T(8,128)S(1)} all-reduce(f32[19,64]{1,0:T(8,128)S(1)} %convolution_bitcast_fusion), channel_id=1, replica_groups=mesh['dp'=8,'tensor'=4] {'tensor'}, use_global_device_ids=true, to_apply=%region_5.7 | all-reduce | flops 1216 | bytes 9728 | tf_op jit(solution)/shard_map/psum | solution.py:112
  179.2 0.1 constant_dynamic-slice_fusion
  179.3 0.1 copy.42
  179.4 0.6 gather_fusion.4
  180.0 0.7 select_select_fusion.1
  180.7 3.3 %all-to-all-start.1 = ((f32[19,8,4]{0,2,1:T(4,128)}), f32[19,8,4]{0,2,1:T(4,128)S(1)}, u32[]{:S(2)}, u32[]{:S(2)}) async-start(f32[19,8,4]{0,2,1:T(4,128)} %select_select_fusion.1), calls=%async_computation.1 | async-start | bytes 32768 | tf_op jit(solution)/shard_map/all_to_all | solution.py:118
  184.0 1.3 compare_and_fusion.4
  185.3 1.1 scatter_custom_fusion.1
  186.4 1.4 scatter_custom_fusion
  187.8 0.8 copy.47
  188.6 0.8 copy.46
  189.4 0.6 gather_fusion.5
  190.0 0.1 select_bitcast_fusion
  190.1 0.7 copy.45
  (55 shorter events, 0.2 us)
Async XLA Ops:
  0.6 5.4 %copy-start = (bf16[32,4,84,84]{3,1,2,0:T(4,128)(2,1)S(1)}, bf16[32,4,84,84]{3,1,2,0:T(4,128)(2,1)}, u32[]{:S(2)}) copy-start(bf16[32,4,84,84]{3,1,2,0:T(4,128)(2,1)} %param.18) | copy-start | bytes 5419012
  15.1 5.4 %copy-start.19 = (s32[1,64]{1,0:T(1,128)S(1)}, s32[1,64]{1,0:T(1,128)}, u32[]{:S(2)}) copy-start(s32[1,64]{1,0:T(1,128)} %param.20) | copy-start | bytes 772
  15.1 6.2 %copy-start.2 = (s32[1,128]{1,0:T(1,128)S(1)}, s32[1,128]{1,0:T(1,128)}, u32[]{:S(2)}) copy-start(s32[1,128]{1,0:T(1,128)} %param.21) | copy-start | bytes 1540
  15.1 7.0 %copy-start.5 = (f32[512,128]{1,0:T(8,128)S(1)}, f32[512,128]{1,0:T(8,128)}, u32[]{:S(2)}) copy-start(f32[512,128]{1,0:T(8,128)} %param.22) | copy-start | bytes 786436
  15.1 7.2 %copy-start.7 = (f32[4,512]{1,0:T(4,128)S(1)}, f32[4,512]{1,0:T(4,128)}, u32[]{:S(2)}) copy-start(f32[4,512]{1,0:T(4,128)} %param.32) | copy-start | bytes 24580
  15.1 7.2 %copy-start.6 = (f32[512,128]{1,0:T(8,128)S(1)}, f32[512,128]{1,0:T(8,128)}, u32[]{:S(2)}) copy-start(f32[512,128]{1,0:T(8,128)} %param.23) | copy-start | bytes 786436
  15.2 39.1 %all-to-all-start = ((bf16[32,4,84,84]{3,1,2,0:T(4,128)(2,1)}), bf16[32,4,84,84]{3,1,2,0:T(4,128)(2,1)}, u32[]{:S(2)}, u32[]{:S(2)}) async-start(bf16[32,4,84,84]{3,1,2,0:T(4,128)(2,1)} %select_select_fusion), calls=%async_computation | async-start | bytes 5505024 | tf_op jit(solution)/shard_map/all_to_all | solution.py:85
  20.5 0.8 copy-start.12
  22.1 1.7 copy-start.8
  23.9 16.5 %copy-start.10 = (pred[64]{0:T(512)(128)(4,1)}, pred[64]{0:T(512)(128)(4,1)S(1)}, u32[]{:S(2)}) copy-start(pred[64]{0:T(512)(128)(4,1)S(1)} %compare_and_fusion.1) | copy-start | bytes 196
  58.4 7.6 %copy-start.18 = (bf16[16,4,3,3]{0,1,3,2:T(4,128)(2,1)S(1)}, bf16[16,4,3,3]{0,1,3,2:T(4,128)(2,1)}, u32[]{:S(2)}) copy-start(bf16[16,4,3,3]{0,1,3,2:T(4,128)(2,1)} %param.24) | copy-start | bytes 3460
  94.2 16.0 %copy-start.16 = (bf16[32,16,3,3]{0,1,3,2:T(8,128)(2,1)S(1)}, bf16[32,16,3,3]{0,1,3,2:T(8,128)(2,1)}, u32[]{:S(2)}) copy-start(bf16[32,16,3,3]{0,1,3,2:T(8,128)(2,1)} %param.25) | copy-start | bytes 27652
  121.9 1.6 copy-start.13
  123.5 3.8 %copy-start.14 = (bf16[32,32,3,3]{1,0,3,2:T(8,128)(2,1)S(1)}, bf16[32,32,3,3]{1,0,3,2:T(8,128)(2,1)}, u32[]{:S(2)}) copy-start(bf16[32,32,3,3]{1,0,3,2:T(8,128)(2,1)} %param.28) | copy-start | bytes 55300
  123.5 3.8 %copy-start.15 = (bf16[32,32,3,3]{1,0,3,2:T(8,128)(2,1)S(1)}, bf16[32,32,3,3]{1,0,3,2:T(8,128)(2,1)}, u32[]{:S(2)}) copy-start(bf16[32,32,3,3]{1,0,3,2:T(8,128)(2,1)} %param.27) | copy-start | bytes 55300
  135.6 17.6 %copy-start.4 = (bf16[2048,64]{0,1:T(8,128)(2,1)S(1)}, bf16[2048,64]{0,1:T(8,128)(2,1)}, u32[]{:S(2)}) copy-start(bf16[2048,64]{0,1:T(8,128)(2,1)} %all_gather.7) | copy-start | bytes 786436
  153.3 6.2 %copy-start.9 = (f32[64]{0:T(128)S(1)}, f32[64]{0:T(128)}, u32[]{:S(2)}) copy-start(f32[64]{0:T(128)} %copy-done.8) | copy-start | bytes 772
  153.3 6.2 %copy-start.11 = (pred[64]{0:T(512)(128)(4,1)S(1)}, pred[64]{0:T(512)(128)(4,1)}, u32[]{:S(2)}) copy-start(pred[64]{0:T(512)(128)(4,1)} %copy-done.10) | copy-start | bytes 196
  153.3 7.0 %copy-start.17 = (bf16[19,512]{1,0:T(8,128)(2,1)S(1)}, bf16[19,512]{1,0:T(8,128)(2,1)}, u32[]{:S(2)}) copy-start(bf16[19,512]{1,0:T(8,128)(2,1)} %param.33) | copy-start | bytes 58372
  153.3 37.5 %copy-start.1 = (bf16[32,4,84,84]{3,1,2,0:T(4,128)(2,1)S(1)}, bf16[32,4,84,84]{3,1,2,0:T(4,128)(2,1)}, u32[]{:S(2)}) copy-start(bf16[32,4,84,84]{3,1,2,0:T(4,128)(2,1)} %param.18) | copy-start | bytes 5419012
  159.5 0.8 copy-start.3
  180.7 8.8 %all-to-all-start.1 = ((f32[19,8,4]{0,2,1:T(4,128)}), f32[19,8,4]{0,2,1:T(4,128)S(1)}, u32[]{:S(2)}, u32[]{:S(2)}) async-start(f32[19,8,4]{0,2,1:T(4,128)} %select_select_fusion.1), calls=%async_computation.1 | async-start | bytes 32768 | tf_op jit(solution)/shard_map/all_to_all | solution.py:118
where the time goes:
time: 191 us
  matrix products  57.1 us (30%)
  blocking collectives  48.5 us (25%)
  other arithmetic  31 us (16%)
  local copies, waits for them, and re-layouts  30.7 us (16%)
  waiting for transfers between devices  13.7 us (7%)
  starting transfers between devices  8.67 us (5%)
    conv_general_dilated x4, matrix products, conv_same(): lax.conv_general_dilated(inputs, kernel, (1, 1), 'SAME', dimension_number...  47.1 us
    psum x1, blocking collectives, body(): totals = lax.psum(partial_heads, 'tensor')  18.7 us
    another operation x3, other arithmetic, pooled(): lax.reduce_window(inputs, -jnp.inf, lax.max, (1, 1, 3, 3), (1, 1, 2, 2),...  18.7 us
    all_gather x1, blocking collectives, body(): lax.all_gather(prev_hidden.astype(jnp.bfloat16), 'tensor', axis=0, tiled=...  15.7 us
    all_gather x1, blocking collectives, body(): lax.all_gather(features, 'tensor', axis=1, tiled=True)  14 us
    all_to_all x1, waiting for transfers between devices, body(): lax.all_to_all(outgoing, 'dp', split_axis=0, concat_axis=0, tiled=True)  13.7 us
    select_n x1, local copies, waits for them, and re-layouts, body(): jnp.take(incoming, take_slots, axis=0)  7.59 us
    dot_general x1, matrix products, body(): jnp.dot(recur_weight.reshape(4 * hidden_share, -1), all_hidden, preferred...  6.2 us
  transfers between devices with their start and end apart: 2, of which 1 were waited for; matrix products, arithmetic and copies ran while one was open for 5% of the time, Pallas kernels for 0%

commit v1 on v0

v1 whole, which is shorter than its diff:
```python
import functools

import jax
import jax.numpy as jnp
import numpy as np
from jax import lax
from jax.experimental import pallas as pl
from jax.experimental.pallas import tpu as pltpu
from jax.sharding import PartitionSpec as P

F32, BF16, I32 = jnp.float32, jnp.bfloat16, jnp.int32
LANES = 128
PACK = 16
Y1, Y2, P3, Y4 = 12, 6, 2, 4
NN = (((1,), (0,)), ((), ()))
NT = (((1,), (1,)), ((), ()))
TN = (((0,), (0,)), ((), ()))
VMEM = pl.BlockSpec(memory_space=pltpu.VMEM)
SMEM = pl.BlockSpec(memory_space=pltpu.SMEM)


def mm(a, b, dims=NN, precision=None):
    return lax.dot_general(a, b, dims, precision=precision, preferred_element_type=F32)


def iota(shape, axis):
    return lax.broadcasted_iota(I32, shape, axis)


def log2(n):
    assert n & (n - 1) == 0
    return n.bit_length() - 1


def one_hot(mask):
    return jnp.where(mask, 1.0, 0.0).astype(BF16)


class Sizes:
    def __init__(self, frames, first, second, projection):
        self.cap, self.c0, self.f, _ = frames
        self.c1, self.c2, self.feat = first[0], second[0], projection[0]
        self.w1 = -(-self.f // 2)
        self.w2 = -(-self.w1 // 2)
        self.w3 = -(-self.w2 // 2)
        self.n1 = LANES // self.w1
        self.n2 = 2 * self.n1
        assert self.f % 4 == 0 and self.w2 % 2 == 1 and self.n2 * self.w2 <= LANES
        assert self.f % Y1 == 0 and Y1 % 2 == 0 and self.w1 % Y2 == 0 and Y2 % 2 == 0
        self.pad1 = PACK // self.c0
        self.win1 = Y1 + 2 * self.pad1
        self.win2 = Y2 + 3
        self.win3 = 2 * P3 + 3
        self.win4 = Y4 + 2
        self.subs = -(-self.cap // self.n1)
        self.groups = -(-self.cap // self.n2)
        self.blocks3 = -(-self.w3 // P3)
        self.blocks4 = -(-self.w3 // Y4)
        self.wide = -(-self.w3 * self.cap // LANES) * LANES
        assert self.wide - self.w3 * self.cap >= self.cap

    def tables(self):
        rows = []
        four = np.arange(4 * LANES)
        quarter, lane = four // LANES, four % LANES

        def source(width, half, where, count):
            image, j = lane // half, lane % half
            x = 2 * j + quarter - 1
            live = (image < count) & (x >= 0) & (x < width)
            return np.where(live, where(image) + x, -1)

        for i in range(self.n1):
            own = source(self.f, self.w1, lambda image: 0 * image, self.n1)
            rows.append(np.where(lane // self.w1 == i, own, -1))
        rows.append(
            source(
                self.w1,
                self.w2,
                lambda image: image // self.n1 * LANES + image % self.n1 * self.w1,
                self.n2,
            )
        )
        rows.append(source(self.w2, self.w3, lambda image: image * self.w2, self.n2))
        final = np.arange(self.wide)
        x, image = final // self.cap, final % self.cap
        rows.append(np.where(x < self.w3, image * self.w3 + x, -(1 << 20)))
        k1, k2 = np.arange(3 * self.win1 * self.c0), np.arange(3 * self.win2 * self.c1)
        k3, k4 = np.arange(self.win3 * self.c2), np.arange(self.win4 * self.c2)
        for k, window, c in ((k1, self.win1, self.c0), (k2, self.win2, self.c1)):
            rows += [k // (window * c), k % (window * c) // c, k % c]
        for k, c in ((k3, self.c2), (k4, self.c2)):
            rows += [k // c, k % c]
        n = self.c2 * self.w3
        k = np.arange(n)
        rows.append(k % self.w3 * self.c2 + k // self.w3)
        k = np.arange(PACK * self.w3)
        rows += [k % self.w3, k // self.w3]
        width = max(len(r) for r in rows)
        table = np.full((-(-len(rows) // 8) * 8, width), -(1 << 20), np.int32)
        for i, r in enumerate(rows):
            table[i, : len(r)] = r
        return table, [len(r) for r in rows]


def encoder_kernel(
    z, lengths, dp, tensor, dp_index, tensor_index,
    counts, frames, w1, w2, w3, r1, r2, proj, table, out,
    p1, p2, p3, t1, t2, t3, t4, t5, g1, s1, g2, s2, g3, s3, total, x4, x5, projx,
):
    def row(i):
        return table[i : i + 1, : lengths[i]]

    def pick(rows, i):
        return one_hot(iota((rows, lengths[i]), 0) == row(i))

    for i in range(z.n1):
        p1[i] = pick(z.f, i)
    p2[...] = pick(2 * LANES, z.n1)
    p3[...] = pick(LANES, z.n1 + 1)
    base = z.n1 + 3

    def banded(m, cout, band, kx):
        a = one_hot((iota((m, cout), 0) & (cout - 1)) == iota((m, cout), 1))
        gap = band - (iota((m, kx), 0) >> log2(cout))
        return a, gap

    def band_all(weights, m, cin, cout, index, first):
        kx = lengths[index]
        a, gap = banded(m, cout, row(index + 1), kx)
        acc = jnp.zeros((m, kx), F32)
        for dy in range(3):
            part = jnp.zeros((m, kx), F32)
            for dx in range(3):
                mixed = mm(a, weights[dy, dx], NT).astype(BF16)
                spread = one_hot(
                    (iota((cin, kx), 0) == row(index + 2)) & (row(index) == dx)
                )
                part = part + mm(mixed, spread)
            acc = jnp.where(gap == first + dy, part, acc)
        return acc.astype(BF16)

    def band_each(weights, m, cin, cout, index, target):
        kx = lengths[index]
        a, gap = banded(m, cout, row(index), kx)
        spread = one_hot(iota((cin, kx), 0) == row(index + 1))
        for dx in range(3):
            acc = jnp.zeros((m, kx), F32)
            for dy in range(3):
                mixed = mm(a, weights[dy, dx]).astype(BF16)
                acc = jnp.where(gap == dy, mm(mixed, spread), acc)
            target[dx] = acc.astype(BF16)

    t1[...] = band_all(w1, (Y1 + 1) * z.c1, z.c0, z.c1, base, z.pad1 - 1)
    t2[...] = band_all(w2, (Y2 + 1) * z.c2, z.c1, z.c2, base + 3, 0)
    band_each(w3, (2 * P3 + 1) * z.c2, z.c2, z.c2, base + 6, t3)
    band_each(r1, Y4 * z.c2, z.c2, z.c2, base + 8, t4)
    band_each(r2, Y4 * z.c2, z.c2, z.c2, base + 8, t5)

    for ref, top, rows in ((g1, PACK, z.f * z.c0), (g2, z.c1, z.w1 * z.c1), (g3, 2 * z.c2, z.w2 * z.c2)):
        for q in range(4):
            ref[q, :top] = jnp.zeros((top, LANES), BF16)
            low = ref.shape[1] - top - rows
            ref[q, top + rows :] = jnp.zeros((low, LANES), BF16)
    for ref in (x4, x5):
        for q in range(3):
            ref[q, : z.c2] = jnp.zeros((z.c2, z.wide), BF16)
            low = ref.shape[1] - z.c2 - z.w3 * z.c2
            ref[q, z.c2 + z.w3 * z.c2 :] = jnp.zeros((low, z.wide), BF16)
    total[...] = jnp.zeros(total.shape, F32)

    own = counts[tensor_index(), dp_index()]
    subs = lax.div(own + (z.n1 - 1), z.n1)
    groups = lax.div(own + (z.n2 - 1), z.n2)
    s1[subs] = jnp.zeros(s1.shape[1:], BF16)

    def sides(ref, dx, low, rows):
        return jnp.concatenate(
            [ref[dx, low : low + rows, :], ref[dx + 1, low : low + rows, :]], axis=1
        )

    def lane_is(rows, half, count, j):
        lane = iota((rows, LANES), 1)
        mask = lane == j
        for i in range(1, count):
            mask = mask | (lane == i * half + j)
        return mask

    def pool_low(acc, half, count):
        even, odd = acc[:, :LANES], acc[:, LANES:]
        nxt = pltpu.roll(even, LANES - 1, 1)
        nxt = jnp.where(lane_is(even.shape[0], half, count, half - 1), even, nxt)
        return jnp.maximum(jnp.maximum(even, odd), nxt)

    def pool_rows(m, c, pairs, last):
        done = []
        for i in range(pairs):
            top = jnp.maximum(m[2 * i * c : (2 * i + 1) * c], m[(2 * i + 1) * c : (2 * i + 2) * c])
            if not (last and i == pairs - 1):
                top = jnp.maximum(top, m[(2 * i + 2) * c : (2 * i + 3) * c])
            done.append(top)
        return jnp.concatenate(done, axis=0)

    def conv_one(s, _):
        mixed = None
        for i in range(z.n1):
            image = frames[jnp.minimum(s * z.n1 + i, z.cap - 1)]
            part = mm(image, p1[i])
            mixed = part if mixed is None else mixed + part
        mixed = mixed.astype(BF16)
        for q in range(4):
            g1[q, PACK : PACK + z.f * z.c0, :] = mixed[:, q * LANES : (q + 1) * LANES]
        for b in range(z.f // Y1):
            low = b * Y1 * z.c0
            around = jnp.concatenate([sides(g1, dx, low, z.win1 * z.c0) for dx in range(3)], axis=0)
            m = pool_low(mm(t1[...], around), z.w1, z.n1)
            rows = pool_rows(m, z.c1, Y1 // 2, b == z.f // Y1 - 1)
            size = Y1 // 2 * z.c1
            s1[s, b * size : (b + 1) * size, :] = jnp.maximum(rows, 0.0).astype(BF16)
        return 0

    lax.fori_loop(0, subs, conv_one, 0)

    def conv_rest(g, _):
        both = jnp.concatenate([s1[2 * g], s1[2 * g + 1]], axis=1)
        mixed = mm(both, p2[...]).astype(BF16)
        for q in range(4):
            g2[q, z.c1 : z.c1 + z.w1 * z.c1, :] = mixed[:, q * LANES : (q + 1) * LANES]
        for b in range(z.w1 // Y2):
            low = b * Y2 * z.c1
            around = jnp.concatenate([sides(g2, dx, low, z.win2 * z.c1) for dx in range(3)], axis=0)
            m = pool_low(mm(t2[...], around), z.w2, z.n2)
            rows = pool_rows(m, z.c2, Y2 // 2, b == z.w1 // Y2 - 1)
            size = Y2 // 2 * z.c2
            s2[b * size : (b + 1) * size, :] = jnp.maximum(rows, 0.0).astype(BF16)
        mixed = mm(s2[...], p3[...]).astype(BF16)
        for q in range(4):
            g3[q, 2 * z.c2 : 2 * z.c2 + z.w2 * z.c2, :] = mixed[:, q * LANES : (q + 1) * LANES]
        c = z.c2
        for b in range(z.blocks3):
            low = b * 2 * P3 * c
            acc = None
            for dx in range(3):
                part = mm(t3[dx], sides(g3, dx, low, z.win3 * c))
                acc = part if acc is None else acc + part
            even, odd = acc[:, :LANES], acc[:, LANES:]
            n = even.shape[0]
            before = jnp.where(lane_is(n, z.w3, z.n2, 0), even, pltpu.roll(odd, 1, 1))
            odd = jnp.where(lane_is(n, z.w3, z.n2, z.w3 - 1), even, odd)
            m = jnp.maximum(jnp.maximum(even, odd), before)
            for i in range(P3):
                pooled = b * P3 + i
                if pooled >= z.w3:
                    continue
                rows = [2 * i + d for d in range(3) if 0 <= 2 * pooled - 1 + d < z.w2]
                top = None
                for r in rows:
                    piece = m[r * c : (r + 1) * c]
                    top = piece if top is None else jnp.maximum(top, piece)
                s3[pooled * c : (pooled + 1) * c, :] = top.astype(BF16)
        shape = (LANES, z.wide)
        line = iota(shape, 0)
        place = one_hot((line == row(z.n1 + 2) - g * (z.n2 * z.w3)) & (line < z.n2 * z.w3))
        total[...] += mm(s3[...], place)
        return 0

    lax.fori_loop(0, groups, conv_rest, 0)

    c, n = z.c2, z.w3 * z.c2
    live = iota((n, z.wide), 1) < z.w3 * z.cap

    def spread_x(ref, value):
        ref[0, c : c + n, :] = pltpu.roll(value, z.cap, 1).astype(BF16)
        ref[1, c : c + n, :] = value.astype(BF16)
        ref[2, c : c + n, :] = pltpu.roll(value, z.wide - z.cap, 1).astype(BF16)

    def residual(ref, kernel, add):
        pieces = []
        for b in range(z.blocks4):
            low = b * Y4 * c
            acc = None
            for dx in range(3):
                part = mm(kernel[dx], ref[dx, low : low + z.win4 * c, :])
                acc = part if acc is None else acc + part
            pieces.append(acc[: min(Y4, z.w3 - b * Y4) * c])
        value = jnp.concatenate(pieces, axis=0)
        if add is not None:
            value = value + add
        return jnp.maximum(value, 0.0)

    spread_x(x4, jnp.maximum(total[...], 0.0))
    inner = residual(x4, t4, None).astype(BF16).astype(F32)
    spread_x(x5, jnp.where(live, inner, 0.0))
    encoded = residual(x5, t5, total[...]).astype(BF16)

    last = len(lengths) - 3
    order = one_hot(iota((n, n), 0) == row(last))
    turned = jnp.swapaxes(encoded, 0, 1)
    turned = mm(turned, order).astype(BF16)
    block = PACK * z.w3
    wanted = iota((block, block), 0)
    regroup = one_hot(((wanted >> log2(PACK)) == row(last + 1)) & ((wanted & (PACK - 1)) == row(last + 2)))
    for b in range(n // PACK):
        moved = mm(regroup, proj[b * block : (b + 1) * block, :]).astype(BF16)
        for x in range(z.w3):
            projx[x, b * PACK : (b + 1) * PACK, :] = moved[x * PACK : (x + 1) * PACK]
    acc = None
    for x in range(z.w3):
        part = mm(turned[x * z.cap : (x + 1) * z.cap], projx[x])
        acc = part if acc is None else acc + part
    features = jnp.maximum(acc, 0.0).astype(BF16)

    start = jnp.int32(0)
    for a in range(dp):
        start = start + jnp.where(a < dp_index(), counts[tensor_index(), a], 0)
    depth = z.cap // dp
    shape = (dp * tensor * depth, z.cap)
    r = iota(shape, 0)
    receiver, level = r >> log2(tensor * depth), r & (depth - 1)
    arrival = ((receiver - start) & (dp - 1)) + level * dp
    route = one_hot((iota(shape, 1) == arrival) & (arrival < own))
    out[...] = mm(route, features).astype(BF16)


def encode_rows(frames, counts, kernels, projection):
    first, second, third, res_first, res_second = kernels
    z = Sizes(frames.shape, first.shape, second.shape, projection.shape)
    table, lengths = z.tables()
    dp, tensor = lax.axis_size("dp"), lax.axis_size("tensor")
    images = jnp.transpose(frames, (0, 2, 1, 3)).reshape(z.cap, z.f * z.c0, z.f)
    ci_co, co_ci = (2, 3, 1, 0), (2, 3, 0, 1)
    n = z.w3 * z.c2
    scratch = [
        pltpu.VMEM((z.n1, z.f, 4 * LANES), BF16),
        pltpu.VMEM((2 * LANES, 4 * LANES), BF16),
        pltpu.VMEM((LANES, 4 * LANES), BF16),
        pltpu.VMEM(((Y1 + 1) * z.c1, 3 * z.win1 * z.c0), BF16),
        pltpu.VMEM(((Y2 + 1) * z.c2, 3 * z.win2 * z.c1), BF16),
        pltpu.VMEM((3, (2 * P3 + 1) * z.c2, z.win3 * z.c2), BF16),
        pltpu.VMEM((3, Y4 * z.c2, z.win4 * z.c2), BF16),
        pltpu.VMEM((3, Y4 * z.c2, z.win4 * z.c2), BF16),
        pltpu.VMEM((4, z.f * z.c0 + 2 * PACK, LANES), BF16),
        pltpu.VMEM((2 * z.groups + 1, z.w1 * z.c1, LANES), BF16),
        pltpu.VMEM((4, (z.w1 - Y2 + z.win2) * z.c1, LANES), BF16),
        pltpu.VMEM((z.w2 * z.c2, LANES), BF16),
        pltpu.VMEM((4, ((z.blocks3 - 1) * 2 * P3 + z.win3) * z.c2, LANES), BF16),
        pltpu.VMEM((n, LANES), BF16),
        pltpu.VMEM((n, z.wide), F32),
        pltpu.VMEM((3, ((z.blocks4 - 1) * Y4 + z.win4) * z.c2, z.wide), BF16),
        pltpu.VMEM((3, ((z.blocks4 - 1) * Y4 + z.win4) * z.c2, z.wide), BF16),
        pltpu.VMEM((z.w3, n, z.feat), BF16),
    ]
    body = functools.partial(
        encoder_kernel, z, lengths, dp, tensor,
        lambda: lax.axis_index("dp"), lambda: lax.axis_index("tensor"),
    )
    depth = z.cap // dp
    return pl.pallas_call(
        body,
        name="encoder",
        out_shape=jax.ShapeDtypeStruct((dp * tensor * depth, z.feat), BF16),
        in_specs=[SMEM] + [VMEM] * 8,
        out_specs=VMEM,
        scratch_shapes=scratch,
        compiler_params=pltpu.CompilerParams(vmem_limit_bytes=40 << 20),
        cost_estimate=pl.CostEstimate(flops=20_000_000_000, bytes_accessed=8_000_000, transcendentals=0),
    )(
        counts,
        images,
        jnp.transpose(first, ci_co),
        jnp.transpose(second, ci_co),
        jnp.transpose(third, co_ci),
        jnp.transpose(res_first, co_ci),
        jnp.transpose(res_second, co_ci),
        jnp.transpose(projection),
        jnp.asarray(table),
    )


def recurrent_kernel(index, weight, bias, *refs):
    *pieces, out, held, sems = refs
    gates, share, _ = weight.shape
    width = pieces[0].shape[0]
    copies = [pltpu.make_async_copy(weight.at[q], held.at[q], sems.at[q]) for q in range(gates)]
    for copy in copies:
        copy.start()
    tensor = len(pieces)
    for q in range(gates):
        copies[q].wait()
        column = jnp.broadcast_to(bias[q : q + 1, :], (out.shape[1], share))
        acc = None
        for back, piece in enumerate(pieces):
            low = pl.multiple_of(((index() - back) & (tensor - 1)) * width, width)
            part = mm(held[q, :, pl.ds(low, width)], piece[...])
            acc = part if acc is None else acc + part
        out[q * share : (q + 1) * share, :] = acc + jnp.transpose(column)


def recurrent(weight, bias, pieces):
    gates, share, hidden = weight.shape
    slots = pieces[0].shape[1]
    return pl.pallas_call(
        functools.partial(recurrent_kernel, lambda: lax.axis_index("tensor")),
        name="recurrent",
        out_shape=jax.ShapeDtypeStruct((gates * share, slots), F32),
        in_specs=[pl.BlockSpec(memory_space=pl.ANY)] + [VMEM] * (1 + len(pieces)),
        out_specs=VMEM,
        scratch_shapes=[
            pltpu.VMEM(weight.shape, BF16),
            pltpu.SemaphoreType.DMA((gates,)),
        ],
        compiler_params=pltpu.CompilerParams(vmem_limit_bytes=24 << 20),
        cost_estimate=pl.CostEstimate(
            flops=2 * gates * share * hidden * slots, bytes_accessed=2 * gates * share * hidden, transcendentals=0
        ),
    )(weight, bias, *pieces)


def core_kernel(dp_index, features, sums, weight, hidden, cell, heads, slots, counts, resets, sent, hidden_out, cell_out):
    tensor, dp = counts.shape
    rows, count = features.shape[0], slots.shape[1]
    depth = rows // (dp * tensor)
    share, places = hidden.shape
    mine = dp_index()
    exact = lax.Precision.HIGHEST
    tallies = counts[...].astype(F32)
    before = jnp.where(iota((dp, dp), 0) < iota((dp, dp), 1), 1.0, 0.0)
    starts = mm(tallies, before, precision=exact)
    line = iota((rows, 1), 0)
    sender, group, level = line >> log2(tensor * depth), (line >> log2(depth)) & (tensor - 1), line & (depth - 1)
    by_group = jnp.where(iota((rows, tensor), 1) == group, 1.0, 0.0)
    own = iota((rows, dp), 1) == sender

    def of_row(table):
        wide = mm(by_group, table, precision=exact)
        return jnp.sum(jnp.where(own, wide, 0.0), axis=1, keepdims=True).astype(I32)

    start = of_row(starts)
    end = of_row(starts + tallies)
    rank = start + ((mine - start) & (dp - 1)) + level * dp
    balanced = group * (count // tensor) + ((rank - mine) >> log2(dp))
    to_row = one_hot((iota((rows, count), 1) == balanced) & (rank < end))
    of_slot = one_hot(iota((places, count), 0) == slots[...])
    chosen = mm(to_row, of_slot, NT)
    taken = jnp.sum(chosen, axis=0, keepdims=True) > 0.5
    inputs = mm(features[...], chosen.astype(BF16), TN).astype(BF16)
    keep = 1.0 - resets[...].astype(F32)
    old_cell = cell[...]

    def gate(q):
        low = q * share
        return mm(weight[q], inputs) + sums[low : low + share, :]

    next_cell = jax.nn.sigmoid(gate(1)) * (old_cell * keep) + jax.nn.sigmoid(gate(0)) * jnp.tanh(gate(2))
    next_hidden = jax.nn.sigmoid(gate(3)) * jnp.tanh(next_cell)
    values = mm(heads[...], next_hidden.astype(BF16))
    sent[...] = mm(chosen, values, NT, precision=exact)
    cell_out[...] = jnp.where(taken, next_cell, old_cell)
    hidden_out[...] = jnp.where(taken, next_hidden, hidden[...])


def core(features, sums, weight, hidden, cell, heads, slots, counts, resets):
    share = hidden.shape[0]
    return pl.pallas_call(
        functools.partial(core_kernel, lambda: lax.axis_index("dp")),
        name="core",
        out_shape=(
            jax.ShapeDtypeStruct((features.shape[0], heads.shape[0]), F32),
            jax.ShapeDtypeStruct(hidden.shape, F32),
            jax.ShapeDtypeStruct(cell.shape, F32),
        ),
        in_specs=[VMEM] * 9,
        out_specs=(VMEM,) * 3,
        compiler_params=pltpu.CompilerParams(vmem_limit_bytes=24 << 20),
        cost_estimate=pl.CostEstimate(
            flops=8 * share * weight.shape[2] * hidden.shape[1], bytes_accessed=4_000_000, transcendentals=0
        ),
    )(features, sums, weight, hidden, cell, heads, slots, counts, resets)


def answers_kernel(tensor, dp_index, tensor_index, counts, received, out):
    dp = counts.shape[1]
    rows, cap = received.shape[0], out.shape[1]
    depth = cap // dp
    start = jnp.int32(0)
    for a in range(dp):
        start = start + jnp.where(a < dp_index(), counts[tensor_index(), a], 0)
    own = counts[tensor_index(), dp_index()]
    line = iota((rows, cap), 0)
    giver, level = line >> log2(tensor * depth), line & (depth - 1)
    arrival = ((giver - start) & (dp - 1)) + level * dp
    place = jnp.where((iota((rows, cap), 1) == arrival) & (arrival < own), 1.0, 0.0)
    out[...] = mm(received[...], place, TN, precision=lax.Precision.HIGHEST)


def answers(counts, received, cap):
    return pl.pallas_call(
        functools.partial(
            answers_kernel,
            counts.shape[0],
            lambda: lax.axis_index("dp"),
            lambda: lax.axis_index("tensor"),
        ),
        name="answers",
        out_shape=jax.ShapeDtypeStruct((received.shape[1], cap), F32),
        in_specs=[SMEM, VMEM],
        out_specs=VMEM,
    )(counts, received)


def body(
    frames, counts, slot_ids, reset_flags, hidden_state, cell_state,
    conv_first, conv_second, conv_third, res_first, res_second,
    projection, input_weight, recur_weight, gate_bias, head_weight,
):
    tensor = lax.axis_size("tensor")
    own = (hidden_state * (1 - reset_flags).astype(F32)).astype(BF16)
    pieces = [own] + [
        lax.ppermute(own, "tensor", [(i, (i + back) % tensor) for i in range(tensor)])
        for back in range(1, tensor)
    ]
    kernels = (conv_first, conv_second, conv_third, res_first, res_second)
    features = encode_rows(frames, counts, kernels, projection)
    features = lax.all_to_all(features, ("dp", "tensor"), 0, 0, tiled=True)
    sums = recurrent(recur_weight, gate_bias, pieces)
    sent, hidden_after, cell_after = core(
        features, sums, input_weight, hidden_state, cell_state, head_weight, slot_ids, counts, reset_flags
    )
    received = lax.all_to_all(sent, ("dp", "tensor"), 0, 0, tiled=True)
    return answers(counts, received, frames.shape[0]), hidden_after, cell_after


def solution(mesh):
    return jax.shard_map(
        body,
        mesh=mesh,
        in_specs=(
            P(("dp", "tensor"), None, None, None),
            P(),
            P("dp", None),
            P("dp", None),
            P("tensor", "dp"),
            P("tensor", "dp"),
            P(),
            P(),
            P(),
            P(),
            P(),
            P(),
            P(None, "tensor", None),
            P(None, "tensor", None),
            P(None, "tensor"),
            P(None, "tensor"),
        ),
        out_specs=(P(None, ("dp", "tensor")), P("tensor", "dp"), P("tensor", "dp")),
        check_vma=False,
    )
```

time: 191 us -> 76.6 us (0.40)
  matrix products: 57.1 us -> 0 us
  other arithmetic: 31 us -> 1.63 us
  local copies, waits for them, and re-layouts: 30.7 us -> 12.4 us
  Pallas kernels: 0 us -> 17.2 us
  waiting for transfers between devices: 13.7 us -> 0.01 us
  blocking collectives: 48.5 us -> 38.7 us
  starting transfers between devices: 8.67 us -> 6.14 us
    conv_general_dilated x4 -> x0, matrix products: 47.1 us -> none  [conv_same(): lax.conv_general_dilated(inputs, kernel, (1, 1), 'SAME', dimension_number...]
    all_to_all x0 -> x2, blocking collectives: none -> 38.7 us  [the longest x1 28.9 us: body(): features = lax.all_to_all(features, ('dp', 'tensor'), 0, 0, tiled=True)]
    all_gather x2 -> x0, blocking collectives: 29.7 us -> none  [the longest x1 15.7 us: body(): lax.all_gather(prev_hidden.astype(jnp.bfloat16), 'tensor', axis=0, tiled=...]
    another operation x4 -> x0, other arithmetic: 18.9 us -> none  [the longest x3 18.7 us: pooled(): lax.reduce_window(inputs, -jnp.inf, lax.max, (1, 1, 3, 3), (1, 1, 2, 2),...]
    psum x1 -> x0, blocking collectives: 18.7 us -> none  [body(): totals = lax.psum(partial_heads, 'tensor')]
    pallas_call x0 -> x4, Pallas kernels: none -> 17.2 us  [the longest x1 10.1 us: encode_rows(): pl.pallas_call(body, name='encoder', out_shape=jax.ShapeDtypeStruct((dp *...]
    all_to_all x2 -> x0, waiting for transfers between devices: 13.7 us -> none  [the longest x1 13.7 us: body(): lax.all_to_all(outgoing, 'dp', split_axis=0, concat_axis=0, tiled=True)]
    gather x8 -> x0, local copies, waits for them, and re-layouts: 11.7 us -> none  [the longest x1 4.34 us: body(): jnp.take(frames, send_safe, axis=0)]
  transfers between devices with their start and end apart: 2 -> 3, of which waited for: 1 -> 0; matrix products, arithmetic and copies ran while one was open for 5% -> 0% of each run, Pallas kernels for 0% -> 13%
where the time goes in v1:
time: 76.6 us; the launch traced here: 76.8 us
  blocking collectives  38.7 us (51%)
  Pallas kernels  17.2 us (22%)
  local copies, waits for them, and re-layouts  12.4 us (16%)
  starting transfers between devices  6.14 us (8%)
  other arithmetic  1.63 us (2%)
  between operations  0.77 us (1%)
    all_to_all x1, blocking collectives, body(): features = lax.all_to_all(features, ('dp', 'tensor'), 0, 0, tiled=True)  28.9 us
    unnamed x36, local copies, waits for them, and re-layouts  12.3 us
    pallas_call x1, Pallas kernels, encode_rows(): pl.pallas_call(body, name='encoder', out_shape=jax.ShapeDtypeStruct((dp *...  10.1 us
    all_to_all x1, blocking collectives, body(): received = lax.all_to_all(sent, ('dp', 'tensor'), 0, 0, tiled=True)  9.84 us
    ppermute x3, starting transfers between devices, body(): lax.ppermute(own, 'tensor', [(i, (i + back) % tensor) for i in range(tens...  6.14 us
    pallas_call x1, Pallas kernels, recurrent(): pl.pallas_call(functools.partial(recurrent_kernel, lambda: lax.axis_index...  3.47 us
    pallas_call x1, Pallas kernels, core(): pl.pallas_call(functools.partial(core_kernel, lambda: lax.axis_index('dp'...  1.94 us
    pallas_call x1, Pallas kernels, answers(): pl.pallas_call(functools.partial(answers_kernel, counts.shape[0], lambda:...  1.67 us
  transfers between devices with their start and end apart: 3, of which 0 were waited for; matrix products, arithmetic and copies ran while one was open for 0% of the time, Pallas kernels for 13%

profile of v1, /device:TPU:0, one launch (start us, length us, event | category | flops | bytes accessed | tf_op | source)
XLA Modules:
  0.0 76.8 jit_solution(3081336087982553080)
XLA Ops:
  0.6 0.7 convert_bitcast_fusion
  1.3 1.0 %multiply_convert_fusion.refs_0_ = bf16[512,128]{1,0:T(8,128)(2,1)S(1)} fusion(f32[512,128]{1,0:T(8,128)} %hidden.1, f32[128]{0:T(128)S(1)} %convert_bitcast_fusion), kind=kLoop, calls=%fused_computation | loop fusion | flops 131072 | bytes 393728 | tf_op jit(solution)/shard_map/convert_element_type | solution.py:517
  2.3 5.1 %collective-permute-start.2 = (bf16[512,128]{1,0:T(8,128)(2,1)S(1)}, bf16[512,128]{1,0:T(8,128)(2,1)S(1)}, u32[]{:S(2)}, u32[]{:S(2)}) collective-permute-start(bf16[512,128]{1,0:T(8,128)(2,1)S(1)} %multiply_convert_fusion.refs_0_), channel_id=1, source_target_pairs={{0,3},{1,0},{2,1},{3,2},{4,7},{5,4},{6,5},{7,6},{8,11},{9,8},{10,9... | collective-permute-start | bytes 393224 | tf_op jit(solution)/shard_map/ppermute | solution.py:519
  7.4 0.0 collective-permute-start.1
  7.4 1.0 %collective-permute-start = (bf16[512,128]{1,0:T(8,128)(2,1)S(1)}, bf16[512,128]{1,0:T(8,128)(2,1)S(1)}, u32[]{:S(2)}, u32[]{:S(2)}) collective-permute-start(bf16[512,128]{1,0:T(8,128)(2,1)S(1)} %multiply_convert_fusion.refs_0_), channel_id=1, source_target_pairs={{0,1},{1,2},{2,3},{3,0},{4,5},{5,6},{6,7},{7,4},{8,9},{9,10},{10,1... | collective-permute-start | bytes 393224 | tf_op jit(solution)/shard_map/ppermute | solution.py:519
  8.4 0.0 copy-start.5
  8.4 0.7 copy-done.5
  9.1 0.0 copy-start.10
  9.1 1.8 %copy-done.10 = bf16[32,4,84,84]{3,1,2,0:T(4,128)(2,1)S(1)} copy-done((bf16[32,4,84,84]{3,1,2,0:T(4,128)(2,1)S(1)}, bf16[32,4,84,84]{3,1,2,0:T(4,128)(2,1)}, u32[]{:S(2)}) %copy-start.10) | copy-done | bytes 1806360
  10.9 0.0 copy-start.11
  10.9 1.5 %copy-done.11 = bf16[256,3872]{0,1:T(8,128)(2,1)S(1)} copy-done((bf16[256,3872]{0,1:T(8,128)(2,1)S(1)}, bf16[256,3872]{0,1:T(8,128)(2,1)}, u32[]{:S(2)}) %copy-start.11) | copy-done | bytes 1982488
  12.4 0.0 copy-start.12
  12.4 0.9 %copy-done.12 = bf16[32,32,3,3]{1,0,3,2:T(8,128)(2,1)S(1)} copy-done((bf16[32,32,3,3]{1,0,3,2:T(8,128)(2,1)S(1)}, bf16[32,32,3,3]{1,0,3,2:T(8,128)(2,1)}, u32[]{:S(2)}) %copy-start.12) | copy-done | bytes 18456
  13.3 0.0 copy-start.13
  13.3 0.9 %copy-done.13 = bf16[32,32,3,3]{1,0,3,2:T(8,128)(2,1)S(1)} copy-done((bf16[32,32,3,3]{1,0,3,2:T(8,128)(2,1)S(1)}, bf16[32,32,3,3]{1,0,3,2:T(8,128)(2,1)}, u32[]{:S(2)}) %copy-start.13) | copy-done | bytes 18456
  14.2 0.0 copy-start.14
  14.2 0.9 %copy-done.14 = bf16[32,32,3,3]{1,0,3,2:T(8,128)(2,1)S(1)} copy-done((bf16[32,32,3,3]{1,0,3,2:T(8,128)(2,1)S(1)}, bf16[32,32,3,3]{1,0,3,2:T(8,128)(2,1)}, u32[]{:S(2)}) %copy-start.14) | copy-done | bytes 18456
  15.1 0.0 copy-start.15
  15.1 0.8 copy-done.15
  15.8 0.0 copy-start.16
  15.8 0.7 copy-done.16
  16.5 0.0 copy-start.17
  16.5 0.8 %copy-done.17 = s32[24,512]{1,0:T(8,128)S(1)} copy-done((s32[24,512]{1,0:T(8,128)S(1)}, s32[24,512]{1,0:T(8,128)}, u32[]{:S(2)}) %copy-start.17) | copy-done | bytes 49176
  17.3 0.0 copy-start.7
  17.3 10.1 %encoder.1 = bf16[128,256]{1,0:T(8,128)(2,1)S(1)} custom-call(s32[4,8]{1,0:T(4,128)S(1)} %copy-done.5, bf16[32,336,84]{2,1,0:T(8,128)(2,1)S(1)} %bitcast.14, bf16[3,3,4,16]{3,2,1,0:T(4,128)(2,1)S(1)} %bitcast.20, bf16[3,3,16,32]{3,2,1,0:T(8,128)(2,1)S(1)} %bitcast.19, bf16[3,3,32,32]{3,2,1,0:T(8,128)(2,1)S(1)} %bitcast.16, ...), custom_call_target="tpu_custom_call" | custom-call | flops 20000000000 | bytes 8000000 | tf_op jit(solution)/shard_map/encoder/pallas_call | solution.py:358
  27.5 28.9 %all_to_all.22 = bf16[32,4,256]{2,1,0:T(4,128)(2,1)S(1)} all-to-all(bf16[32,4,256]{2,1,0:T(4,128)(2,1)S(1)} %all_to_all.14), channel_id=1, replica_groups=mesh['dp'=8,'tensor'=4] {'dp','tensor'}, dimensions={0} | all-to-all | bytes 131072 | tf_op jit(solution)/shard_map/all_to_all | solution.py:524
  56.4 0.0 copy-start.4
  56.4 0.0 copy-start.6
  56.4 0.0 copy-start.8
  56.4 0.0 copy-start.9
  56.4 0.0 collective-permute-done.2.refs_3_
  56.4 0.0 collective-permute-done.1.refs_2_
  56.4 0.0 collective-permute-done.refs_1_
  56.4 0.0 copy-done.7
  56.5 0.0 copy-start
  56.5 3.4 %copy-done = bf16[4,512,2048]{2,1,0:T(8,128)(2,1)S(1)} copy-done((bf16[4,512,2048]{2,1,0:T(8,128)(2,1)S(1)}, bf16[4,512,2048]{2,1,0:T(8,128)(2,1)}, u32[]{:S(2)}) %copy-start) | copy-done | bytes 8388632
  59.8 0.0 copy-start.1
  59.8 0.0 copy-start.2
  59.8 0.0 copy-start.3
  59.8 3.5 %recurrent.1.sums = f32[2048,128]{1,0:T(8,128)S(1)} custom-call(bf16[4,512,2048]{2,1,0:T(8,128)(2,1)S(1)} %copy-done, f32[4,512]{1,0:T(4,128)S(1)} %copy-done.7, bf16[512,128]{1,0:T(8,128)(2,1)S(1)} %multiply_convert_fusion.refs_0_, bf16[512,128]{1,0:T(8,128)(2,1)S(1)} %collective-permute-done.refs_1_, bf16[512,128]{1,0:T(8,128)(2,1)S(1)} %collective-permute-done.1.refs_2_, ...), custom_call_target="tpu_custom_call" | custom-call | flops 1073741824 | bytes 8388608 | tf_op jit(solution)/shard_map/recurrent/pallas_call | solution.py:402
  63.3 0.0 copy-done.4
  63.3 0.0 copy-done.6
  63.3 0.0 copy-done.8
  63.4 0.0 copy-done.9
  63.4 0.0 copy-done.1
  63.4 0.0 copy-done.2
  63.4 0.0 copy-done.3
  63.4 1.9 %core.1 = (f32[128,19]{1,0:T(8,128)S(1)}, f32[512,128]{1,0:T(8,128)}, f32[512,128]{1,0:T(8,128)}) custom-call(bf16[128,256]{1,0:T(8,128)(2,1)S(1)} %all_to_all.16.features, f32[2048,128]{1,0:T(8,128)S(1)} %recurrent.1.sums, bf16[4,512,256]{2,1,0:T(8,128)(2,1)S(1)} %copy-done.1, f32[512,128]{1,0:T(8,128)S(1)} %copy-done.2, f32[512,128]{1,0:T(8,128)S(1)} %copy-done.3, ...), custom_call_target="tpu_custom_call" | custom-call | flops 134217728 | bytes 4000000 | tf_op jit(solution)/shard_map/core/pallas_call | solution.py:464
  65.3 9.8 %all_to_all.23 = f32[32,4,19]{2,1,0:T(4,128)} all-to-all(f32[32,4,19]{2,1,0:T(4,128)S(1)} %bitcast.13), channel_id=1, replica_groups=mesh['dp'=8,'tensor'=4] {'dp','tensor'}, dimensions={0} | all-to-all | bytes 19456 | tf_op jit(solution)/shard_map/all_to_all | solution.py:529
  75.2 1.7 %answers.1 = f32[19,32]{1,0:T(8,128)} custom-call(s32[4,8]{1,0:T(4,128)} %counts.5, f32[128,19]{1,0:T(8,128)} %bitcast.21), custom_call_target="tpu_custom_call" | custom-call | tf_op jit(solution)/shard_map/answers/pallas_call | solution.py:497
  (2 shorter events, 0.0 us)
Async XLA Ops:
  2.3 54.2 %collective-permute-start.2 = (bf16[512,128]{1,0:T(8,128)(2,1)S(1)}, bf16[512,128]{1,0:T(8,128)(2,1)S(1)}, u32[]{:S(2)}, u32[]{:S(2)}) collective-permute-start(bf16[512,128]{1,0:T(8,128)(2,1)S(1)} %multiply_convert_fusion.refs_0_), channel_id=1, source_target_pairs={{0,3},{1,0},{2,1},{3,2},{4,7},{5,4},{6,5},{7,6},{8,11},{9,8},{10,9... | collective-permute-start | bytes 393224 | tf_op jit(solution)/shard_map/ppermute | solution.py:519
  7.4 49.0 %collective-permute-start.1 = (bf16[512,128]{1,0:T(8,128)(2,1)S(1)}, bf16[512,128]{1,0:T(8,128)(2,1)S(1)}, u32[]{:S(2)}, u32[]{:S(2)}) collective-permute-start(bf16[512,128]{1,0:T(8,128)(2,1)S(1)} %multiply_convert_fusion.refs_0_), channel_id=1, source_target_pairs={{0,2},{1,3},{2,0},{3,1},{4,6},{5,7},{6,4},{7,5},{8,10},{9,11},{10,... | collective-permute-start | bytes 393224 | tf_op jit(solution)/shard_map/ppermute | solution.py:519
  7.4 49.0 %collective-permute-start = (bf16[512,128]{1,0:T(8,128)(2,1)S(1)}, bf16[512,128]{1,0:T(8,128)(2,1)S(1)}, u32[]{:S(2)}, u32[]{:S(2)}) collective-permute-start(bf16[512,128]{1,0:T(8,128)(2,1)S(1)} %multiply_convert_fusion.refs_0_), channel_id=1, source_target_pairs={{0,1},{1,2},{2,3},{3,0},{4,5},{5,6},{6,7},{7,4},{8,9},{9,10},{10,1... | collective-permute-start | bytes 393224 | tf_op jit(solution)/shard_map/ppermute | solution.py:519
  8.4 0.7 copy-start.5
  9.1 1.8 %copy-start.10 = (bf16[32,4,84,84]{3,1,2,0:T(4,128)(2,1)S(1)}, bf16[32,4,84,84]{3,1,2,0:T(4,128)(2,1)}, u32[]{:S(2)}) copy-start(bf16[32,4,84,84]{3,1,2,0:T(4,128)(2,1)} %param.17) | copy-start | bytes 5419012
  10.9 1.6 %copy-start.11 = (bf16[256,3872]{0,1:T(8,128)(2,1)S(1)}, bf16[256,3872]{0,1:T(8,128)(2,1)}, u32[]{:S(2)}) copy-start(bf16[256,3872]{0,1:T(8,128)(2,1)} %param.28) | copy-start | bytes 5947396
  12.4 0.9 %copy-start.12 = (bf16[32,32,3,3]{1,0,3,2:T(8,128)(2,1)S(1)}, bf16[32,32,3,3]{1,0,3,2:T(8,128)(2,1)}, u32[]{:S(2)}) copy-start(bf16[32,32,3,3]{1,0,3,2:T(8,128)(2,1)} %param.25) | copy-start | bytes 55300
  13.3 0.9 %copy-start.13 = (bf16[32,32,3,3]{1,0,3,2:T(8,128)(2,1)S(1)}, bf16[32,32,3,3]{1,0,3,2:T(8,128)(2,1)}, u32[]{:S(2)}) copy-start(bf16[32,32,3,3]{1,0,3,2:T(8,128)(2,1)} %param.26) | copy-start | bytes 55300
  14.2 0.9 %copy-start.14 = (bf16[32,32,3,3]{1,0,3,2:T(8,128)(2,1)S(1)}, bf16[32,32,3,3]{1,0,3,2:T(8,128)(2,1)}, u32[]{:S(2)}) copy-start(bf16[32,32,3,3]{1,0,3,2:T(8,128)(2,1)} %param.27) | copy-start | bytes 55300
  15.1 0.8 copy-start.15
  15.8 0.7 copy-start.16
  16.5 0.8 %copy-start.17 = (s32[24,512]{1,0:T(8,128)S(1)}, s32[24,512]{1,0:T(8,128)}, u32[]{:S(2)}) copy-start(s32[24,512]{1,0:T(8,128)} %constant.4.clone.table) | copy-start | bytes 147460
  17.3 39.1 %copy-start.7 = (f32[4,512]{1,0:T(4,128)S(1)}, f32[4,512]{1,0:T(4,128)}, u32[]{:S(2)}) copy-start(f32[4,512]{1,0:T(4,128)} %bias.1) | copy-start | bytes 24580
  56.4 7.0 %copy-start.4 = (bf16[19,512]{1,0:T(8,128)(2,1)S(1)}, bf16[19,512]{1,0:T(8,128)(2,1)}, u32[]{:S(2)}) copy-start(bf16[19,512]{1,0:T(8,128)(2,1)} %heads.1) | copy-start | bytes 58372
  56.4 7.0 %copy-start.6 = (s32[4,8]{1,0:T(4,128)S(1)}, s32[4,8]{1,0:T(4,128)}, u32[]{:S(2)}) copy-start(s32[4,8]{1,0:T(4,128)} %counts.5) | copy-start | bytes 388
  56.4 7.0 %copy-start.8 = (s32[1,128]{1,0:T(1,128)S(1)}, s32[1,128]{1,0:T(1,128)}, u32[]{:S(2)}) copy-start(s32[1,128]{1,0:T(1,128)} %resets.1) | copy-start | bytes 1540
  56.4 7.0 %copy-start.9 = (s32[1,64]{1,0:T(1,128)S(1)}, s32[1,64]{1,0:T(1,128)}, u32[]{:S(2)}) copy-start(s32[1,64]{1,0:T(1,128)} %slots.1) | copy-start | bytes 772
  56.5 3.4 %copy-start = (bf16[4,512,2048]{2,1,0:T(8,128)(2,1)S(1)}, bf16[4,512,2048]{2,1,0:T(8,128)(2,1)}, u32[]{:S(2)}) copy-start(bf16[4,512,2048]{2,1,0:T(8,128)(2,1)} %weight.2) | copy-start | bytes 25165828
  59.8 3.5 %copy-start.1 = (bf16[4,512,256]{2,1,0:T(8,128)(2,1)S(1)}, bf16[4,512,256]{2,1,0:T(8,128)(2,1)}, u32[]{:S(2)}) copy-start(bf16[4,512,256]{2,1,0:T(8,128)(2,1)} %weight.3) | copy-start | bytes 3145732
  59.8 3.5 %copy-start.2 = (f32[512,128]{1,0:T(8,128)S(1)}, f32[512,128]{1,0:T(8,128)}, u32[]{:S(2)}) copy-start(f32[512,128]{1,0:T(8,128)} %hidden.1) | copy-start | bytes 786436
  59.8 3.5 %copy-start.3 = (f32[512,128]{1,0:T(8,128)S(1)}, f32[512,128]{1,0:T(8,128)}, u32[]{:S(2)}) copy-start(f32[512,128]{1,0:T(8,128)} %cell.1) | copy-start | bytes 786436

commit v2 on v1

--- a/solution.py
+++ b/solution.py
@@ -10,6 +10,7 @@
 
 F32, BF16, I32 = jnp.float32, jnp.bfloat16, jnp.int32
 LANES = 128
+VMEM_MOST = 67_043_328
 PACK = 16
 Y1, Y2, P3, Y4 = 12, 6, 2, 4
 NN = (((1,), (0,)), ((), ()))
@@ -17,6 +18,7 @@
 TN = (((0,), (0,)), ((), ()))
 VMEM = pl.BlockSpec(memory_space=pltpu.VMEM)
 SMEM = pl.BlockSpec(memory_space=pltpu.SMEM)
+HBM = pl.BlockSpec(memory_space=pltpu.HBM)
 
 
 def mm(a, b, dims=NN, precision=None):
@@ -105,14 +107,37 @@
 
 def encoder_kernel(
     z, lengths, dp, tensor, dp_index, tensor_index,
-    counts, frames, w1, w2, w3, r1, r2, proj, table, out,
-    p1, p2, p3, t1, t2, t3, t4, t5, g1, s1, g2, s2, g3, s3, total, x4, x5, projx,
+    *refs,
 ):
+    far, out, near = refs[:9], refs[9], refs[10:19]
+    p1, p2, p3, t1, t2, t3, t4, t5, g1, s1, g2, s2, g3, s3, total, x4, x5, projx, sems = refs[19:]
+    counts, table, w1, w2, w3, r1, r2, frames, proj = near
+    copies = [pltpu.make_async_copy(a, b, sems.at[i]) for i, (a, b) in enumerate(zip(far, near))]
+    for copy in copies:
+        copy.start()
+
     def row(i):
         return table[i : i + 1, : lengths[i]]
 
     def pick(rows, i):
         return one_hot(iota((rows, lengths[i]), 0) == row(i))
+
+    def zero_padding():
+        for ref, top, rows in ((g1, PACK, z.f * z.c0), (g2, z.c1, z.w1 * z.c1), (g3, 2 * z.c2, z.w2 * z.c2)):
+            for q in range(4):
+                ref[q, :top] = jnp.zeros((top, LANES), BF16)
+                low = ref.shape[1] - top - rows
+                ref[q, top + rows :] = jnp.zeros((low, LANES), BF16)
+        for ref in (x4, x5):
+            for q in range(3):
+                ref[q, : z.c2] = jnp.zeros((z.c2, z.wide), BF16)
+                low = ref.shape[1] - z.c2 - z.w3 * z.c2
+                ref[q, z.c2 + z.w3 * z.c2 :] = jnp.zeros((low, z.wide), BF16)
+        total[...] = jnp.zeros(total.shape, F32)
+
+    zero_padding()
+    for copy in copies[:7]:
+        copy.wait()
 
     for i in range(z.n1):
         p1[i] = pick(z.f, i)
@@ -156,18 +181,6 @@
     band_each(w3, (2 * P3 + 1) * z.c2, z.c2, z.c2, base + 6, t3)
     band_each(r1, Y4 * z.c2, z.c2, z.c2, base + 8, t4)
     band_each(r2, Y4 * z.c2, z.c2, z.c2, base + 8, t5)
-
-    for ref, top, rows in ((g1, PACK, z.f * z.c0), (g2, z.c1, z.w1 * z.c1), (g3, 2 * z.c2, z.w2 * z.c2)):
-        for q in range(4):
-            ref[q, :top] = jnp.zeros((top, LANES), BF16)
-            low = ref.shape[1] - top - rows
-            ref[q, top + rows :] = jnp.zeros((low, LANES), BF16)
-    for ref in (x4, x5):
-        for q in range(3):
-            ref[q, : z.c2] = jnp.zeros((z.c2, z.wide), BF16)
-            low = ref.shape[1] - z.c2 - z.w3 * z.c2
-            ref[q, z.c2 + z.w3 * z.c2 :] = jnp.zeros((low, z.wide), BF16)
-    total[...] = jnp.zeros(total.shape, F32)
 
     own = counts[tensor_index(), dp_index()]
     subs = lax.div(own + (z.n1 - 1), z.n1)
@@ -219,6 +232,7 @@
             s1[s, b * size : (b + 1) * size, :] = jnp.maximum(rows, 0.0).astype(BF16)
         return 0
 
+    copies[7].wait()
     lax.fori_loop(0, subs, conv_one, 0)
 
     def conv_rest(g, _):
@@ -297,6 +311,7 @@
     order = one_hot(iota((n, n), 0) == row(last))
     turned = jnp.swapaxes(encoded, 0, 1)
     turned = mm(turned, order).astype(BF16)
+    copies[8].wait()
     block = PACK * z.w3
     wanted = iota((block, block), 0)
     regroup = one_hot(((wanted >> log2(PACK)) == row(last + 1)) & ((wanted & (PACK - 1)) == row(last + 2)))
@@ -330,7 +345,20 @@
     images = jnp.transpose(frames, (0, 2, 1, 3)).reshape(z.cap, z.f * z.c0, z.f)
     ci_co, co_ci = (2, 3, 1, 0), (2, 3, 0, 1)
     n = z.w3 * z.c2
-    scratch = [
+    operands = (
+        counts,
+        jnp.asarray(table),
+        jnp.transpose(first, ci_co),
+        jnp.transpose(second, ci_co),
+        jnp.transpose(third, co_ci),
+        jnp.transpose(res_first, co_ci),
+        jnp.transpose(res_second, co_ci),
+        images,
+        jnp.transpose(projection),
+    )
+    scratch = [pltpu.SMEM(counts.shape, I32)]
+    scratch += [pltpu.VMEM(x.shape, x.dtype) for x in operands[1:]]
+    scratch += [
         pltpu.VMEM((z.n1, z.f, 4 * LANES), BF16),
         pltpu.VMEM((2 * LANES, 4 * LANES), BF16),
         pltpu.VMEM((LANES, 4 * LANES), BF16),
@@ -349,6 +377,7 @@
         pltpu.VMEM((3, ((z.blocks4 - 1) * Y4 + z.win4) * z.c2, z.wide), BF16),
         pltpu.VMEM((3, ((z.blocks4 - 1) * Y4 + z.win4) * z.c2, z.wide), BF16),
         pltpu.VMEM((z.w3, n, z.feat), BF16),
+        pltpu.SemaphoreType.DMA((len(operands),)),
     ]
     body = functools.partial(
         encoder_kernel, z, lengths, dp, tensor,
@@ -359,25 +388,15 @@
         body,
         name="encoder",
         out_shape=jax.ShapeDtypeStruct((dp * tensor * depth, z.feat), BF16),
-        in_specs=[SMEM] + [VMEM] * 8,
+        in_specs=[HBM] * len(operands),
         out_specs=VMEM,
         scratch_shapes=scratch,
-        compiler_params=pltpu.CompilerParams(vmem_limit_bytes=40 << 20),
+        compiler_params=pltpu.CompilerParams(vmem_limit_bytes=VMEM_MOST),
         cost_estimate=pl.CostEstimate(flops=20_000_000_000, bytes_accessed=8_000_000, transcendentals=0),
-    )(
-        counts,
-        images,
-        jnp.transpose(first, ci_co),
-        jnp.transpose(second, ci_co),
-        jnp.transpose(third, co_ci),
-        jnp.transpose(res_first, co_ci),
-        jnp.transpose(res_second, co_ci),
-        jnp.transpose(projection),
-        jnp.asarray(table),
-    )
-
-
-def recurrent_kernel(index, weight, bias, *refs):
+    )(*operands)
+
+
+def recurrent_kernel(index, weight, *refs):
     *pieces, out, held, sems = refs
     gates, share, _ = weight.shape
     width = pieces[0].shape[0]
@@ -387,23 +406,22 @@
     tensor = len(pieces)
     for q in range(gates):
         copies[q].wait()
-        column = jnp.broadcast_to(bias[q : q + 1, :], (out.shape[1], share))
         acc = None
         for back, piece in enumerate(pieces):
             low = pl.multiple_of(((index() - back) & (tensor - 1)) * width, width)
             part = mm(held[q, :, pl.ds(low, width)], piece[...])
             acc = part if acc is None else acc + part
-        out[q * share : (q + 1) * share, :] = acc + jnp.transpose(column)
-
-
-def recurrent(weight, bias, pieces):
+        out[q * share : (q + 1) * share, :] = acc
+
+
+def recurrent(weight, pieces):
     gates, share, hidden = weight.shape
     slots = pieces[0].shape[1]
     return pl.pallas_call(
         functools.partial(recurrent_kernel, lambda: lax.axis_index("tensor")),
         name="recurrent",
         out_shape=jax.ShapeDtypeStruct((gates * share, slots), F32),
-        in_specs=[pl.BlockSpec(memory_space=pl.ANY)] + [VMEM] * (1 + len(pieces)),
+        in_specs=[HBM] + [VMEM] * len(pieces),
         out_specs=VMEM,
         scratch_shapes=[
             pltpu.VMEM(weight.shape, BF16),
@@ -413,10 +431,10 @@
         cost_estimate=pl.CostEstimate(
             flops=2 * gates * share * hidden * slots, bytes_accessed=2 * gates * share * hidden, transcendentals=0
         ),
-    )(weight, bias, *pieces)
-
-
-def core_kernel(dp_index, features, sums, weight, hidden, cell, heads, slots, counts, resets, sent, hidden_out, cell_out):
+    )(weight, *pieces)
+
+
+def core_kernel(dp_index, features, sums, bias, weight, hidden, cell, heads, slots, counts, resets, sent, hidden_out, cell_out):
     tensor, dp = counts.shape
     rows, count = features.shape[0], slots.shape[1]
     depth = rows // (dp * tensor)
@@ -449,7 +467,8 @@
 
     def gate(q):
         low = q * share
-        return mm(weight[q], inputs) + sums[low : low + share, :]
+        column = jnp.transpose(jnp.broadcast_to(bias[q : q + 1, :], (places, share)))
+        return mm(weight[q], inputs) + (sums[low : low + share, :] * keep + column)
 
     next_cell = jax.nn.sigmoid(gate(1)) * (old_cell * keep) + jax.nn.sigmoid(gate(0)) * jnp.tanh(gate(2))
     next_hidden = jax.nn.sigmoid(gate(3)) * jnp.tanh(next_cell)
@@ -459,7 +478,7 @@
     hidden_out[...] = jnp.where(taken, next_hidden, hidden[...])
 
 
-def core(features, sums, weight, hidden, cell, heads, slots, counts, resets):
+def core(features, sums, bias, weight, hidden, cell, heads, slots, counts, resets):
     share = hidden.shape[0]
     return pl.pallas_call(
         functools.partial(core_kernel, lambda: lax.axis_index("dp")),
@@ -469,13 +488,13 @@
             jax.ShapeDtypeStruct(hidden.shape, F32),
             jax.ShapeDtypeStruct(cell.shape, F32),
         ),
-        in_specs=[VMEM] * 9,
+        in_specs=[VMEM] * 10,
         out_specs=(VMEM,) * 3,
         compiler_params=pltpu.CompilerParams(vmem_limit_bytes=24 << 20),
         cost_estimate=pl.CostEstimate(
             flops=8 * share * weight.shape[2] * hidden.shape[1], bytes_accessed=4_000_000, transcendentals=0
         ),
-    )(features, sums, weight, hidden, cell, heads, slots, counts, resets)
+    )(features, sums, bias, weight, hidden, cell, heads, slots, counts, resets)
 
 
 def answers_kernel(tensor, dp_index, tensor_index, counts, received, out):
@@ -514,17 +533,18 @@
     projection, input_weight, recur_weight, gate_bias, head_weight,
 ):
     tensor = lax.axis_size("tensor")
-    own = (hidden_state * (1 - reset_flags).astype(F32)).astype(BF16)
+    own = hidden_state.astype(BF16)
     pieces = [own] + [
         lax.ppermute(own, "tensor", [(i, (i + back) % tensor) for i in range(tensor)])
         for back in range(1, tensor)
     ]
     kernels = (conv_first, conv_second, conv_third, res_first, res_second)
     features = encode_rows(frames, counts, kernels, projection)
+    features, pieces = lax.optimization_barrier((features, pieces))
     features = lax.all_to_all(features, ("dp", "tensor"), 0, 0, tiled=True)
-    sums = recurrent(recur_weight, gate_bias, pieces)
+    sums = recurrent(recur_weight, pieces)
     sent, hidden_after, cell_after = core(
-        features, sums, input_weight, hidden_state, cell_state, head_weight, slot_ids, counts, reset_flags
+        features, sums, gate_bias, input_weight, hidden_state, cell_state, head_weight, slot_ids, counts, reset_flags
     )
     received = lax.all_to_all(sent, ("dp", "tensor"), 0, 0, tiled=True)
     return answers(counts, received, frames.shape[0]), hidden_after, cell_after

time: 76.6 us -> 70 us (0.914); the launches traced: 76.8 us -> 69.2 us
  blocking collectives: 38.7 us -> 13.2 us
  starting transfers between devices: 6.14 us -> 20.1 us
  Pallas kernels: 17.2 us -> 28.5 us
  local copies, waits for them, and re-layouts: 12.4 us -> 4.93 us
    all_to_all x1 -> x0, blocking collectives: 28.9 us -> none  [body(): features = lax.all_to_all(features, ('dp', 'tensor'), 0, 0, tiled=True)]
    all_to_all x0 -> x1, starting transfers between devices: none -> 14.1 us  [body(): features = lax.all_to_all(features, ('dp', 'tensor'), 0, 0, tiled=True)]
    unnamed x36 -> x18, local copies, waits for them, and re-layouts: 12.3 us -> 3.42 us
    pallas_call x1, Pallas kernels: 10.1 us -> 18.2 us  [encode_rows(): pl.pallas_call(body, name='encoder', out_shape=jax.ShapeDtypeStruct((dp *...]
    all_to_all x1, blocking collectives: 9.84 us -> 13.2 us  [body(): received = lax.all_to_all(sent, ('dp', 'tensor'), 0, 0, tiled=True)]
    pallas_call x1, Pallas kernels: 3.47 us -> 6.71 us  [recurrent(): pl.pallas_call(functools.partial(recurrent_kernel, lambda: lax.axis_index...]
    all_to_all x2, local copies, waits for them, and re-layouts: 0.04 us -> 1.51 us  [body(): features = lax.all_to_all(features, ('dp', 'tensor'), 0, 0, tiled=True)]
  transfers between devices with their start and end apart: 3 -> 4, of which waited for: 0 -> 0; matrix products, arithmetic and copies ran while one was open for 0% -> 0% of each run, Pallas kernels for 13% -> 36%
where the time goes in v2:
time: 70 us; the launch traced here: 69.2 us
  Pallas kernels  28.5 us (41%)
  starting transfers between devices  20.1 us (29%)
  blocking collectives  13.2 us (19%)
  local copies, waits for them, and re-layouts  4.93 us (7%)
  other arithmetic  1.62 us (2%)
  between operations  0.8 us (1%)
    pallas_call x1, Pallas kernels, encode_rows(): pl.pallas_call(body, name='encoder', out_shape=jax.ShapeDtypeStruct((dp *...  18.2 us
    all_to_all x1, starting transfers between devices, body(): features = lax.all_to_all(features, ('dp', 'tensor'), 0, 0, tiled=True)  14.1 us
    all_to_all x1, blocking collectives, body(): received = lax.all_to_all(sent, ('dp', 'tensor'), 0, 0, tiled=True)  13.2 us
    pallas_call x1, Pallas kernels, recurrent(): pl.pallas_call(functools.partial(recurrent_kernel, lambda: lax.axis_index...  6.71 us
    ppermute x3, starting transfers between devices, body(): lax.ppermute(own, 'tensor', [(i, (i + back) % tensor) for i in range(tens...  6.09 us
    unnamed x18, local copies, waits for them, and re-layouts  3.42 us
    pallas_call x1, Pallas kernels, core(): pl.pallas_call(functools.partial(core_kernel, lambda: lax.axis_index('dp'...  1.95 us
    pallas_call x1, Pallas kernels, answers(): pl.pallas_call(functools.partial(answers_kernel, counts.shape[0], lambda:...  1.67 us
  transfers between devices with their start and end apart: 4, of which 0 were waited for; matrix products, arithmetic and copies ran while one was open for 0% of the time, Pallas kernels for 36%

profile of v2, /device:TPU:0, one launch (start us, length us, event | category | flops | bytes accessed | tf_op | source)
XLA Modules:
  0.0 69.2 jit_solution(1167503997034775457)
XLA Ops:
  0.6 1.6 %convert_element_type.3.refs_0_ = bf16[512,128]{1,0:T(8,128)(2,1)} convert(f32[512,128]{1,0:T(8,128)} %hidden.1) | non-fusion elementwise | flops 65536 | bytes 393216 | tf_op jit(solution)/shard_map/convert_element_type | solution.py:536
  2.2 5.1 %collective-permute-start.2 = (bf16[512,128]{1,0:T(8,128)(2,1)}, bf16[512,128]{1,0:T(8,128)(2,1)}, u32[]{:S(2)}, u32[]{:S(2)}) collective-permute-start(bf16[512,128]{1,0:T(8,128)(2,1)} %convert_element_type.3.refs_0_), channel_id=1, source_target_pairs={{0,3},{1,0},{2,1},{3,2},{4,7},{5,4},{6,5},{7,6},{8,11},{9,8},{10,9... | collective-permute-start | bytes 393224 | tf_op jit(solution)/shard_map/ppermute | solution.py:538
  7.3 0.0 collective-permute-start.1
  7.3 1.0 %collective-permute-start = (bf16[512,128]{1,0:T(8,128)(2,1)}, bf16[512,128]{1,0:T(8,128)(2,1)}, u32[]{:S(2)}, u32[]{:S(2)}) collective-permute-start(bf16[512,128]{1,0:T(8,128)(2,1)} %convert_element_type.3.refs_0_), channel_id=1, source_target_pairs={{0,1},{1,2},{2,3},{3,0},{4,5},{5,6},{6,7},{7,4},{8,9},{9,10},{10,1... | collective-permute-start | bytes 393224 | tf_op jit(solution)/shard_map/ppermute | solution.py:538
  8.3 18.2 %encoder.1 = bf16[128,256]{1,0:T(8,128)(2,1)} custom-call(s32[4,8]{1,0:T(4,128)} %counts.3, s32[24,512]{1,0:T(8,128)} %constant.2.clone.refs_1_, bf16[3,3,4,16]{3,2,1,0:T(4,128)(2,1)} %bitcast.19, bf16[3,3,16,32]{3,2,1,0:T(8,128)(2,1)} %bitcast.18, bf16[3,3,32,32]{3,2,1,0:T(8,128)(2,1)} %bitcast.15, bf16[3,3,32,32]{3,2,1,0:T(8,128)(2,1)} %bitcast.16, ...), custom_call_target="tpu_custom_call" | custom-call | flops 20000000000 | bytes 8000000 | tf_op jit(solution)/shard_map/encoder/pallas_call | solution.py:387
  26.5 0.0 collective-permute-done.2.refs_3_
  26.5 0.0 collective-permute-done.1.refs_2_
  26.5 0.0 collective-permute-done.refs_1_
  26.5 1.5 %all_to_all.14 = bf16[32,4,256]{2,1,0:T(4,128)(2,1)} reshape(bf16[128,256]{1,0:T(8,128)(2,1)} %encoder.1) | data formatting | bytes 131072 | tf_op jit(solution)/shard_map/all_to_all | solution.py:544
  28.0 14.1 %all-to-all-start = ((bf16[32,4,256]{2,1,0:T(4,128)(2,1)}), bf16[32,4,256]{2,1,0:T(4,128)(2,1)S(1)}, u32[]{:S(2)}, u32[]{:S(2)}) async-start(bf16[32,4,256]{2,1,0:T(4,128)(2,1)} %all_to_all.14), calls=%async_computation | async-start | bytes 131072 | tf_op jit(solution)/shard_map/all_to_all | solution.py:544
  42.1 0.0 copy-start
  42.1 3.4 %copy-done = bf16[4,512,2048]{2,1,0:T(8,128)(2,1)S(1)} copy-done((bf16[4,512,2048]{2,1,0:T(8,128)(2,1)S(1)}, bf16[4,512,2048]{2,1,0:T(8,128)(2,1)}, u32[]{:S(2)}) %copy-start) | copy-done | bytes 8388632
  45.5 0.0 copy-start.1
  45.5 0.0 copy-start.2
  45.5 0.0 copy-start.3
  45.5 0.0 copy-start.4
  45.5 0.0 copy-start.5
  45.5 0.0 copy-start.6
  45.5 0.0 copy-start.7
  45.5 0.0 copy-start.8
  45.5 6.7 %recurrent.1.sums = f32[2048,128]{1,0:T(8,128)S(1)} custom-call(bf16[4,512,2048]{2,1,0:T(8,128)(2,1)S(1)} %copy-done, bf16[512,128]{1,0:T(8,128)(2,1)} %convert_element_type.3.refs_0_, bf16[512,128]{1,0:T(8,128)(2,1)} %collective-permute-done.refs_1_, bf16[512,128]{1,0:T(8,128)(2,1)} %collective-permute-done.1.refs_2_, ...), custom_call_target="tpu_custom_call" | custom-call | flops 1073741824 | bytes 8388608 | tf_op jit(solution)/shard_map/recurrent/pallas_call | solution.py:420
  52.3 0.0 all-to-all-done
  52.3 0.0 copy-done.1
  52.3 0.0 copy-done.2
  52.3 0.0 copy-done.3
  52.3 0.0 copy-done.4
  52.3 0.0 copy-done.5
  52.3 0.0 copy-done.6
  52.3 0.0 copy-done.7
  52.4 0.0 copy-done.8
  52.4 2.0 %core.1 = (f32[128,19]{1,0:T(8,128)S(1)}, f32[512,128]{1,0:T(8,128)}, f32[512,128]{1,0:T(8,128)}) custom-call(bf16[128,256]{1,0:T(8,128)(2,1)S(1)} %all_to_all.16.features, f32[2048,128]{1,0:T(8,128)S(1)} %recurrent.1.sums, f32[4,512]{1,0:T(4,128)S(1)} %copy-done.5, bf16[4,512,256]{2,1,0:T(8,128)(2,1)S(1)} %copy-done.2, f32[512,128]{1,0:T(8,128)S(1)} %copy-done.1, ...), custom_call_target="tpu_custom_call" | custom-call | flops 134217728 | bytes 4000000 | tf_op jit(solution)/shard_map/core/pallas_call | solution.py:483
  54.3 13.2 %all_to_all.22 = f32[32,4,19]{2,1,0:T(4,128)} all-to-all(f32[32,4,19]{2,1,0:T(4,128)S(1)} %bitcast.11), channel_id=1, replica_groups=mesh['dp'=8,'tensor'=4] {'dp','tensor'}, dimensions={0} | all-to-all | bytes 19456 | tf_op jit(solution)/shard_map/all_to_all | solution.py:549
  67.5 1.7 %answers.1 = f32[19,32]{1,0:T(8,128)} custom-call(s32[4,8]{1,0:T(4,128)} %counts.3, f32[128,19]{1,0:T(8,128)} %bitcast.12), custom_call_target="tpu_custom_call" | custom-call | tf_op jit(solution)/shard_map/answers/pallas_call | solution.py:516
  (1 shorter events, 0.0 us)
Async XLA Ops:
  2.2 24.3 %collective-permute-start.2 = (bf16[512,128]{1,0:T(8,128)(2,1)}, bf16[512,128]{1,0:T(8,128)(2,1)}, u32[]{:S(2)}, u32[]{:S(2)}) collective-permute-start(bf16[512,128]{1,0:T(8,128)(2,1)} %convert_element_type.3.refs_0_), channel_id=1, source_target_pairs={{0,3},{1,0},{2,1},{3,2},{4,7},{5,4},{6,5},{7,6},{8,11},{9,8},{10,9... | collective-permute-start | bytes 393224 | tf_op jit(solution)/shard_map/ppermute | solution.py:538
  7.3 19.2 %collective-permute-start.1 = (bf16[512,128]{1,0:T(8,128)(2,1)}, bf16[512,128]{1,0:T(8,128)(2,1)}, u32[]{:S(2)}, u32[]{:S(2)}) collective-permute-start(bf16[512,128]{1,0:T(8,128)(2,1)} %convert_element_type.3.refs_0_), channel_id=1, source_target_pairs={{0,2},{1,3},{2,0},{3,1},{4,6},{5,7},{6,4},{7,5},{8,10},{9,11},{10,... | collective-permute-start | bytes 393224 | tf_op jit(solution)/shard_map/ppermute | solution.py:538
  7.3 19.2 %collective-permute-start = (bf16[512,128]{1,0:T(8,128)(2,1)}, bf16[512,128]{1,0:T(8,128)(2,1)}, u32[]{:S(2)}, u32[]{:S(2)}) collective-permute-start(bf16[512,128]{1,0:T(8,128)(2,1)} %convert_element_type.3.refs_0_), channel_id=1, source_target_pairs={{0,1},{1,2},{2,3},{3,0},{4,5},{5,6},{6,7},{7,4},{8,9},{9,10},{10,1... | collective-permute-start | bytes 393224 | tf_op jit(solution)/shard_map/ppermute | solution.py:538
  28.0 24.2 %all-to-all-start = ((bf16[32,4,256]{2,1,0:T(4,128)(2,1)}), bf16[32,4,256]{2,1,0:T(4,128)(2,1)S(1)}, u32[]{:S(2)}, u32[]{:S(2)}) async-start(bf16[32,4,256]{2,1,0:T(4,128)(2,1)} %all_to_all.14), calls=%async_computation | async-start | bytes 131072 | tf_op jit(solution)/shard_map/all_to_all | solution.py:544
  42.1 3.4 %copy-start = (bf16[4,512,2048]{2,1,0:T(8,128)(2,1)S(1)}, bf16[4,512,2048]{2,1,0:T(8,128)(2,1)}, u32[]{:S(2)}) copy-start(bf16[4,512,2048]{2,1,0:T(8,128)(2,1)} %weight.2) | copy-start | bytes 25165828
  45.5 6.8 %copy-start.1 = (f32[512,128]{1,0:T(8,128)S(1)}, f32[512,128]{1,0:T(8,128)}, u32[]{:S(2)}) copy-start(f32[512,128]{1,0:T(8,128)} %hidden.1) | copy-start | bytes 786436
  45.5 6.8 %copy-start.2 = (bf16[4,512,256]{2,1,0:T(8,128)(2,1)S(1)}, bf16[4,512,256]{2,1,0:T(8,128)(2,1)}, u32[]{:S(2)}) copy-start(bf16[4,512,256]{2,1,0:T(8,128)(2,1)} %weight.3) | copy-start | bytes 3145732
  45.5 6.8 %copy-start.3 = (f32[512,128]{1,0:T(8,128)S(1)}, f32[512,128]{1,0:T(8,128)}, u32[]{:S(2)}) copy-start(f32[512,128]{1,0:T(8,128)} %cell.1) | copy-start | bytes 786436
  45.5 6.8 %copy-start.4 = (bf16[19,512]{1,0:T(8,128)(2,1)S(1)}, bf16[19,512]{1,0:T(8,128)(2,1)}, u32[]{:S(2)}) copy-start(bf16[19,512]{1,0:T(8,128)(2,1)} %heads.1) | copy-start | bytes 58372
  45.5 6.8 %copy-start.5 = (f32[4,512]{1,0:T(4,128)S(1)}, f32[4,512]{1,0:T(4,128)}, u32[]{:S(2)}) copy-start(f32[4,512]{1,0:T(4,128)} %bias.1) | copy-start | bytes 24580
  45.5 6.8 %copy-start.6 = (s32[4,8]{1,0:T(4,128)S(1)}, s32[4,8]{1,0:T(4,128)}, u32[]{:S(2)}) copy-start(s32[4,8]{1,0:T(4,128)} %counts.3) | copy-start | bytes 388
  45.5 6.8 %copy-start.7 = (s32[1,64]{1,0:T(1,128)S(1)}, s32[1,64]{1,0:T(1,128)}, u32[]{:S(2)}) copy-start(s32[1,64]{1,0:T(1,128)} %slots.1) | copy-start | bytes 772
  45.5 6.8 %copy-start.8 = (s32[1,128]{1,0:T(1,128)S(1)}, s32[1,128]{1,0:T(1,128)}, u32[]{:S(2)}) copy-start(s32[1,128]{1,0:T(1,128)} %resets.1) | copy-start | bytes 1540

commit v3 on v2

--- a/solution.py
+++ b/solution.py
@@ -334,7 +334,7 @@
     receiver, level = r >> log2(tensor * depth), r & (depth - 1)
     arrival = ((receiver - start) & (dp - 1)) + level * dp
     route = one_hot((iota(shape, 1) == arrival) & (arrival < own))
-    out[...] = mm(route, features).astype(BF16)
+    out[...] = mm(route, features).astype(BF16).reshape(out.shape)
 
 
 def encode_rows(frames, counts, kernels, projection):
@@ -387,7 +387,7 @@
     return pl.pallas_call(
         body,
         name="encoder",
-        out_shape=jax.ShapeDtypeStruct((dp * tensor * depth, z.feat), BF16),
+        out_shape=jax.ShapeDtypeStruct((dp * tensor, depth, z.feat), BF16),
         in_specs=[HBM] * len(operands),
         out_specs=VMEM,
         scratch_shapes=scratch,
@@ -427,7 +427,7 @@
             pltpu.VMEM(weight.shape, BF16),
             pltpu.SemaphoreType.DMA((gates,)),
         ],
-        compiler_params=pltpu.CompilerParams(vmem_limit_bytes=24 << 20),
+        compiler_params=pltpu.CompilerParams(vmem_limit_bytes=57 << 20),
         cost_estimate=pl.CostEstimate(
             flops=2 * gates * share * hidden * slots, bytes_accessed=2 * gates * share * hidden, transcendentals=0
         ),
@@ -436,8 +436,8 @@
 
 def core_kernel(dp_index, features, sums, bias, weight, hidden, cell, heads, slots, counts, resets, sent, hidden_out, cell_out):
     tensor, dp = counts.shape
-    rows, count = features.shape[0], slots.shape[1]
-    depth = rows // (dp * tensor)
+    depth, count = features.shape[1], slots.shape[1]
+    rows = dp * tensor * depth
     share, places = hidden.shape
     mine = dp_index()
     exact = lax.Precision.HIGHEST
@@ -461,7 +461,7 @@
     of_slot = one_hot(iota((places, count), 0) == slots[...])
     chosen = mm(to_row, of_slot, NT)
     taken = jnp.sum(chosen, axis=0, keepdims=True) > 0.5
-    inputs = mm(features[...], chosen.astype(BF16), TN).astype(BF16)
+    inputs = mm(features[...].reshape(rows, -1), chosen.astype(BF16), TN).astype(BF16)
     keep = 1.0 - resets[...].astype(F32)
     old_cell = cell[...]
 
@@ -484,7 +484,7 @@
         functools.partial(core_kernel, lambda: lax.axis_index("dp")),
         name="core",
         out_shape=(
-            jax.ShapeDtypeStruct((features.shape[0], heads.shape[0]), F32),
+            jax.ShapeDtypeStruct((features.shape[0] * features.shape[1], heads.shape[0]), F32),
             jax.ShapeDtypeStruct(hidden.shape, F32),
             jax.ShapeDtypeStruct(cell.shape, F32),
         ),

time: 70 us -> 69 us (0.986)
  starting transfers between devices: 20.1 us -> 24.7 us
  local copies, waits for them, and re-layouts: 4.93 us -> 1.27 us
  Pallas kernels: 28.5 us -> 27.1 us
    all_to_all x1, starting transfers between devices: 14.1 us -> 18.6 us  [body(): features = lax.all_to_all(features, ('dp', 'tensor'), 0, 0, tiled=True)]
    pallas_call x1, Pallas kernels: 18.2 us -> 14.8 us  [encode_rows(): pl.pallas_call(body, name='encoder', out_shape=jax.ShapeDtypeStruct((dp *...]
    unnamed x18, local copies, waits for them, and re-layouts: 3.42 us -> 1.27 us
    pallas_call x1, Pallas kernels: 6.71 us -> 8.72 us  [recurrent(): pl.pallas_call(functools.partial(recurrent_kernel, lambda: lax.axis_index...]
    all_to_all x2 -> x0, local copies, waits for them, and re-layouts: 1.51 us -> none  [body(): features = lax.all_to_all(features, ('dp', 'tensor'), 0, 0, tiled=True)]
  transfers between devices with their start and end apart: 4 -> 4, of which waited for: 0 -> 0; matrix products, arithmetic and copies ran while one was open for 0% -> 0% of each run, Pallas kernels for 36% -> 34%
where the time goes in v3:
time: 69 us; the launch traced here: 68.7 us
  Pallas kernels  27.1 us (39%)
  starting transfers between devices  24.7 us (36%)
  blocking collectives  13.2 us (19%)
  other arithmetic  1.62 us (2%)
  local copies, waits for them, and re-layouts  1.27 us (2%)
  between operations  0.82 us (1%)
    all_to_all x1, starting transfers between devices, body(): features = lax.all_to_all(features, ('dp', 'tensor'), 0, 0, tiled=True)  18.6 us
    pallas_call x1, Pallas kernels, encode_rows(): pl.pallas_call(body, name='encoder', out_shape=jax.ShapeDtypeStruct((dp *...  14.8 us
    all_to_all x1, blocking collectives, body(): received = lax.all_to_all(sent, ('dp', 'tensor'), 0, 0, tiled=True)  13.2 us
    pallas_call x1, Pallas kernels, recurrent(): pl.pallas_call(functools.partial(recurrent_kernel, lambda: lax.axis_index...  8.72 us
    ppermute x3, starting transfers between devices, body(): lax.ppermute(own, 'tensor', [(i, (i + back) % tensor) for i in range(tens...  6.09 us
    pallas_call x1, Pallas kernels, core(): pl.pallas_call(functools.partial(core_kernel, lambda: lax.axis_index('dp'...  1.95 us
    pallas_call x1, Pallas kernels, answers(): pl.pallas_call(functools.partial(answers_kernel, counts.shape[0], lambda:...  1.67 us
    convert_element_type x1, other arithmetic, body(): own = hidden_state.astype(BF16)  1.62 us
  transfers between devices with their start and end apart: 4, of which 0 were waited for; matrix products, arithmetic and copies ran while one was open for 0% of the time, Pallas kernels for 34%

profile of v3, /device:TPU:0, one launch (start us, length us, event | category | flops | bytes accessed | tf_op | source)
XLA Modules:
  0.0 68.7 jit_solution(6917219727236524698)
XLA Ops:
  0.6 1.6 %convert_element_type.3.refs_0_ = bf16[512,128]{1,0:T(8,128)(2,1)} convert(f32[512,128]{1,0:T(8,128)} %hidden.1) | non-fusion elementwise | flops 65536 | bytes 393216 | tf_op jit(solution)/shard_map/convert_element_type | solution.py:536
  2.2 5.1 %collective-permute-start.2 = (bf16[512,128]{1,0:T(8,128)(2,1)}, bf16[512,128]{1,0:T(8,128)(2,1)}, u32[]{:S(2)}, u32[]{:S(2)}) collective-permute-start(bf16[512,128]{1,0:T(8,128)(2,1)} %convert_element_type.3.refs_0_), channel_id=1, source_target_pairs={{0,3},{1,0},{2,1},{3,2},{4,7},{5,4},{6,5},{7,6},{8,11},{9,8},{10,9... | collective-permute-start | bytes 393224 | tf_op jit(solution)/shard_map/ppermute | solution.py:538
  7.3 0.0 collective-permute-start.1
  7.3 1.0 %collective-permute-start = (bf16[512,128]{1,0:T(8,128)(2,1)}, bf16[512,128]{1,0:T(8,128)(2,1)}, u32[]{:S(2)}, u32[]{:S(2)}) collective-permute-start(bf16[512,128]{1,0:T(8,128)(2,1)} %convert_element_type.3.refs_0_), channel_id=1, source_target_pairs={{0,1},{1,2},{2,3},{3,0},{4,5},{5,6},{6,7},{7,4},{8,9},{9,10},{10,1... | collective-permute-start | bytes 393224 | tf_op jit(solution)/shard_map/ppermute | solution.py:538
  8.3 14.8 %encoder.1 = bf16[32,4,256]{2,1,0:T(4,128)(2,1)} custom-call(s32[4,8]{1,0:T(4,128)} %counts.3, s32[24,512]{1,0:T(8,128)} %constant.2.clone.refs_1_, bf16[3,3,4,16]{3,2,1,0:T(4,128)(2,1)} %bitcast.19, bf16[3,3,16,32]{3,2,1,0:T(8,128)(2,1)} %bitcast.18, bf16[3,3,32,32]{3,2,1,0:T(8,128)(2,1)} %bitcast.15, bf16[3,3,32,32]{3,2,1,0:T(8,128)(2,1)} %bitcast.16, ...), custom_call_target="tpu_custom_call" | custom-call | flops 20000000000 | bytes 8000000 | tf_op jit(solution)/shard_map/encoder/pallas_call | solution.py:387
  23.1 0.0 collective-permute-done.2.refs_3_
  23.1 0.0 collective-permute-done.1.refs_2_
  23.1 0.0 collective-permute-done.refs_1_
  23.2 18.6 %all-to-all-start = ((bf16[32,4,256]{2,1,0:T(4,128)(2,1)}), bf16[32,4,256]{2,1,0:T(4,128)(2,1)S(1)}, u32[]{:S(2)}, u32[]{:S(2)}) async-start(bf16[32,4,256]{2,1,0:T(4,128)(2,1)} %encoder.1), calls=%async_computation | async-start | bytes 131072 | tf_op jit(solution)/shard_map/all_to_all | solution.py:544
  41.7 0.0 copy-start.1
  41.7 0.0 copy-start.2
  41.8 0.0 copy-start.3
  41.8 0.0 copy-start.4
  41.8 0.0 copy-start.5
  41.8 0.0 copy-start.6
  41.8 0.0 copy-start.7
  41.8 0.0 copy-start.8
  41.8 8.7 %recurrent.1.sums = f32[2048,128]{1,0:T(8,128)} custom-call(bf16[4,512,2048]{2,1,0:T(8,128)(2,1)} %weight.2, bf16[512,128]{1,0:T(8,128)(2,1)} %convert_element_type.3.refs_0_, bf16[512,128]{1,0:T(8,128)(2,1)} %collective-permute-done.refs_1_, bf16[512,128]{1,0:T(8,128)(2,1)} %collective-permute-done.1.refs_2_, bf16[512,128]{1,0:T(8,128)(2,1)} %collective-permute-done.2.refs_3_), custom_call_target="tpu_custom_call" | custom-call | flops 1073741824 | bytes 8388608 | tf_op jit(solution)/shard_map/recurrent/pallas_call | solution.py:420
  50.6 0.0 all-to-all-done.features
  50.6 0.0 copy-done.1
  50.6 0.0 copy-done.2
  50.6 0.0 copy-done.3
  50.6 0.0 copy-done.4
  50.6 0.0 copy-done.5
  50.6 0.0 copy-done.6
  50.6 0.0 copy-done.7
  50.6 0.0 copy-done.8
  50.6 0.0 copy-start
  50.7 1.2 %copy-done = f32[2048,128]{1,0:T(8,128)S(1)} copy-done((f32[2048,128]{1,0:T(8,128)S(1)}, f32[2048,128]{1,0:T(8,128)}, u32[]{:S(2)}) %copy-start) | copy-done | bytes 1048600
  51.9 1.9 %core.1 = (f32[128,19]{1,0:T(8,128)S(1)}, f32[512,128]{1,0:T(8,128)}, f32[512,128]{1,0:T(8,128)}) custom-call(bf16[32,4,256]{2,1,0:T(4,128)(2,1)S(1)} %all-to-all-done.features, f32[2048,128]{1,0:T(8,128)S(1)} %copy-done, f32[4,512]{1,0:T(4,128)S(1)} %copy-done.5, bf16[4,512,256]{2,1,0:T(8,128)(2,1)S(1)} %copy-done.2, f32[512,128]{1,0:T(8,128)S(1)} %copy-done.1, ...), custom_call_target="tpu_custom_call" | custom-call | flops 134217728 | bytes 4000000 | tf_op jit(solution)/shard_map/core/pallas_call | solution.py:483
  53.8 13.2 %all_to_all.16 = f32[32,4,19]{2,1,0:T(4,128)} all-to-all(f32[32,4,19]{2,1,0:T(4,128)S(1)} %bitcast.11), channel_id=1, replica_groups=mesh['dp'=8,'tensor'=4] {'dp','tensor'}, dimensions={0} | all-to-all | bytes 19456 | tf_op jit(solution)/shard_map/all_to_all | solution.py:549
  67.0 1.7 %answers.1 = f32[19,32]{1,0:T(8,128)} custom-call(s32[4,8]{1,0:T(4,128)} %counts.3, f32[128,19]{1,0:T(8,128)} %bitcast.12), custom_call_target="tpu_custom_call" | custom-call | tf_op jit(solution)/shard_map/answers/pallas_call | solution.py:516
Async XLA Ops:
  2.2 20.9 %collective-permute-start.2 = (bf16[512,128]{1,0:T(8,128)(2,1)}, bf16[512,128]{1,0:T(8,128)(2,1)}, u32[]{:S(2)}, u32[]{:S(2)}) collective-permute-start(bf16[512,128]{1,0:T(8,128)(2,1)} %convert_element_type.3.refs_0_), channel_id=1, source_target_pairs={{0,3},{1,0},{2,1},{3,2},{4,7},{5,4},{6,5},{7,6},{8,11},{9,8},{10,9... | collective-permute-start | bytes 393224 | tf_op jit(solution)/shard_map/ppermute | solution.py:538
  7.3 15.8 %collective-permute-start.1 = (bf16[512,128]{1,0:T(8,128)(2,1)}, bf16[512,128]{1,0:T(8,128)(2,1)}, u32[]{:S(2)}, u32[]{:S(2)}) collective-permute-start(bf16[512,128]{1,0:T(8,128)(2,1)} %convert_element_type.3.refs_0_), channel_id=1, source_target_pairs={{0,2},{1,3},{2,0},{3,1},{4,6},{5,7},{6,4},{7,5},{8,10},{9,11},{10,... | collective-permute-start | bytes 393224 | tf_op jit(solution)/shard_map/ppermute | solution.py:538
  7.3 15.8 %collective-permute-start = (bf16[512,128]{1,0:T(8,128)(2,1)}, bf16[512,128]{1,0:T(8,128)(2,1)}, u32[]{:S(2)}, u32[]{:S(2)}) collective-permute-start(bf16[512,128]{1,0:T(8,128)(2,1)} %convert_element_type.3.refs_0_), channel_id=1, source_target_pairs={{0,1},{1,2},{2,3},{3,0},{4,5},{5,6},{6,7},{7,4},{8,9},{9,10},{10,1... | collective-permute-start | bytes 393224 | tf_op jit(solution)/shard_map/ppermute | solution.py:538
  23.2 27.4 %all-to-all-start = ((bf16[32,4,256]{2,1,0:T(4,128)(2,1)}), bf16[32,4,256]{2,1,0:T(4,128)(2,1)S(1)}, u32[]{:S(2)}, u32[]{:S(2)}) async-start(bf16[32,4,256]{2,1,0:T(4,128)(2,1)} %encoder.1), calls=%async_computation | async-start | bytes 131072 | tf_op jit(solution)/shard_map/all_to_all | solution.py:544
  41.7 8.8 %copy-start.1 = (f32[512,128]{1,0:T(8,128)S(1)}, f32[512,128]{1,0:T(8,128)}, u32[]{:S(2)}) copy-start(f32[512,128]{1,0:T(8,128)} %hidden.1) | copy-start | bytes 786436
  41.7 8.8 %copy-start.2 = (bf16[4,512,256]{2,1,0:T(8,128)(2,1)S(1)}, bf16[4,512,256]{2,1,0:T(8,128)(2,1)}, u32[]{:S(2)}) copy-start(bf16[4,512,256]{2,1,0:T(8,128)(2,1)} %weight.3) | copy-start | bytes 3145732
  41.8 8.8 %copy-start.3 = (f32[512,128]{1,0:T(8,128)S(1)}, f32[512,128]{1,0:T(8,128)}, u32[]{:S(2)}) copy-start(f32[512,128]{1,0:T(8,128)} %cell.1) | copy-start | bytes 786436
  41.8 8.8 %copy-start.4 = (bf16[19,512]{1,0:T(8,128)(2,1)S(1)}, bf16[19,512]{1,0:T(8,128)(2,1)}, u32[]{:S(2)}) copy-start(bf16[19,512]{1,0:T(8,128)(2,1)} %heads.1) | copy-start | bytes 58372
  41.8 8.8 %copy-start.5 = (f32[4,512]{1,0:T(4,128)S(1)}, f32[4,512]{1,0:T(4,128)}, u32[]{:S(2)}) copy-start(f32[4,512]{1,0:T(4,128)} %bias.1) | copy-start | bytes 24580
  41.8 8.8 %copy-start.6 = (s32[4,8]{1,0:T(4,128)S(1)}, s32[4,8]{1,0:T(4,128)}, u32[]{:S(2)}) copy-start(s32[4,8]{1,0:T(4,128)} %counts.3) | copy-start | bytes 388
  41.8 8.8 %copy-start.7 = (s32[1,64]{1,0:T(1,128)S(1)}, s32[1,64]{1,0:T(1,128)}, u32[]{:S(2)}) copy-start(s32[1,64]{1,0:T(1,128)} %slots.1) | copy-start | bytes 772
  41.8 8.8 %copy-start.8 = (s32[1,128]{1,0:T(1,128)S(1)}, s32[1,128]{1,0:T(1,128)}, u32[]{:S(2)}) copy-start(s32[1,128]{1,0:T(1,128)} %resets.1) | copy-start | bytes 1540
  50.6 1.2 %copy-start = (f32[2048,128]{1,0:T(8,128)S(1)}, f32[2048,128]{1,0:T(8,128)}, u32[]{:S(2)}) copy-start(f32[2048,128]{1,0:T(8,128)} %recurrent.1.sums) | copy-start | bytes 3145732

commit v4 on v3

--- a/solution.py
+++ b/solution.py
@@ -12,7 +12,7 @@
 LANES = 128
 VMEM_MOST = 67_043_328
 PACK = 16
-Y1, Y2, P3, Y4 = 12, 6, 2, 4
+Y1, Y2 = 12, 3
 NN = (((1,), (0,)), ((), ()))
 NT = (((1,), (1,)), ((), ()))
 TN = (((0,), (0,)), ((), ()))
@@ -47,68 +47,62 @@
         self.w3 = -(-self.w2 // 2)
         self.n1 = LANES // self.w1
         self.n2 = 2 * self.n1
+        self.n3 = 2 * self.n2
         assert self.f % 4 == 0 and self.w2 % 2 == 1 and self.n2 * self.w2 <= LANES
-        assert self.f % Y1 == 0 and Y1 % 2 == 0 and self.w1 % Y2 == 0 and Y2 % 2 == 0
+        assert self.f % Y1 == 0 and self.w1 % Y2 == 0 and self.w2 % Y2 == 0
         self.pad1 = PACK // self.c0
         self.win1 = Y1 + 2 * self.pad1
-        self.win2 = Y2 + 3
-        self.win3 = 2 * P3 + 3
-        self.win4 = Y4 + 2
+        self.win2 = Y2 + 2
         self.subs = -(-self.cap // self.n1)
         self.groups = -(-self.cap // self.n2)
-        self.blocks3 = -(-self.w3 // P3)
-        self.blocks4 = -(-self.w3 // Y4)
+        self.pairs = -(-self.cap // self.n3)
+        self.blocks4 = -(-self.w3 // Y2)
         self.wide = -(-self.w3 * self.cap // LANES) * LANES
         assert self.wide - self.w3 * self.cap >= self.cap
 
     def tables(self):
+        none = -(1 << 20)
         rows = []
         four = np.arange(4 * LANES)
         quarter, lane = four // LANES, four % LANES
 
-        def source(width, half, where, count):
-            image, j = lane // half, lane % half
-            x = 2 * j + quarter - 1
-            live = (image < count) & (x >= 0) & (x < width)
-            return np.where(live, where(image) + x, -1)
-
-        for i in range(self.n1):
-            own = source(self.f, self.w1, lambda image: 0 * image, self.n1)
-            rows.append(np.where(lane // self.w1 == i, own, -1))
-        rows.append(
-            source(
-                self.w1,
-                self.w2,
-                lambda image: image // self.n1 * LANES + image % self.n1 * self.w1,
-                self.n2,
-            )
-        )
-        rows.append(source(self.w2, self.w3, lambda image: image * self.w2, self.n2))
+        def source(x, width, live, where):
+            return np.where(live & (x >= 0) & (x < width), where, none)
+
+        j, i = lane // self.n1, lane % self.n1
+        x = 2 * j + quarter - 1
+        rows.append(source(x, self.f, j < self.w1, i * self.f + x))
+        j, i = lane // self.n2, lane % self.n2
+        x = 2 * j + quarter - 1
+        rows.append(source(x, self.w1, j < self.w2, i // self.n1 * LANES + x * self.n1 + i % self.n1))
+        six = np.arange(6 * LANES)
+        dx, half, lane = six // (2 * LANES), six // LANES % 2, six % LANES
+        evens = self.n2 * self.w3
+        odd = lane >= evens
+        j, i = np.where(odd, lane - evens, lane) // self.n2, lane % self.n2
+        x = 2 * j + odd + dx - 1
+        rows.append(source(x, self.w2, lane < self.n2 * self.w2, half * LANES + x * self.n2 + i))
         final = np.arange(self.wide)
         x, image = final // self.cap, final % self.cap
-        rows.append(np.where(x < self.w3, image * self.w3 + x, -(1 << 20)))
-        k1, k2 = np.arange(3 * self.win1 * self.c0), np.arange(3 * self.win2 * self.c1)
-        k3, k4 = np.arange(self.win3 * self.c2), np.arange(self.win4 * self.c2)
-        for k, window, c in ((k1, self.win1, self.c0), (k2, self.win2, self.c1)):
+        for pair in range(self.pairs):
+            i = image - pair * self.n3
+            live = (i >= 0) & (i < self.n3)
+            rows.append(source(x, self.w3, live, i // self.n2 * LANES + x * self.n2 + i % self.n2))
+        for window, c in ((self.win1, self.c0), (self.win2, self.c1), (self.win2, self.c2)):
+            k = np.arange(3 * window * c)
             rows += [k // (window * c), k % (window * c) // c, k % c]
-        for k, c in ((k3, self.c2), (k4, self.c2)):
-            rows += [k // c, k % c]
-        n = self.c2 * self.w3
-        k = np.arange(n)
+        k = np.arange(self.c2 * self.w3)
         rows.append(k % self.w3 * self.c2 + k // self.w3)
         k = np.arange(PACK * self.w3)
         rows += [k % self.w3, k // self.w3]
         width = max(len(r) for r in rows)
-        table = np.full((-(-len(rows) // 8) * 8, width), -(1 << 20), np.int32)
+        table = np.full((-(-len(rows) // 8) * 8, width), none, np.int32)
         for i, r in enumerate(rows):
             table[i, : len(r)] = r
         return table, [len(r) for r in rows]
 
 
-def encoder_kernel(
-    z, lengths, dp, tensor, dp_index, tensor_index,
-    *refs,
-):
+def encoder_kernel(z, lengths, dp, tensor, dp_index, tensor_index, *refs):
     far, out, near = refs[:9], refs[9], refs[10:19]
     p1, p2, p3, t1, t2, t3, t4, t5, g1, s1, g2, s2, g3, s3, total, x4, x5, projx, sems = refs[19:]
     counts, table, w1, w2, w3, r1, r2, frames, proj = near
@@ -122,163 +116,146 @@
     def pick(rows, i):
         return one_hot(iota((rows, lengths[i]), 0) == row(i))
 
-    def zero_padding():
-        for ref, top, rows in ((g1, PACK, z.f * z.c0), (g2, z.c1, z.w1 * z.c1), (g3, 2 * z.c2, z.w2 * z.c2)):
-            for q in range(4):
-                ref[q, :top] = jnp.zeros((top, LANES), BF16)
-                low = ref.shape[1] - top - rows
-                ref[q, top + rows :] = jnp.zeros((low, LANES), BF16)
-        for ref in (x4, x5):
-            for q in range(3):
-                ref[q, : z.c2] = jnp.zeros((z.c2, z.wide), BF16)
-                low = ref.shape[1] - z.c2 - z.w3 * z.c2
-                ref[q, z.c2 + z.w3 * z.c2 :] = jnp.zeros((low, z.wide), BF16)
-        total[...] = jnp.zeros(total.shape, F32)
-
-    zero_padding()
+    for ref, top, rows in ((g1, PACK, z.f * z.c0), (g2, z.c1, z.w1 * z.c1), (g3, z.c2, z.w2 * z.c2)):
+        for q in range(ref.shape[0]):
+            ref[q, :top] = jnp.zeros((top, ref.shape[2]), BF16)
+            low = ref.shape[1] - top - rows
+            ref[q, top + rows :] = jnp.zeros((low, ref.shape[2]), BF16)
+    for ref in (x4, x5):
+        for q in range(3):
+            ref[q, : z.c2] = jnp.zeros((z.c2, z.wide), BF16)
+            low = ref.shape[1] - z.c2 - z.w3 * z.c2
+            ref[q, z.c2 + z.w3 * z.c2 :] = jnp.zeros((low, z.wide), BF16)
+    total[...] = jnp.zeros(total.shape, F32)
     for copy in copies[:7]:
         copy.wait()
-
-    for i in range(z.n1):
-        p1[i] = pick(z.f, i)
-    p2[...] = pick(2 * LANES, z.n1)
-    p3[...] = pick(LANES, z.n1 + 1)
-    base = z.n1 + 3
-
-    def banded(m, cout, band, kx):
-        a = one_hot((iota((m, cout), 0) & (cout - 1)) == iota((m, cout), 1))
-        gap = band - (iota((m, kx), 0) >> log2(cout))
-        return a, gap
-
-    def band_all(weights, m, cin, cout, index, first):
-        kx = lengths[index]
-        a, gap = banded(m, cout, row(index + 1), kx)
-        acc = jnp.zeros((m, kx), F32)
-        for dy in range(3):
-            part = jnp.zeros((m, kx), F32)
-            for dx in range(3):
-                mixed = mm(a, weights[dy, dx], NT).astype(BF16)
-                spread = one_hot(
-                    (iota((cin, kx), 0) == row(index + 2)) & (row(index) == dx)
-                )
-                part = part + mm(mixed, spread)
-            acc = jnp.where(gap == first + dy, part, acc)
-        return acc.astype(BF16)
-
-    def band_each(weights, m, cin, cout, index, target):
-        kx = lengths[index]
-        a, gap = banded(m, cout, row(index), kx)
-        spread = one_hot(iota((cin, kx), 0) == row(index + 1))
-        for dx in range(3):
-            acc = jnp.zeros((m, kx), F32)
-            for dy in range(3):
-                mixed = mm(a, weights[dy, dx]).astype(BF16)
-                acc = jnp.where(gap == dy, mm(mixed, spread), acc)
-            target[dx] = acc.astype(BF16)
-
-    t1[...] = band_all(w1, (Y1 + 1) * z.c1, z.c0, z.c1, base, z.pad1 - 1)
-    t2[...] = band_all(w2, (Y2 + 1) * z.c2, z.c1, z.c2, base + 3, 0)
-    band_each(w3, (2 * P3 + 1) * z.c2, z.c2, z.c2, base + 6, t3)
-    band_each(r1, Y4 * z.c2, z.c2, z.c2, base + 8, t4)
-    band_each(r2, Y4 * z.c2, z.c2, z.c2, base + 8, t5)
-
     own = counts[tensor_index(), dp_index()]
     subs = lax.div(own + (z.n1 - 1), z.n1)
     groups = lax.div(own + (z.n2 - 1), z.n2)
+    pairs = lax.div(own + (z.n3 - 1), z.n3)
     s1[subs] = jnp.zeros(s1.shape[1:], BF16)
+    s2[groups] = jnp.zeros(s2.shape[1:], BF16)
+
+    p1[...] = pick(z.n1 * z.f, 0)
+    p2[...] = pick(2 * LANES, 1)
+    p3[...] = pick(2 * LANES, 2)
+    base = 3 + z.pairs
+
+    def banded(weights, target, rows, cin, cout, index, first, dims):
+        which, line, channel = row(index), row(index + 1), row(index + 2)
+        k = lengths[index]
+        spread = [one_hot((iota((cin, k), 0) == channel) & (which == dx)) for dx in range(3)]
+        lines = []
+        for dy in range(3):
+            acc = None
+            for dx in range(3):
+                part = mm(weights[dy, dx], spread[dx], dims)
+                acc = part if acc is None else acc + part
+            lines.append(acc)
+        for y in range(rows):
+            value = jnp.zeros((cout, k), F32)
+            for dy in range(3):
+                value = jnp.where(line == y + first + dy, lines[dy], value)
+            target[y * cout : (y + 1) * cout, :] = value.astype(BF16)
+
+    banded(w1, t1, Y1, z.c0, z.c1, base, z.pad1 - 1, TN)
+    banded(w2, t2, Y2, z.c1, z.c2, base + 3, 0, TN)
+    for weights, target in ((w3, t3), (r1, t4), (r2, t5)):
+        banded(weights, target, Y2, z.c2, z.c2, base + 6, 0, NN)
 
     def sides(ref, dx, low, rows):
         return jnp.concatenate(
             [ref[dx, low : low + rows, :], ref[dx + 1, low : low + rows, :]], axis=1
         )
 
-    def lane_is(rows, half, count, j):
-        lane = iota((rows, LANES), 1)
-        mask = lane == j
-        for i in range(1, count):
-            mask = mask | (lane == i * half + j)
-        return mask
-
-    def pool_low(acc, half, count):
+    def pool_low(acc, n, half):
         even, odd = acc[:, :LANES], acc[:, LANES:]
-        nxt = pltpu.roll(even, LANES - 1, 1)
-        nxt = jnp.where(lane_is(even.shape[0], half, count, half - 1), even, nxt)
+        nxt = pltpu.roll(even, LANES - n, 1)
+        nxt = jnp.where(iota(even.shape, 1) < (half - 1) * n, nxt, even)
         return jnp.maximum(jnp.maximum(even, odd), nxt)
 
-    def pool_rows(m, c, pairs, last):
-        done = []
-        for i in range(pairs):
-            top = jnp.maximum(m[2 * i * c : (2 * i + 1) * c], m[(2 * i + 1) * c : (2 * i + 2) * c])
-            if not (last and i == pairs - 1):
-                top = jnp.maximum(top, m[(2 * i + 2) * c : (2 * i + 3) * c])
-            done.append(top)
-        return jnp.concatenate(done, axis=0)
+    def pool_rows(blocks, c, height, before, write):
+        held, done = [], 0
+        for m in blocks:
+            held += [m[y * c : (y + 1) * c] for y in range(m.shape[0] // c)]
+            while done < -(-height // 2):
+                reach = [y for y in range(2 * done - before, 2 * done - before + 3) if 0 <= y < height]
+                if reach[-1] >= len(held):
+                    break
+                top = held[reach[0]]
+                for y in reach[1:]:
+                    top = jnp.maximum(top, held[y])
+                write(done, top)
+                done += 1
 
     def conv_one(s, _):
-        mixed = None
-        for i in range(z.n1):
-            image = frames[jnp.minimum(s * z.n1 + i, z.cap - 1)]
-            part = mm(image, p1[i])
-            mixed = part if mixed is None else mixed + part
-        mixed = mixed.astype(BF16)
+        images = [frames[jnp.minimum(s * z.n1 + i, z.cap - 1)] for i in range(z.n1)]
+        mixed = mm(jnp.concatenate(images, axis=1), p1[...]).astype(BF16)
         for q in range(4):
             g1[q, PACK : PACK + z.f * z.c0, :] = mixed[:, q * LANES : (q + 1) * LANES]
-        for b in range(z.f // Y1):
-            low = b * Y1 * z.c0
-            around = jnp.concatenate([sides(g1, dx, low, z.win1 * z.c0) for dx in range(3)], axis=0)
-            m = pool_low(mm(t1[...], around), z.w1, z.n1)
-            rows = pool_rows(m, z.c1, Y1 // 2, b == z.f // Y1 - 1)
-            size = Y1 // 2 * z.c1
-            s1[s, b * size : (b + 1) * size, :] = jnp.maximum(rows, 0.0).astype(BF16)
+
+        def blocks():
+            for b in range(z.f // Y1):
+                low = b * Y1 * z.c0
+                around = jnp.concatenate([sides(g1, dx, low, z.win1 * z.c0) for dx in range(3)], axis=0)
+                yield pool_low(mm(t1[...], around), z.n1, z.w1)
+
+        def write(y, top):
+            s1[s, y * z.c1 : (y + 1) * z.c1, :] = jnp.maximum(top, 0.0).astype(BF16)
+
+        pool_rows(blocks(), z.c1, z.f, 0, write)
         return 0
 
-    copies[7].wait()
-    lax.fori_loop(0, subs, conv_one, 0)
-
-    def conv_rest(g, _):
+    def conv_two(g, _):
         both = jnp.concatenate([s1[2 * g], s1[2 * g + 1]], axis=1)
         mixed = mm(both, p2[...]).astype(BF16)
         for q in range(4):
             g2[q, z.c1 : z.c1 + z.w1 * z.c1, :] = mixed[:, q * LANES : (q + 1) * LANES]
-        for b in range(z.w1 // Y2):
-            low = b * Y2 * z.c1
-            around = jnp.concatenate([sides(g2, dx, low, z.win2 * z.c1) for dx in range(3)], axis=0)
-            m = pool_low(mm(t2[...], around), z.w2, z.n2)
-            rows = pool_rows(m, z.c2, Y2 // 2, b == z.w1 // Y2 - 1)
-            size = Y2 // 2 * z.c2
-            s2[b * size : (b + 1) * size, :] = jnp.maximum(rows, 0.0).astype(BF16)
-        mixed = mm(s2[...], p3[...]).astype(BF16)
-        for q in range(4):
-            g3[q, 2 * z.c2 : 2 * z.c2 + z.w2 * z.c2, :] = mixed[:, q * LANES : (q + 1) * LANES]
-        c = z.c2
-        for b in range(z.blocks3):
-            low = b * 2 * P3 * c
-            acc = None
-            for dx in range(3):
-                part = mm(t3[dx], sides(g3, dx, low, z.win3 * c))
-                acc = part if acc is None else acc + part
-            even, odd = acc[:, :LANES], acc[:, LANES:]
-            n = even.shape[0]
-            before = jnp.where(lane_is(n, z.w3, z.n2, 0), even, pltpu.roll(odd, 1, 1))
-            odd = jnp.where(lane_is(n, z.w3, z.n2, z.w3 - 1), even, odd)
-            m = jnp.maximum(jnp.maximum(even, odd), before)
-            for i in range(P3):
-                pooled = b * P3 + i
-                if pooled >= z.w3:
-                    continue
-                rows = [2 * i + d for d in range(3) if 0 <= 2 * pooled - 1 + d < z.w2]
-                top = None
-                for r in rows:
-                    piece = m[r * c : (r + 1) * c]
-                    top = piece if top is None else jnp.maximum(top, piece)
-                s3[pooled * c : (pooled + 1) * c, :] = top.astype(BF16)
-        shape = (LANES, z.wide)
-        line = iota(shape, 0)
-        place = one_hot((line == row(z.n1 + 2) - g * (z.n2 * z.w3)) & (line < z.n2 * z.w3))
-        total[...] += mm(s3[...], place)
+
+        def blocks():
+            for b in range(z.w1 // Y2):
+                low = b * Y2 * z.c1
+                around = jnp.concatenate([sides(g2, dx, low, z.win2 * z.c1) for dx in range(3)], axis=0)
+                yield pool_low(mm(t2[...], around), z.n2, z.w2)
+
+        def write(y, top):
+            s2[g, y * z.c2 : (y + 1) * z.c2, :] = jnp.maximum(top, 0.0).astype(BF16)
+
+        pool_rows(blocks(), z.c2, z.w1, 0, write)
         return 0
 
-    lax.fori_loop(0, groups, conv_rest, 0)
+    def conv_three(p, _):
+        both = jnp.concatenate([s2[2 * p], s2[2 * p + 1]], axis=1)
+        mixed = mm(both, p3[...]).astype(BF16)
+        for dx in range(3):
+            g3[dx, z.c2 : z.c2 + z.w2 * z.c2, :] = mixed[:, dx * 2 * LANES : (dx + 1) * 2 * LANES]
+        evens = z.n2 * z.w3
+
+        def pool(acc):
+            lane = iota(acc.shape, 1)
+            same = jnp.where(lane < evens - z.n2, pltpu.roll(acc, LANES - evens, 1), acc)
+            before = jnp.where(lane >= z.n2, pltpu.roll(acc, LANES - evens + z.n2, 1), acc)
+            return jnp.maximum(jnp.maximum(acc, same), before)
+
+        def blocks():
+            for b in range(z.w2 // Y2):
+                low = b * Y2 * z.c2
+                around = jnp.concatenate([g3[dx, low : low + z.win2 * z.c2, :] for dx in range(3)], axis=0)
+                acc = mm(t3[...], around)
+                yield jnp.concatenate([pool(acc[:, :LANES]), pool(acc[:, LANES:])], axis=1)
+
+        def write(y, top):
+            s3[y * z.c2 : (y + 1) * z.c2, :] = top.astype(BF16)
+
+        pool_rows(blocks(), z.c2, z.w2, 1, write)
+        source = table[pl.ds(3 + p, 1), :][:, : z.wide]
+        total[...] += mm(s3[...], one_hot(iota((2 * LANES, z.wide), 0) == source))
+        return 0
+
+    copies[7].wait()
+    lax.fori_loop(0, subs, conv_one, 0)
+    lax.fori_loop(0, groups, conv_two, 0)
+    lax.fori_loop(0, pairs, conv_three, 0)
 
     c, n = z.c2, z.w3 * z.c2
     live = iota((n, z.wide), 1) < z.w3 * z.cap
@@ -291,12 +268,9 @@
     def residual(ref, kernel, add):
         pieces = []
         for b in range(z.blocks4):
-            low = b * Y4 * c
-            acc = None
-            for dx in range(3):
-                part = mm(kernel[dx], ref[dx, low : low + z.win4 * c, :])
-                acc = part if acc is None else acc + part
-            pieces.append(acc[: min(Y4, z.w3 - b * Y4) * c])
+            low = b * Y2 * c
+            around = jnp.concatenate([ref[dx, low : low + z.win2 * c, :] for dx in range(3)], axis=0)
+            pieces.append(mm(kernel[...], around)[: min(Y2, z.w3 - b * Y2) * c])
         value = jnp.concatenate(pieces, axis=0)
         if add is not None:
             value = value + add
@@ -356,26 +330,28 @@
         images,
         jnp.transpose(projection),
     )
+    tall = pltpu.VMEM((3, (Y2 * z.blocks4 + 2) * z.c2, z.wide), BF16)
+    band = pltpu.VMEM((Y2 * z.c2, 3 * z.win2 * z.c2), BF16)
     scratch = [pltpu.SMEM(counts.shape, I32)]
     scratch += [pltpu.VMEM(x.shape, x.dtype) for x in operands[1:]]
     scratch += [
-        pltpu.VMEM((z.n1, z.f, 4 * LANES), BF16),
+        pltpu.VMEM((z.n1 * z.f, 4 * LANES), BF16),
         pltpu.VMEM((2 * LANES, 4 * LANES), BF16),
-        pltpu.VMEM((LANES, 4 * LANES), BF16),
-        pltpu.VMEM(((Y1 + 1) * z.c1, 3 * z.win1 * z.c0), BF16),
-        pltpu.VMEM(((Y2 + 1) * z.c2, 3 * z.win2 * z.c1), BF16),
-        pltpu.VMEM((3, (2 * P3 + 1) * z.c2, z.win3 * z.c2), BF16),
-        pltpu.VMEM((3, Y4 * z.c2, z.win4 * z.c2), BF16),
-        pltpu.VMEM((3, Y4 * z.c2, z.win4 * z.c2), BF16),
+        pltpu.VMEM((2 * LANES, 6 * LANES), BF16),
+        pltpu.VMEM((Y1 * z.c1, 3 * z.win1 * z.c0), BF16),
+        pltpu.VMEM((Y2 * z.c2, 3 * z.win2 * z.c1), BF16),
+        band,
+        band,
+        band,
         pltpu.VMEM((4, z.f * z.c0 + 2 * PACK, LANES), BF16),
         pltpu.VMEM((2 * z.groups + 1, z.w1 * z.c1, LANES), BF16),
-        pltpu.VMEM((4, (z.w1 - Y2 + z.win2) * z.c1, LANES), BF16),
-        pltpu.VMEM((z.w2 * z.c2, LANES), BF16),
-        pltpu.VMEM((4, ((z.blocks3 - 1) * 2 * P3 + z.win3) * z.c2, LANES), BF16),
-        pltpu.VMEM((n, LANES), BF16),
+        pltpu.VMEM((4, (z.w1 + 2) * z.c1, LANES), BF16),
+        pltpu.VMEM((2 * z.pairs + 1, z.w2 * z.c2, LANES), BF16),
+        pltpu.VMEM((3, (z.w2 + 2) * z.c2, 2 * LANES), BF16),
+        pltpu.VMEM((n, 2 * LANES), BF16),
         pltpu.VMEM((n, z.wide), F32),
-        pltpu.VMEM((3, ((z.blocks4 - 1) * Y4 + z.win4) * z.c2, z.wide), BF16),
-        pltpu.VMEM((3, ((z.blocks4 - 1) * Y4 + z.win4) * z.c2, z.wide), BF16),
+        tall,
+        tall,
         pltpu.VMEM((z.w3, n, z.feat), BF16),
         pltpu.SemaphoreType.DMA((len(operands),)),
     ]
@@ -383,11 +359,10 @@
         encoder_kernel, z, lengths, dp, tensor,
         lambda: lax.axis_index("dp"), lambda: lax.axis_index("tensor"),
     )
-    depth = z.cap // dp
     return pl.pallas_call(
         body,
         name="encoder",
-        out_shape=jax.ShapeDtypeStruct((dp * tensor, depth, z.feat), BF16),
+        out_shape=jax.ShapeDtypeStruct((dp * tensor, z.cap // dp, z.feat), BF16),
         in_specs=[HBM] * len(operands),
         out_specs=VMEM,
         scratch_shapes=scratch,

time: 69 us -> 60 us (0.87)
  starting transfers between devices: 24.7 us -> 16.2 us
    all_to_all x1, starting transfers between devices: 18.6 us -> 10.1 us  [body(): features = lax.all_to_all(features, ('dp', 'tensor'), 0, 0, tiled=True)]
  transfers between devices with their start and end apart: 4 -> 4, of which waited for: 0 -> 0; matrix products, arithmetic and copies ran while one was open for 0% -> 0% of each run, Pallas kernels for 34% -> 39%
where the time goes in v4:
time: 60 us; the launch traced here: 60.2 us
  Pallas kernels  27.1 us (45%)
  starting transfers between devices  16.2 us (27%)
  blocking collectives  13.2 us (22%)
  other arithmetic  1.62 us (3%)
  local copies, waits for them, and re-layouts  1.27 us (2%)
  between operations  0.82 us (1%)
    pallas_call x1, Pallas kernels, encode_rows(): pl.pallas_call(body, name='encoder', out_shape=jax.ShapeDtypeStruct((dp *...  14.7 us
    all_to_all x1, blocking collectives, body(): received = lax.all_to_all(sent, ('dp', 'tensor'), 0, 0, tiled=True)  13.2 us
    all_to_all x1, starting transfers between devices, body(): features = lax.all_to_all(features, ('dp', 'tensor'), 0, 0, tiled=True)  10.1 us
    pallas_call x1, Pallas kernels, recurrent(): pl.pallas_call(functools.partial(recurrent_kernel, lambda: lax.axis_index...  8.72 us
    ppermute x3, starting transfers between devices, body(): lax.ppermute(own, 'tensor', [(i, (i + back) % tensor) for i in range(tens...  6.09 us
    pallas_call x1, Pallas kernels, core(): pl.pallas_call(functools.partial(core_kernel, lambda: lax.axis_index('dp'...  1.94 us
    pallas_call x1, Pallas kernels, answers(): pl.pallas_call(functools.partial(answers_kernel, counts.shape[0], lambda:...  1.67 us
    convert_element_type x1, other arithmetic, body(): own = hidden_state.astype(BF16)  1.62 us
  transfers between devices with their start and end apart: 4, of which 0 were waited for; matrix products, arithmetic and copies ran while one was open for 0% of the time, Pallas kernels for 39%

profile of v4, /device:TPU:0, one launch (start us, length us, event | category | flops | bytes accessed | tf_op | source)
XLA Modules:
  0.0 60.2 jit_solution(14599930293029447050)
XLA Ops:
  0.6 1.6 %convert_element_type.3.refs_0_ = bf16[512,128]{1,0:T(8,128)(2,1)} convert(f32[512,128]{1,0:T(8,128)} %hidden.1) | non-fusion elementwise | flops 65536 | bytes 393216 | tf_op jit(solution)/shard_map/convert_element_type | solution.py:511
  2.2 5.1 %collective-permute-start.2 = (bf16[512,128]{1,0:T(8,128)(2,1)}, bf16[512,128]{1,0:T(8,128)(2,1)}, u32[]{:S(2)}, u32[]{:S(2)}) collective-permute-start(bf16[512,128]{1,0:T(8,128)(2,1)} %convert_element_type.3.refs_0_), channel_id=1, source_target_pairs={{0,3},{1,0},{2,1},{3,2},{4,7},{5,4},{6,5},{7,6},{8,11},{9,8},{10,9... | collective-permute-start | bytes 393224 | tf_op jit(solution)/shard_map/ppermute | solution.py:513
  7.3 0.0 collective-permute-start.1
  7.3 1.0 %collective-permute-start = (bf16[512,128]{1,0:T(8,128)(2,1)}, bf16[512,128]{1,0:T(8,128)(2,1)}, u32[]{:S(2)}, u32[]{:S(2)}) collective-permute-start(bf16[512,128]{1,0:T(8,128)(2,1)} %convert_element_type.3.refs_0_), channel_id=1, source_target_pairs={{0,1},{1,2},{2,3},{3,0},{4,5},{5,6},{6,7},{7,4},{8,9},{9,10},{10,1... | collective-permute-start | bytes 393224 | tf_op jit(solution)/shard_map/ppermute | solution.py:513
  8.3 14.7 %encoder.1 = bf16[32,4,256]{2,1,0:T(4,128)(2,1)} custom-call(s32[4,8]{1,0:T(4,128)} %counts.3, s32[24,768]{1,0:T(8,128)} %constant.2.clone.refs_1_, bf16[3,3,4,16]{3,2,1,0:T(4,128)(2,1)} %bitcast.19, bf16[3,3,16,32]{3,2,1,0:T(8,128)(2,1)} %bitcast.18, bf16[3,3,32,32]{3,2,1,0:T(8,128)(2,1)} %bitcast.15, bf16[3,3,32,32]{3,2,1,0:T(8,128)(2,1)} %bitcast.16, ...), custom_call_target="tpu_custom_call" | custom-call | flops 20000000000 | bytes 8000000 | tf_op jit(solution)/shard_map/encoder/pallas_call | solution.py:362
  23.1 0.0 collective-permute-done.2.refs_3_
  23.1 0.0 collective-permute-done.1.refs_2_
  23.1 0.0 collective-permute-done.refs_1_
  23.1 10.1 %all-to-all-start = ((bf16[32,4,256]{2,1,0:T(4,128)(2,1)}), bf16[32,4,256]{2,1,0:T(4,128)(2,1)S(1)}, u32[]{:S(2)}, u32[]{:S(2)}) async-start(bf16[32,4,256]{2,1,0:T(4,128)(2,1)} %encoder.1), calls=%async_computation | async-start | bytes 131072 | tf_op jit(solution)/shard_map/all_to_all | solution.py:519
  33.2 0.0 copy-start.1
  33.2 0.0 copy-start.2
  33.2 0.0 copy-start.3
  33.2 0.0 copy-start.4
  33.3 0.0 copy-start.5
  33.3 0.0 copy-start.6
  33.3 0.0 copy-start.7
  33.3 0.0 copy-start.8
  33.3 8.7 %recurrent.1.sums = f32[2048,128]{1,0:T(8,128)} custom-call(bf16[4,512,2048]{2,1,0:T(8,128)(2,1)} %weight.2, bf16[512,128]{1,0:T(8,128)(2,1)} %convert_element_type.3.refs_0_, bf16[512,128]{1,0:T(8,128)(2,1)} %collective-permute-done.refs_1_, bf16[512,128]{1,0:T(8,128)(2,1)} %collective-permute-done.1.refs_2_, bf16[512,128]{1,0:T(8,128)(2,1)} %collective-permute-done.2.refs_3_), custom_call_target="tpu_custom_call" | custom-call | flops 1073741824 | bytes 8388608 | tf_op jit(solution)/shard_map/recurrent/pallas_call | solution.py:395
  42.0 0.0 all-to-all-done.features
  42.0 0.0 copy-done.1
  42.1 0.0 copy-done.2
  42.1 0.0 copy-done.3
  42.1 0.0 copy-done.4
  42.1 0.0 copy-done.5
  42.1 0.0 copy-done.6
  42.1 0.0 copy-done.7
  42.1 0.0 copy-done.8
  42.1 0.0 copy-start
  42.1 1.2 %copy-done = f32[2048,128]{1,0:T(8,128)S(1)} copy-done((f32[2048,128]{1,0:T(8,128)S(1)}, f32[2048,128]{1,0:T(8,128)}, u32[]{:S(2)}) %copy-start) | copy-done | bytes 1048600
  43.4 1.9 %core.1 = (f32[128,19]{1,0:T(8,128)S(1)}, f32[512,128]{1,0:T(8,128)}, f32[512,128]{1,0:T(8,128)}) custom-call(bf16[32,4,256]{2,1,0:T(4,128)(2,1)S(1)} %all-to-all-done.features, f32[2048,128]{1,0:T(8,128)S(1)} %copy-done, f32[4,512]{1,0:T(4,128)S(1)} %copy-done.5, bf16[4,512,256]{2,1,0:T(8,128)(2,1)S(1)} %copy-done.2, f32[512,128]{1,0:T(8,128)S(1)} %copy-done.1, ...), custom_call_target="tpu_custom_call" | custom-call | flops 134217728 | bytes 4000000 | tf_op jit(solution)/shard_map/core/pallas_call | solution.py:458
  45.3 13.2 %all_to_all.16 = f32[32,4,19]{2,1,0:T(4,128)} all-to-all(f32[32,4,19]{2,1,0:T(4,128)S(1)} %bitcast.11), channel_id=1, replica_groups=mesh['dp'=8,'tensor'=4] {'dp','tensor'}, dimensions={0} | all-to-all | bytes 19456 | tf_op jit(solution)/shard_map/all_to_all | solution.py:524
  58.5 1.7 %answers.1 = f32[19,32]{1,0:T(8,128)} custom-call(s32[4,8]{1,0:T(4,128)} %counts.3, f32[128,19]{1,0:T(8,128)} %bitcast.12), custom_call_target="tpu_custom_call" | custom-call | tf_op jit(solution)/shard_map/answers/pallas_call | solution.py:491
Async XLA Ops:
  2.2 20.8 %collective-permute-start.2 = (bf16[512,128]{1,0:T(8,128)(2,1)}, bf16[512,128]{1,0:T(8,128)(2,1)}, u32[]{:S(2)}, u32[]{:S(2)}) collective-permute-start(bf16[512,128]{1,0:T(8,128)(2,1)} %convert_element_type.3.refs_0_), channel_id=1, source_target_pairs={{0,3},{1,0},{2,1},{3,2},{4,7},{5,4},{6,5},{7,6},{8,11},{9,8},{10,9... | collective-permute-start | bytes 393224 | tf_op jit(solution)/shard_map/ppermute | solution.py:513
  7.3 15.8 %collective-permute-start.1 = (bf16[512,128]{1,0:T(8,128)(2,1)}, bf16[512,128]{1,0:T(8,128)(2,1)}, u32[]{:S(2)}, u32[]{:S(2)}) collective-permute-start(bf16[512,128]{1,0:T(8,128)(2,1)} %convert_element_type.3.refs_0_), channel_id=1, source_target_pairs={{0,2},{1,3},{2,0},{3,1},{4,6},{5,7},{6,4},{7,5},{8,10},{9,11},{10,... | collective-permute-start | bytes 393224 | tf_op jit(solution)/shard_map/ppermute | solution.py:513
  7.3 15.8 %collective-permute-start = (bf16[512,128]{1,0:T(8,128)(2,1)}, bf16[512,128]{1,0:T(8,128)(2,1)}, u32[]{:S(2)}, u32[]{:S(2)}) collective-permute-start(bf16[512,128]{1,0:T(8,128)(2,1)} %convert_element_type.3.refs_0_), channel_id=1, source_target_pairs={{0,1},{1,2},{2,3},{3,0},{4,5},{5,6},{6,7},{7,4},{8,9},{9,10},{10,1... | collective-permute-start | bytes 393224 | tf_op jit(solution)/shard_map/ppermute | solution.py:513
  23.1 18.9 %all-to-all-start = ((bf16[32,4,256]{2,1,0:T(4,128)(2,1)}), bf16[32,4,256]{2,1,0:T(4,128)(2,1)S(1)}, u32[]{:S(2)}, u32[]{:S(2)}) async-start(bf16[32,4,256]{2,1,0:T(4,128)(2,1)} %encoder.1), calls=%async_computation | async-start | bytes 131072 | tf_op jit(solution)/shard_map/all_to_all | solution.py:519
  33.2 8.8 %copy-start.1 = (f32[512,128]{1,0:T(8,128)S(1)}, f32[512,128]{1,0:T(8,128)}, u32[]{:S(2)}) copy-start(f32[512,128]{1,0:T(8,128)} %hidden.1) | copy-start | bytes 786436
  33.2 8.8 %copy-start.2 = (bf16[4,512,256]{2,1,0:T(8,128)(2,1)S(1)}, bf16[4,512,256]{2,1,0:T(8,128)(2,1)}, u32[]{:S(2)}) copy-start(bf16[4,512,256]{2,1,0:T(8,128)(2,1)} %weight.3) | copy-start | bytes 3145732
  33.2 8.8 %copy-start.3 = (f32[512,128]{1,0:T(8,128)S(1)}, f32[512,128]{1,0:T(8,128)}, u32[]{:S(2)}) copy-start(f32[512,128]{1,0:T(8,128)} %cell.1) | copy-start | bytes 786436
  33.2 8.8 %copy-start.4 = (bf16[19,512]{1,0:T(8,128)(2,1)S(1)}, bf16[19,512]{1,0:T(8,128)(2,1)}, u32[]{:S(2)}) copy-start(bf16[19,512]{1,0:T(8,128)(2,1)} %heads.1) | copy-start | bytes 58372
  33.3 8.8 %copy-start.5 = (f32[4,512]{1,0:T(4,128)S(1)}, f32[4,512]{1,0:T(4,128)}, u32[]{:S(2)}) copy-start(f32[4,512]{1,0:T(4,128)} %bias.1) | copy-start | bytes 24580
  33.3 8.8 %copy-start.6 = (s32[4,8]{1,0:T(4,128)S(1)}, s32[4,8]{1,0:T(4,128)}, u32[]{:S(2)}) copy-start(s32[4,8]{1,0:T(4,128)} %counts.3) | copy-start | bytes 388
  33.3 8.8 %copy-start.7 = (s32[1,64]{1,0:T(1,128)S(1)}, s32[1,64]{1,0:T(1,128)}, u32[]{:S(2)}) copy-start(s32[1,64]{1,0:T(1,128)} %slots.1) | copy-start | bytes 772
  33.3 8.8 %copy-start.8 = (s32[1,128]{1,0:T(1,128)S(1)}, s32[1,128]{1,0:T(1,128)}, u32[]{:S(2)}) copy-start(s32[1,128]{1,0:T(1,128)} %resets.1) | copy-start | bytes 1540
  42.1 1.2 %copy-start = (f32[2048,128]{1,0:T(8,128)S(1)}, f32[2048,128]{1,0:T(8,128)}, u32[]{:S(2)}) copy-start(f32[2048,128]{1,0:T(8,128)} %recurrent.1.sums) | copy-start | bytes 3145732

commit v5 on v4

--- a/solution.py
+++ b/solution.py
@@ -53,8 +53,6 @@
         self.pad1 = PACK // self.c0
         self.win1 = Y1 + 2 * self.pad1
         self.win2 = Y2 + 2
-        self.subs = -(-self.cap // self.n1)
-        self.groups = -(-self.cap // self.n2)
         self.pairs = -(-self.cap // self.n3)
         self.blocks4 = -(-self.w3 // Y2)
         self.wide = -(-self.w3 * self.cap // LANES) * LANES
@@ -104,7 +102,7 @@
 
 def encoder_kernel(z, lengths, dp, tensor, dp_index, tensor_index, *refs):
     far, out, near = refs[:9], refs[9], refs[10:19]
-    p1, p2, p3, t1, t2, t3, t4, t5, g1, s1, g2, s2, g3, s3, total, x4, x5, projx, sems = refs[19:]
+    p1, p2, p3, t1, t2, t3, t4, t5, g1, s1, g2, s2, g3, s3, x4, x5, projx, sems = refs[19:]
     counts, table, w1, w2, w3, r1, r2, frames, proj = near
     copies = [pltpu.make_async_copy(a, b, sems.at[i]) for i, (a, b) in enumerate(zip(far, near))]
     for copy in copies:
@@ -116,7 +114,9 @@
     def pick(rows, i):
         return one_hot(iota((rows, lengths[i]), 0) == row(i))
 
-    for ref, top, rows in ((g1, PACK, z.f * z.c0), (g2, z.c1, z.w1 * z.c1), (g3, z.c2, z.w2 * z.c2)):
+    maps = [(g1.at[i], PACK, z.f * z.c0) for i in range(4)]
+    maps += [(g2.at[i], z.c1, z.w1 * z.c1) for i in range(2)]
+    for ref, top, rows in maps + [(g3, z.c2, z.w2 * z.c2)]:
         for q in range(ref.shape[0]):
             ref[q, :top] = jnp.zeros((top, ref.shape[2]), BF16)
             low = ref.shape[1] - top - rows
@@ -126,15 +126,11 @@
             ref[q, : z.c2] = jnp.zeros((z.c2, z.wide), BF16)
             low = ref.shape[1] - z.c2 - z.w3 * z.c2
             ref[q, z.c2 + z.w3 * z.c2 :] = jnp.zeros((low, z.wide), BF16)
-    total[...] = jnp.zeros(total.shape, F32)
     for copy in copies[:7]:
         copy.wait()
     own = counts[tensor_index(), dp_index()]
-    subs = lax.div(own + (z.n1 - 1), z.n1)
-    groups = lax.div(own + (z.n2 - 1), z.n2)
     pairs = lax.div(own + (z.n3 - 1), z.n3)
-    s1[subs] = jnp.zeros(s1.shape[1:], BF16)
-    s2[groups] = jnp.zeros(s2.shape[1:], BF16)
+    s3[...] = jnp.zeros(s3.shape, BF16)
 
     p1[...] = pick(z.n1 * z.f, 0)
     p2[...] = pick(2 * LANES, 1)
@@ -188,45 +184,47 @@
                 write(done, top)
                 done += 1
 
-    def conv_one(s, _):
+    def mix_one(s, slot):
         images = [frames[jnp.minimum(s * z.n1 + i, z.cap - 1)] for i in range(z.n1)]
         mixed = mm(jnp.concatenate(images, axis=1), p1[...]).astype(BF16)
         for q in range(4):
-            g1[q, PACK : PACK + z.f * z.c0, :] = mixed[:, q * LANES : (q + 1) * LANES]
-
+            g1[slot, q, PACK : PACK + z.f * z.c0, :] = mixed[:, q * LANES : (q + 1) * LANES]
+
+    def conv_one(slot):
         def blocks():
             for b in range(z.f // Y1):
                 low = b * Y1 * z.c0
-                around = jnp.concatenate([sides(g1, dx, low, z.win1 * z.c0) for dx in range(3)], axis=0)
-                yield pool_low(mm(t1[...], around), z.n1, z.w1)
+                around = jnp.concatenate(
+                    [sides(g1.at[slot], dx, low, z.win1 * z.c0) for dx in range(3)], axis=0
+                )
+                yield pool_low(mm(t1[...], around).astype(BF16), z.n1, z.w1)
 
         def write(y, top):
-            s1[s, y * z.c1 : (y + 1) * z.c1, :] = jnp.maximum(top, 0.0).astype(BF16)
+            lanes = slice(slot % 2 * LANES, (slot % 2 + 1) * LANES)
+            s1[slot // 2, y * z.c1 : (y + 1) * z.c1, lanes] = jnp.maximum(top, 0)
 
         pool_rows(blocks(), z.c1, z.f, 0, write)
-        return 0
-
-    def conv_two(g, _):
-        both = jnp.concatenate([s1[2 * g], s1[2 * g + 1]], axis=1)
-        mixed = mm(both, p2[...]).astype(BF16)
+
+    def conv_two(half):
+        mixed = mm(s1[half], p2[...]).astype(BF16)
         for q in range(4):
-            g2[q, z.c1 : z.c1 + z.w1 * z.c1, :] = mixed[:, q * LANES : (q + 1) * LANES]
+            g2[half, q, z.c1 : z.c1 + z.w1 * z.c1, :] = mixed[:, q * LANES : (q + 1) * LANES]
 
         def blocks():
             for b in range(z.w1 // Y2):
                 low = b * Y2 * z.c1
-                around = jnp.concatenate([sides(g2, dx, low, z.win2 * z.c1) for dx in range(3)], axis=0)
-                yield pool_low(mm(t2[...], around), z.n2, z.w2)
+                around = jnp.concatenate(
+                    [sides(g2.at[half], dx, low, z.win2 * z.c1) for dx in range(3)], axis=0
+                )
+                yield pool_low(mm(t2[...], around).astype(BF16), z.n2, z.w2)
 
         def write(y, top):
-            s2[g, y * z.c2 : (y + 1) * z.c2, :] = jnp.maximum(top, 0.0).astype(BF16)
+            s2[y * z.c2 : (y + 1) * z.c2, half * LANES : (half + 1) * LANES] = jnp.maximum(top, 0)
 
         pool_rows(blocks(), z.c2, z.w1, 0, write)
-        return 0
-
-    def conv_three(p, _):
-        both = jnp.concatenate([s2[2 * p], s2[2 * p + 1]], axis=1)
-        mixed = mm(both, p3[...]).astype(BF16)
+
+    def conv_three(p):
+        mixed = mm(s2[...], p3[...]).astype(BF16)
         for dx in range(3):
             g3[dx, z.c2 : z.c2 + z.w2 * z.c2, :] = mixed[:, dx * 2 * LANES : (dx + 1) * 2 * LANES]
         evens = z.n2 * z.w3
@@ -241,21 +239,32 @@
             for b in range(z.w2 // Y2):
                 low = b * Y2 * z.c2
                 around = jnp.concatenate([g3[dx, low : low + z.win2 * z.c2, :] for dx in range(3)], axis=0)
-                acc = mm(t3[...], around)
+                acc = mm(t3[...], around).astype(BF16)
                 yield jnp.concatenate([pool(acc[:, :LANES]), pool(acc[:, LANES:])], axis=1)
 
         def write(y, top):
-            s3[y * z.c2 : (y + 1) * z.c2, :] = top.astype(BF16)
+            s3[p, y * z.c2 : (y + 1) * z.c2, :] = top
 
         pool_rows(blocks(), z.c2, z.w2, 1, write)
-        source = table[pl.ds(3 + p, 1), :][:, : z.wide]
-        total[...] += mm(s3[...], one_hot(iota((2 * LANES, z.wide), 0) == source))
+
+    def convolve(p, _):
+        for half in range(2):
+            for slot in (2 * half, 2 * half + 1):
+                mix_one(4 * p + slot, slot)
+        for half in range(2):
+            for slot in (2 * half, 2 * half + 1):
+                conv_one(slot)
+        for half in range(2):
+            conv_two(half)
+        conv_three(p)
         return 0
 
     copies[7].wait()
-    lax.fori_loop(0, subs, conv_one, 0)
-    lax.fori_loop(0, groups, conv_two, 0)
-    lax.fori_loop(0, pairs, conv_three, 0)
+    lax.fori_loop(0, pairs, convolve, 0)
+    total = None
+    for p in range(z.pairs):
+        part = mm(s3[p], pick(2 * LANES, 3 + p))
+        total = part if total is None else total + part
 
     c, n = z.c2, z.w3 * z.c2
     live = iota((n, z.wide), 1) < z.w3 * z.cap
@@ -276,10 +285,10 @@
             value = value + add
         return jnp.maximum(value, 0.0)
 
-    spread_x(x4, jnp.maximum(total[...], 0.0))
+    spread_x(x4, jnp.maximum(total, 0.0))
     inner = residual(x4, t4, None).astype(BF16).astype(F32)
     spread_x(x5, jnp.where(live, inner, 0.0))
-    encoded = residual(x5, t5, total[...]).astype(BF16)
+    encoded = residual(x5, t5, total).astype(BF16)
 
     last = len(lengths) - 3
     order = one_hot(iota((n, n), 0) == row(last))
@@ -343,13 +352,12 @@
         band,
         band,
         band,
-        pltpu.VMEM((4, z.f * z.c0 + 2 * PACK, LANES), BF16),
-        pltpu.VMEM((2 * z.groups + 1, z.w1 * z.c1, LANES), BF16),
-        pltpu.VMEM((4, (z.w1 + 2) * z.c1, LANES), BF16),
-        pltpu.VMEM((2 * z.pairs + 1, z.w2 * z.c2, LANES), BF16),
+        pltpu.VMEM((4, 4, z.f * z.c0 + 2 * PACK, LANES), BF16),
+        pltpu.VMEM((2, z.w1 * z.c1, 2 * LANES), BF16),
+        pltpu.VMEM((2, 4, (z.w1 + 2) * z.c1, LANES), BF16),
+        pltpu.VMEM((z.w2 * z.c2, 2 * LANES), BF16),
         pltpu.VMEM((3, (z.w2 + 2) * z.c2, 2 * LANES), BF16),
-        pltpu.VMEM((n, 2 * LANES), BF16),
-        pltpu.VMEM((n, z.wide), F32),
+        pltpu.VMEM((z.pairs, n, 2 * LANES), BF16),
         tall,
         tall,
         pltpu.VMEM((z.w3, n, z.feat), BF16),
@@ -372,21 +380,14 @@
 
 
 def recurrent_kernel(index, weight, *refs):
-    *pieces, out, held, sems = refs
+    *pieces, out, hidden = refs
     gates, share, _ = weight.shape
     width = pieces[0].shape[0]
-    copies = [pltpu.make_async_copy(weight.at[q], held.at[q], sems.at[q]) for q in range(gates)]
-    for copy in copies:
-        copy.start()
-    tensor = len(pieces)
+    for back, piece in enumerate(pieces):
+        low = pl.multiple_of(((index() - back) & (len(pieces) - 1)) * width, width)
+        hidden[pl.ds(low, width), :] = piece[...]
     for q in range(gates):
-        copies[q].wait()
-        acc = None
-        for back, piece in enumerate(pieces):
-            low = pl.multiple_of(((index() - back) & (tensor - 1)) * width, width)
-            part = mm(held[q, :, pl.ds(low, width)], piece[...])
-            acc = part if acc is None else acc + part
-        out[q * share : (q + 1) * share, :] = acc
+        out[q * share : (q + 1) * share, :] = mm(weight[q], hidden[...])
 
 
 def recurrent(weight, pieces):
@@ -396,13 +397,10 @@
         functools.partial(recurrent_kernel, lambda: lax.axis_index("tensor")),
         name="recurrent",
         out_shape=jax.ShapeDtypeStruct((gates * share, slots), F32),
-        in_specs=[HBM] + [VMEM] * len(pieces),
+        in_specs=[VMEM] * (1 + len(pieces)),
         out_specs=VMEM,
-        scratch_shapes=[
-            pltpu.VMEM(weight.shape, BF16),
-            pltpu.SemaphoreType.DMA((gates,)),
-        ],
-        compiler_params=pltpu.CompilerParams(vmem_limit_bytes=57 << 20),
+        scratch_shapes=[pltpu.VMEM((hidden, slots), BF16)],
+        compiler_params=pltpu.CompilerParams(vmem_limit_bytes=24 << 20),
         cost_estimate=pl.CostEstimate(
             flops=2 * gates * share * hidden * slots, bytes_accessed=2 * gates * share * hidden, transcendentals=0
         ),
@@ -499,6 +497,7 @@
         out_shape=jax.ShapeDtypeStruct((received.shape[1], cap), F32),
         in_specs=[SMEM, VMEM],
         out_specs=VMEM,
+        compiler_params=pltpu.CompilerParams(vmem_limit_bytes=8 << 20),
     )(counts, received)
 
 

time: 60 us -> 51.7 us (0.86)
  Pallas kernels: 27.1 us -> 18.8 us
  local copies, waits for them, and re-layouts: 1.27 us -> 3.42 us
  starting transfers between devices: 16.2 us -> 14.2 us
    pallas_call x1, Pallas kernels: 8.72 us -> 3.56 us  [recurrent(): pl.pallas_call(functools.partial(recurrent_kernel, lambda: lax.axis_index...]
    pallas_call x1, Pallas kernels: 14.7 us -> 11.9 us  [encode_rows(): pl.pallas_call(body, name='encoder', out_shape=jax.ShapeDtypeStruct((dp *...]
    unnamed x18, local copies, waits for them, and re-layouts: 1.27 us -> 3.42 us
    all_to_all x1, starting transfers between devices: 10.1 us -> 8.1 us  [body(): features = lax.all_to_all(features, ('dp', 'tensor'), 0, 0, tiled=True)]
  transfers between devices with their start and end apart: 4 -> 4, of which waited for: 0 -> 1; matrix products, arithmetic and copies ran while one was open for 0% -> 0% of each run, Pallas kernels for 39% -> 30%
where the time goes in v5:
time: 51.7 us; the launch traced here: 51.9 us
  Pallas kernels  18.8 us (36%)
  starting transfers between devices  14.2 us (27%)
  blocking collectives  12.7 us (25%)
  local copies, waits for them, and re-layouts  3.42 us (7%)
  other arithmetic  1.62 us (3%)
  between operations  0.77 us (1%)
    all_to_all x1, blocking collectives, body(): received = lax.all_to_all(sent, ('dp', 'tensor'), 0, 0, tiled=True)  12.7 us
    pallas_call x1, Pallas kernels, encode_rows(): pl.pallas_call(body, name='encoder', out_shape=jax.ShapeDtypeStruct((dp *...  11.9 us
    all_to_all x1, starting transfers between devices, body(): features = lax.all_to_all(features, ('dp', 'tensor'), 0, 0, tiled=True)  8.1 us
    ppermute x3, starting transfers between devices, body(): lax.ppermute(own, 'tensor', [(i, (i + back) % tensor) for i in range(tens...  6.09 us
    pallas_call x1, Pallas kernels, recurrent(): pl.pallas_call(functools.partial(recurrent_kernel, lambda: lax.axis_index...  3.56 us
    unnamed x18, local copies, waits for them, and re-layouts  3.42 us
    pallas_call x1, Pallas kernels, core(): pl.pallas_call(functools.partial(core_kernel, lambda: lax.axis_index('dp'...  1.98 us
    convert_element_type x1, other arithmetic, body(): own = hidden_state.astype(BF16)  1.62 us
  transfers between devices with their start and end apart: 4, of which 1 were waited for; matrix products, arithmetic and copies ran while one was open for 0% of the time, Pallas kernels for 30%

profile of v5, /device:TPU:0, one launch (start us, length us, event | category | flops | bytes accessed | tf_op | source)
XLA Modules:
  0.0 51.9 jit_solution(16240541203574144874)
XLA Ops:
  0.6 1.6 %convert_element_type.3.refs_0_ = bf16[512,128]{1,0:T(8,128)(2,1)} convert(f32[512,128]{1,0:T(8,128)} %hidden.1) | non-fusion elementwise | flops 65536 | bytes 393216 | tf_op jit(solution)/shard_map/convert_element_type | solution.py:510
  2.2 5.1 %collective-permute-start.2 = (bf16[512,128]{1,0:T(8,128)(2,1)}, bf16[512,128]{1,0:T(8,128)(2,1)}, u32[]{:S(2)}, u32[]{:S(2)}) collective-permute-start(bf16[512,128]{1,0:T(8,128)(2,1)} %convert_element_type.3.refs_0_), channel_id=1, source_target_pairs={{0,3},{1,0},{2,1},{3,2},{4,7},{5,4},{6,5},{7,6},{8,11},{9,8},{10,9... | collective-permute-start | bytes 393224 | tf_op jit(solution)/shard_map/ppermute | solution.py:512
  7.3 0.0 collective-permute-start.1
  7.3 1.0 %collective-permute-start = (bf16[512,128]{1,0:T(8,128)(2,1)}, bf16[512,128]{1,0:T(8,128)(2,1)}, u32[]{:S(2)}, u32[]{:S(2)}) collective-permute-start(bf16[512,128]{1,0:T(8,128)(2,1)} %convert_element_type.3.refs_0_), channel_id=1, source_target_pairs={{0,1},{1,2},{2,3},{3,0},{4,5},{5,6},{6,7},{7,4},{8,9},{9,10},{10,1... | collective-permute-start | bytes 393224 | tf_op jit(solution)/shard_map/ppermute | solution.py:512
  8.3 11.9 %encoder.1 = bf16[32,4,256]{2,1,0:T(4,128)(2,1)} custom-call(s32[4,8]{1,0:T(4,128)} %counts.3, s32[24,768]{1,0:T(8,128)} %constant.2.clone.refs_1_, bf16[3,3,4,16]{3,2,1,0:T(4,128)(2,1)} %bitcast.19, bf16[3,3,16,32]{3,2,1,0:T(8,128)(2,1)} %bitcast.18, bf16[3,3,32,32]{3,2,1,0:T(8,128)(2,1)} %bitcast.15, bf16[3,3,32,32]{3,2,1,0:T(8,128)(2,1)} %bitcast.16, ...), custom_call_target="tpu_custom_call" | custom-call | flops 20000000000 | bytes 8000000 | tf_op jit(solution)/shard_map/encoder/pallas_call | solution.py:370
  20.2 0.0 collective-permute-done.2.refs_3_
  20.2 0.0 collective-permute-done.1.refs_2_
  20.2 0.0 collective-permute-done.refs_1_
  20.2 8.1 %all-to-all-start = ((bf16[32,4,256]{2,1,0:T(4,128)(2,1)}), bf16[32,4,256]{2,1,0:T(4,128)(2,1)S(1)}, u32[]{:S(2)}, u32[]{:S(2)}) async-start(bf16[32,4,256]{2,1,0:T(4,128)(2,1)} %encoder.1), calls=%async_computation | async-start | bytes 131072 | tf_op jit(solution)/shard_map/all_to_all | solution.py:518
  28.3 0.0 copy-start
  28.4 3.4 %copy-done = bf16[4,512,2048]{2,1,0:T(8,128)(2,1)S(1)} copy-done((bf16[4,512,2048]{2,1,0:T(8,128)(2,1)S(1)}, bf16[4,512,2048]{2,1,0:T(8,128)(2,1)}, u32[]{:S(2)}) %copy-start) | copy-done | bytes 8388632
  31.7 0.0 copy-start.1
  31.7 0.0 copy-start.2
  31.7 0.0 copy-start.3
  31.7 0.0 copy-start.4
  31.7 0.0 copy-start.5
  31.8 0.0 copy-start.6
  31.8 0.0 copy-start.7
  31.8 0.0 copy-start.8
  31.8 3.6 %recurrent.1.sums = f32[2048,128]{1,0:T(8,128)S(1)} custom-call(bf16[4,512,2048]{2,1,0:T(8,128)(2,1)S(1)} %copy-done, bf16[512,128]{1,0:T(8,128)(2,1)} %convert_element_type.3.refs_0_, bf16[512,128]{1,0:T(8,128)(2,1)} %collective-permute-done.refs_1_, bf16[512,128]{1,0:T(8,128)(2,1)} %collective-permute-done.1.refs_2_, ...), custom_call_target="tpu_custom_call" | custom-call | flops 1073741824 | bytes 8388608 | tf_op jit(solution)/shard_map/recurrent/pallas_call | solution.py:396
  35.4 0.5 all-to-all-done.features
  35.8 0.0 copy-done.1
  35.8 0.0 copy-done.2
  35.8 0.0 copy-done.3
  35.9 0.0 copy-done.4
  35.9 0.0 copy-done.5
  35.9 0.0 copy-done.6
  35.9 0.0 copy-done.7
  35.9 0.0 copy-done.8
  35.9 2.0 %core.1 = (f32[128,19]{1,0:T(8,128)S(1)}, f32[512,128]{1,0:T(8,128)}, f32[512,128]{1,0:T(8,128)}) custom-call(bf16[32,4,256]{2,1,0:T(4,128)(2,1)S(1)} %all-to-all-done.features, f32[2048,128]{1,0:T(8,128)S(1)} %recurrent.1.sums, f32[4,512]{1,0:T(4,128)S(1)} %copy-done.5, bf16[4,512,256]{2,1,0:T(8,128)(2,1)S(1)} %copy-done.2, f32[512,128]{1,0:T(8,128)S(1)} %copy-done.1, ...), custom_call_target="tpu_custom_call" | custom-call | flops 134217728 | bytes 4000000 | tf_op jit(solution)/shard_map/core/pallas_call | solution.py:456
  37.9 12.7 %all_to_all.16 = f32[32,4,19]{2,1,0:T(4,128)S(1)} all-to-all(f32[32,4,19]{2,1,0:T(4,128)S(1)} %bitcast.12), channel_id=1, replica_groups=mesh['dp'=8,'tensor'=4] {'dp','tensor'}, dimensions={0} | all-to-all | bytes 19456 | tf_op jit(solution)/shard_map/all_to_all | solution.py:523
  50.6 1.4 %answers.1 = f32[19,32]{1,0:T(8,128)} custom-call(s32[4,8]{1,0:T(4,128)S(1)} %copy-done.6, f32[128,19]{1,0:T(8,128)S(1)} %bitcast.11), custom_call_target="tpu_custom_call" | custom-call | tf_op jit(solution)/shard_map/answers/pallas_call | solution.py:489
Async XLA Ops:
  2.2 18.0 %collective-permute-start.2 = (bf16[512,128]{1,0:T(8,128)(2,1)}, bf16[512,128]{1,0:T(8,128)(2,1)}, u32[]{:S(2)}, u32[]{:S(2)}) collective-permute-start(bf16[512,128]{1,0:T(8,128)(2,1)} %convert_element_type.3.refs_0_), channel_id=1, source_target_pairs={{0,3},{1,0},{2,1},{3,2},{4,7},{5,4},{6,5},{7,6},{8,11},{9,8},{10,9... | collective-permute-start | bytes 393224 | tf_op jit(solution)/shard_map/ppermute | solution.py:512
  7.3 12.9 %collective-permute-start.1 = (bf16[512,128]{1,0:T(8,128)(2,1)}, bf16[512,128]{1,0:T(8,128)(2,1)}, u32[]{:S(2)}, u32[]{:S(2)}) collective-permute-start(bf16[512,128]{1,0:T(8,128)(2,1)} %convert_element_type.3.refs_0_), channel_id=1, source_target_pairs={{0,2},{1,3},{2,0},{3,1},{4,6},{5,7},{6,4},{7,5},{8,10},{9,11},{10,... | collective-permute-start | bytes 393224 | tf_op jit(solution)/shard_map/ppermute | solution.py:512
  7.3 12.9 %collective-permute-start = (bf16[512,128]{1,0:T(8,128)(2,1)}, bf16[512,128]{1,0:T(8,128)(2,1)}, u32[]{:S(2)}, u32[]{:S(2)}) collective-permute-start(bf16[512,128]{1,0:T(8,128)(2,1)} %convert_element_type.3.refs_0_), channel_id=1, source_target_pairs={{0,1},{1,2},{2,3},{3,0},{4,5},{5,6},{6,7},{7,4},{8,9},{9,10},{10,1... | collective-permute-start | bytes 393224 | tf_op jit(solution)/shard_map/ppermute | solution.py:512
  20.2 15.6 %all-to-all-start = ((bf16[32,4,256]{2,1,0:T(4,128)(2,1)}), bf16[32,4,256]{2,1,0:T(4,128)(2,1)S(1)}, u32[]{:S(2)}, u32[]{:S(2)}) async-start(bf16[32,4,256]{2,1,0:T(4,128)(2,1)} %encoder.1), calls=%async_computation | async-start | bytes 131072 | tf_op jit(solution)/shard_map/all_to_all | solution.py:518
  28.3 3.4 %copy-start = (bf16[4,512,2048]{2,1,0:T(8,128)(2,1)S(1)}, bf16[4,512,2048]{2,1,0:T(8,128)(2,1)}, u32[]{:S(2)}) copy-start(bf16[4,512,2048]{2,1,0:T(8,128)(2,1)} %weight.2) | copy-start | bytes 25165828
  31.7 4.1 %copy-start.1 = (f32[512,128]{1,0:T(8,128)S(1)}, f32[512,128]{1,0:T(8,128)}, u32[]{:S(2)}) copy-start(f32[512,128]{1,0:T(8,128)} %hidden.1) | copy-start | bytes 786436
  31.7 4.1 %copy-start.2 = (bf16[4,512,256]{2,1,0:T(8,128)(2,1)S(1)}, bf16[4,512,256]{2,1,0:T(8,128)(2,1)}, u32[]{:S(2)}) copy-start(bf16[4,512,256]{2,1,0:T(8,128)(2,1)} %weight.3) | copy-start | bytes 3145732
  31.7 4.1 %copy-start.3 = (f32[512,128]{1,0:T(8,128)S(1)}, f32[512,128]{1,0:T(8,128)}, u32[]{:S(2)}) copy-start(f32[512,128]{1,0:T(8,128)} %cell.1) | copy-start | bytes 786436
  31.7 4.1 %copy-start.4 = (bf16[19,512]{1,0:T(8,128)(2,1)S(1)}, bf16[19,512]{1,0:T(8,128)(2,1)}, u32[]{:S(2)}) copy-start(bf16[19,512]{1,0:T(8,128)(2,1)} %heads.1) | copy-start | bytes 58372
  31.7 4.1 %copy-start.5 = (f32[4,512]{1,0:T(4,128)S(1)}, f32[4,512]{1,0:T(4,128)}, u32[]{:S(2)}) copy-start(f32[4,512]{1,0:T(4,128)} %bias.1) | copy-start | bytes 24580
  31.8 4.1 %copy-start.6 = (s32[4,8]{1,0:T(4,128)S(1)}, s32[4,8]{1,0:T(4,128)}, u32[]{:S(2)}) copy-start(s32[4,8]{1,0:T(4,128)} %counts.3) | copy-start | bytes 388
  31.8 4.1 %copy-start.7 = (s32[1,64]{1,0:T(1,128)S(1)}, s32[1,64]{1,0:T(1,128)}, u32[]{:S(2)}) copy-start(s32[1,64]{1,0:T(1,128)} %slots.1) | copy-start | bytes 772
  31.8 4.1 %copy-start.8 = (s32[1,128]{1,0:T(1,128)S(1)}, s32[1,128]{1,0:T(1,128)}, u32[]{:S(2)}) copy-start(s32[1,128]{1,0:T(1,128)} %resets.1) | copy-start | bytes 1540

commit v6 on v5

--- a/solution.py
+++ b/solution.py
@@ -2,7 +2,6 @@
 
 import jax
 import jax.numpy as jnp
-import numpy as np
 from jax import lax
 from jax.experimental import pallas as pl
 from jax.experimental.pallas import tpu as pltpu
@@ -32,6 +31,12 @@
 def log2(n):
     assert n & (n - 1) == 0
     return n.bit_length() - 1
+
+
+def divide(v, n, limit):
+    scale = -(-(1 << 16) // n)
+    assert all((k * scale) >> 16 == k // n for k in range(limit))
+    return (v * scale) >> 16
 
 
 def one_hot(mask):
@@ -58,61 +63,41 @@
         self.wide = -(-self.w3 * self.cap // LANES) * LANES
         assert self.wide - self.w3 * self.cap >= self.cap
 
-    def tables(self):
-        none = -(1 << 20)
-        rows = []
-        four = np.arange(4 * LANES)
-        quarter, lane = four // LANES, four % LANES
-
-        def source(x, width, live, where):
-            return np.where(live & (x >= 0) & (x < width), where, none)
-
-        j, i = lane // self.n1, lane % self.n1
-        x = 2 * j + quarter - 1
-        rows.append(source(x, self.f, j < self.w1, i * self.f + x))
-        j, i = lane // self.n2, lane % self.n2
-        x = 2 * j + quarter - 1
-        rows.append(source(x, self.w1, j < self.w2, i // self.n1 * LANES + x * self.n1 + i % self.n1))
-        six = np.arange(6 * LANES)
-        dx, half, lane = six // (2 * LANES), six // LANES % 2, six % LANES
-        evens = self.n2 * self.w3
-        odd = lane >= evens
-        j, i = np.where(odd, lane - evens, lane) // self.n2, lane % self.n2
-        x = 2 * j + odd + dx - 1
-        rows.append(source(x, self.w2, lane < self.n2 * self.w2, half * LANES + x * self.n2 + i))
-        final = np.arange(self.wide)
-        x, image = final // self.cap, final % self.cap
-        for pair in range(self.pairs):
-            i = image - pair * self.n3
-            live = (i >= 0) & (i < self.n3)
-            rows.append(source(x, self.w3, live, i // self.n2 * LANES + x * self.n2 + i % self.n2))
-        for window, c in ((self.win1, self.c0), (self.win2, self.c1), (self.win2, self.c2)):
-            k = np.arange(3 * window * c)
-            rows += [k // (window * c), k % (window * c) // c, k % c]
-        k = np.arange(self.c2 * self.w3)
-        rows.append(k % self.w3 * self.c2 + k // self.w3)
-        k = np.arange(PACK * self.w3)
-        rows += [k % self.w3, k // self.w3]
-        width = max(len(r) for r in rows)
-        table = np.full((-(-len(rows) // 8) * 8, width), none, np.int32)
-        for i, r in enumerate(rows):
-            table[i, : len(r)] = r
-        return table, [len(r) for r in rows]
-
-
-def encoder_kernel(z, lengths, dp, tensor, dp_index, tensor_index, *refs):
-    far, out, near = refs[:9], refs[9], refs[10:19]
-    p1, p2, p3, t1, t2, t3, t4, t5, g1, s1, g2, s2, g3, s3, x4, x5, projx, sems = refs[19:]
-    counts, table, w1, w2, w3, r1, r2, frames, proj = near
+
+def encoder_kernel(z, dp, tensor, dp_index, tensor_index, *refs):
+    far, out, near = refs[:8], refs[8], refs[9:17]
+    p1, p2, p3, t1, t2, t3, t4, t5, g1, s1, g2, s2, g3, s3, x4, x5, p4, flat, sems = refs[17:]
+    counts, w1, w2, w3, r1, r2, frames, proj = near
     copies = [pltpu.make_async_copy(a, b, sems.at[i]) for i, (a, b) in enumerate(zip(far, near))]
     for copy in copies:
         copy.start()
 
-    def row(i):
-        return table[i : i + 1, : lengths[i]]
-
-    def pick(rows, i):
-        return one_hot(iota((rows, lengths[i]), 0) == row(i))
+    def place(ref, x, width, live, where):
+        where = jnp.where(live & (x >= 0) & (x < width), where, -1)
+        ref[...] = one_hot(iota(ref.shape, 0) == where)
+
+    def split(columns, n):
+        v = iota((1, columns), 1)
+        lane = v & (LANES - 1)
+        j = divide(lane, n, LANES)
+        return v >> log2(LANES), lane, j, lane - j * n
+
+    quarter, _, j, i = split(4 * LANES, z.n1)
+    x = 2 * j + quarter - 1
+    place(p1, x, z.f, j < z.w1, i * z.f + x)
+    quarter, _, j, i = split(4 * LANES, z.n2)
+    x = 2 * j + quarter - 1
+    upper = (i >= z.n1).astype(I32)
+    place(p2, x, z.w1, j < z.w2, upper * (LANES - z.n1) + x * z.n1 + i)
+    part, lane, j, i = split(6 * LANES, z.n2)
+    odd = (lane >= z.n2 * z.w3).astype(I32)
+    x = 2 * (j - odd * z.w3) + odd + (part >> 1) - 1
+    place(p3, x, z.w2, lane < z.n2 * z.w2, (part & 1) * LANES + x * z.n2 + i)
+    v = iota((1, z.wide), 1)
+    for pair in range(z.pairs):
+        x, i = v >> log2(z.cap), (v & (z.cap - 1)) - pair * z.n3
+        upper = (i >= z.n2).astype(I32)
+        place(p4.at[pair], x, z.w3, (i >= 0) & (i < z.n3), upper * (LANES - z.n2) + x * z.n2 + i)
 
     maps = [(g1.at[i], PACK, z.f * z.c0) for i in range(4)]
     maps += [(g2.at[i], z.c1, z.w1 * z.c1) for i in range(2)]
@@ -126,20 +111,18 @@
             ref[q, : z.c2] = jnp.zeros((z.c2, z.wide), BF16)
             low = ref.shape[1] - z.c2 - z.w3 * z.c2
             ref[q, z.c2 + z.w3 * z.c2 :] = jnp.zeros((low, z.wide), BF16)
-    for copy in copies[:7]:
+    for copy in copies[:6]:
         copy.wait()
     own = counts[tensor_index(), dp_index()]
     pairs = lax.div(own + (z.n3 - 1), z.n3)
     s3[...] = jnp.zeros(s3.shape, BF16)
 
-    p1[...] = pick(z.n1 * z.f, 0)
-    p2[...] = pick(2 * LANES, 1)
-    p3[...] = pick(2 * LANES, 2)
-    base = 3 + z.pairs
-
-    def banded(weights, target, rows, cin, cout, index, first, dims):
-        which, line, channel = row(index), row(index + 1), row(index + 2)
-        k = lengths[index]
+    def banded(weights, target, rows, cin, cout, window, first, dims):
+        k = 3 * window * cin
+        v = iota((1, k), 1)
+        channel, line = v & (cin - 1), v >> log2(cin)
+        which = divide(line, window, 3 * window)
+        line = line - which * window
         spread = [one_hot((iota((cin, k), 0) == channel) & (which == dx)) for dx in range(3)]
         lines = []
         for dy in range(3):
@@ -154,10 +137,10 @@
                 value = jnp.where(line == y + first + dy, lines[dy], value)
             target[y * cout : (y + 1) * cout, :] = value.astype(BF16)
 
-    banded(w1, t1, Y1, z.c0, z.c1, base, z.pad1 - 1, TN)
-    banded(w2, t2, Y2, z.c1, z.c2, base + 3, 0, TN)
+    banded(w1, t1, Y1, z.c0, z.c1, z.win1, z.pad1 - 1, TN)
+    banded(w2, t2, Y2, z.c1, z.c2, z.win2, 0, TN)
     for weights, target in ((w3, t3), (r1, t4), (r2, t5)):
-        banded(weights, target, Y2, z.c2, z.c2, base + 6, 0, NN)
+        banded(weights, target, Y2, z.c2, z.c2, z.win2, 0, NN)
 
     def sides(ref, dx, low, rows):
         return jnp.concatenate(
@@ -259,11 +242,11 @@
         conv_three(p)
         return 0
 
-    copies[7].wait()
+    copies[6].wait()
     lax.fori_loop(0, pairs, convolve, 0)
     total = None
     for p in range(z.pairs):
-        part = mm(s3[p], pick(2 * LANES, 3 + p))
+        part = mm(s3[p], p4[p])
         total = part if total is None else total + part
 
     c, n = z.c2, z.w3 * z.c2
@@ -288,25 +271,15 @@
     spread_x(x4, jnp.maximum(total, 0.0))
     inner = residual(x4, t4, None).astype(BF16).astype(F32)
     spread_x(x5, jnp.where(live, inner, 0.0))
-    encoded = residual(x5, t5, total).astype(BF16)
-
-    last = len(lengths) - 3
-    order = one_hot(iota((n, n), 0) == row(last))
-    turned = jnp.swapaxes(encoded, 0, 1)
-    turned = mm(turned, order).astype(BF16)
-    copies[8].wait()
-    block = PACK * z.w3
-    wanted = iota((block, block), 0)
-    regroup = one_hot(((wanted >> log2(PACK)) == row(last + 1)) & ((wanted & (PACK - 1)) == row(last + 2)))
-    for b in range(n // PACK):
-        moved = mm(regroup, proj[b * block : (b + 1) * block, :]).astype(BF16)
+    encoded = residual(x5, t5, total).astype(BF16).astype(F32)
+
+    for y in range(z.w3):
         for x in range(z.w3):
-            projx[x, b * PACK : (b + 1) * PACK, :] = moved[x * PACK : (x + 1) * PACK]
-    acc = None
-    for x in range(z.w3):
-        part = mm(turned[x * z.cap : (x + 1) * z.cap], projx[x])
-        acc = part if acc is None else acc + part
-    features = jnp.maximum(acc, 0.0).astype(BF16)
+            flat[pl.ds(y * z.w3 + x, c, stride=z.w3 * z.w3), :] = encoded[
+                y * c : (y + 1) * c, x * z.cap : (x + 1) * z.cap
+            ]
+    copies[7].wait()
+    features = jnp.maximum(mm(flat[...].astype(BF16), proj[...], TN), 0.0).astype(BF16)
 
     start = jnp.int32(0)
     for a in range(dp):
@@ -323,14 +296,12 @@
 def encode_rows(frames, counts, kernels, projection):
     first, second, third, res_first, res_second = kernels
     z = Sizes(frames.shape, first.shape, second.shape, projection.shape)
-    table, lengths = z.tables()
     dp, tensor = lax.axis_size("dp"), lax.axis_size("tensor")
     images = jnp.transpose(frames, (0, 2, 1, 3)).reshape(z.cap, z.f * z.c0, z.f)
     ci_co, co_ci = (2, 3, 1, 0), (2, 3, 0, 1)
     n = z.w3 * z.c2
     operands = (
         counts,
-        jnp.asarray(table),
         jnp.transpose(first, ci_co),
         jnp.transpose(second, ci_co),
         jnp.transpose(third, co_ci),
@@ -360,11 +331,12 @@
         pltpu.VMEM((z.pairs, n, 2 * LANES), BF16),
         tall,
         tall,
-        pltpu.VMEM((z.w3, n, z.feat), BF16),
+        pltpu.VMEM((z.pairs, 2 * LANES, z.wide), BF16),
+        pltpu.VMEM((n * z.w3, z.cap), F32),
         pltpu.SemaphoreType.DMA((len(operands),)),
     ]
     body = functools.partial(
-        encoder_kernel, z, lengths, dp, tensor,
+        encoder_kernel, z, dp, tensor,
         lambda: lax.axis_index("dp"), lambda: lax.axis_index("tensor"),
     )
     return pl.pallas_call(
@@ -379,39 +351,17 @@
     )(*operands)
 
 
-def recurrent_kernel(index, weight, *refs):
-    *pieces, out, hidden = refs
+def recurrent_kernel(index, dp_index, weight, bias, counts, slots, resets, *refs):
+    *pieces, out, chosen, hidden = refs
     gates, share, _ = weight.shape
-    width = pieces[0].shape[0]
+    tensor, dp = counts.shape
+    width, places = pieces[0].shape
     for back, piece in enumerate(pieces):
-        low = pl.multiple_of(((index() - back) & (len(pieces) - 1)) * width, width)
+        low = pl.multiple_of(((index() - back) & (tensor - 1)) * width, width)
         hidden[pl.ds(low, width), :] = piece[...]
-    for q in range(gates):
-        out[q * share : (q + 1) * share, :] = mm(weight[q], hidden[...])
-
-
-def recurrent(weight, pieces):
-    gates, share, hidden = weight.shape
-    slots = pieces[0].shape[1]
-    return pl.pallas_call(
-        functools.partial(recurrent_kernel, lambda: lax.axis_index("tensor")),
-        name="recurrent",
-        out_shape=jax.ShapeDtypeStruct((gates * share, slots), F32),
-        in_specs=[VMEM] * (1 + len(pieces)),
-        out_specs=VMEM,
-        scratch_shapes=[pltpu.VMEM((hidden, slots), BF16)],
-        compiler_params=pltpu.CompilerParams(vmem_limit_bytes=24 << 20),
-        cost_estimate=pl.CostEstimate(
-            flops=2 * gates * share * hidden * slots, bytes_accessed=2 * gates * share * hidden, transcendentals=0
-        ),
-    )(weight, *pieces)
-
-
-def core_kernel(dp_index, features, sums, bias, weight, hidden, cell, heads, slots, counts, resets, sent, hidden_out, cell_out):
-    tensor, dp = counts.shape
-    depth, count = features.shape[1], slots.shape[1]
-    rows = dp * tensor * depth
-    share, places = hidden.shape
+
+    rows, count = chosen.shape[0], slots.shape[1]
+    depth = rows // (dp * tensor)
     mine = dp_index()
     exact = lax.Precision.HIGHEST
     tallies = counts[...].astype(F32)
@@ -432,42 +382,71 @@
     balanced = group * (count // tensor) + ((rank - mine) >> log2(dp))
     to_row = one_hot((iota((rows, count), 1) == balanced) & (rank < end))
     of_slot = one_hot(iota((places, count), 0) == slots[...])
-    chosen = mm(to_row, of_slot, NT)
-    taken = jnp.sum(chosen, axis=0, keepdims=True) > 0.5
-    inputs = mm(features[...].reshape(rows, -1), chosen.astype(BF16), TN).astype(BF16)
+    chosen[...] = mm(to_row, of_slot, NT).astype(BF16)
+
+    keep = 1.0 - resets[...].astype(F32)
+    for q in range(gates):
+        column = jnp.transpose(jnp.broadcast_to(bias[q : q + 1, :], (places, share)))
+        out[q * share : (q + 1) * share, :] = mm(weight[q], hidden[...]) * keep + column
+
+
+def recurrent(weight, bias, counts, slots, resets, pieces, rows):
+    gates, share, hidden = weight.shape
+    places = pieces[0].shape[1]
+    return pl.pallas_call(
+        functools.partial(recurrent_kernel, lambda: lax.axis_index("tensor"), lambda: lax.axis_index("dp")),
+        name="recurrent",
+        out_shape=(
+            jax.ShapeDtypeStruct((gates * share, places), F32),
+            jax.ShapeDtypeStruct((rows, places), BF16),
+        ),
+        in_specs=[VMEM] * (5 + len(pieces)),
+        out_specs=(VMEM, VMEM),
+        scratch_shapes=[pltpu.VMEM((hidden, places), BF16)],
+        compiler_params=pltpu.CompilerParams(vmem_limit_bytes=24 << 20),
+        cost_estimate=pl.CostEstimate(
+            flops=2 * gates * share * hidden * places, bytes_accessed=2 * gates * share * hidden, transcendentals=0
+        ),
+    )(weight, bias, counts, slots, resets, *pieces)
+
+
+def core_kernel(features, sums, chosen, weight, hidden, cell, heads, resets, sent, hidden_out, cell_out):
+    share = hidden.shape[0]
+    rows = chosen.shape[0]
+    picked = chosen[...].astype(F32)
+    taken = jnp.sum(picked, axis=0, keepdims=True) > 0.5
+    inputs = mm(features[...].reshape(rows, -1), chosen[...], TN).astype(BF16)
     keep = 1.0 - resets[...].astype(F32)
     old_cell = cell[...]
 
     def gate(q):
-        low = q * share
-        column = jnp.transpose(jnp.broadcast_to(bias[q : q + 1, :], (places, share)))
-        return mm(weight[q], inputs) + (sums[low : low + share, :] * keep + column)
+        return mm(weight[q], inputs) + sums[q * share : (q + 1) * share, :]
 
     next_cell = jax.nn.sigmoid(gate(1)) * (old_cell * keep) + jax.nn.sigmoid(gate(0)) * jnp.tanh(gate(2))
     next_hidden = jax.nn.sigmoid(gate(3)) * jnp.tanh(next_cell)
     values = mm(heads[...], next_hidden.astype(BF16))
-    sent[...] = mm(chosen, values, NT, precision=exact)
+    sent[...] = mm(picked, values, NT, precision=lax.Precision.HIGHEST)
     cell_out[...] = jnp.where(taken, next_cell, old_cell)
     hidden_out[...] = jnp.where(taken, next_hidden, hidden[...])
 
 
-def core(features, sums, bias, weight, hidden, cell, heads, slots, counts, resets):
+def core(features, sums, chosen, weight, hidden, cell, heads, resets):
     share = hidden.shape[0]
     return pl.pallas_call(
-        functools.partial(core_kernel, lambda: lax.axis_index("dp")),
+        core_kernel,
         name="core",
         out_shape=(
-            jax.ShapeDtypeStruct((features.shape[0] * features.shape[1], heads.shape[0]), F32),
+            jax.ShapeDtypeStruct((chosen.shape[0], heads.shape[0]), F32),
             jax.ShapeDtypeStruct(hidden.shape, F32),
             jax.ShapeDtypeStruct(cell.shape, F32),
         ),
-        in_specs=[VMEM] * 10,
+        in_specs=[VMEM] * 8,
         out_specs=(VMEM,) * 3,
         compiler_params=pltpu.CompilerParams(vmem_limit_bytes=24 << 20),
         cost_estimate=pl.CostEstimate(
             flops=8 * share * weight.shape[2] * hidden.shape[1], bytes_accessed=4_000_000, transcendentals=0
         ),
-    )(features, sums, bias, weight, hidden, cell, heads, slots, counts, resets)
+    )(features, sums, chosen, weight, hidden, cell, heads, resets)
 
 
 def answers_kernel(tensor, dp_index, tensor_index, counts, received, out):
@@ -516,9 +495,10 @@
     features = encode_rows(frames, counts, kernels, projection)
     features, pieces = lax.optimization_barrier((features, pieces))
     features = lax.all_to_all(features, ("dp", "tensor"), 0, 0, tiled=True)
-    sums = recurrent(recur_weight, pieces)
+    rows = features.shape[0] * features.shape[1]
+    sums, chosen = recurrent(recur_weight, gate_bias, counts, slot_ids, reset_flags, pieces, rows)
     sent, hidden_after, cell_after = core(
-        features, sums, gate_bias, input_weight, hidden_state, cell_state, head_weight, slot_ids, counts, reset_flags
+        features, sums, chosen, input_weight, hidden_state, cell_state, head_weight, reset_flags
     )
     received = lax.all_to_all(sent, ("dp", "tensor"), 0, 0, tiled=True)
     return answers(counts, received, frames.shape[0]), hidden_after, cell_after

time: 51.7 us -> 53.5 us (1.035); the launches traced: 51.9 us -> 52.9 us
  Pallas kernels: 18.8 us -> 14.9 us
  local copies, waits for them, and re-layouts: 3.42 us -> 6.09 us
  waiting for transfers between devices: 0.5 us -> 2.38 us
    pallas_call x1, Pallas kernels: 11.9 us -> 8.13 us  [encode_rows(): pl.pallas_call(body, name='encoder', out_shape=jax.ShapeDtypeStruct((dp *...]
    unnamed x18 -> x22, local copies, waits for them, and re-layouts: 3.42 us -> 6.09 us
    ppermute x3, waiting for transfers between devices: 0.01 us -> 2.37 us  [body(): lax.ppermute(own, 'tensor', [(i, (i + back) % tensor) for i in range(tens...]
    pallas_call x1, Pallas kernels: 1.98 us -> 1.4 us  [core(): pl.pallas_call(core_kernel, name='core', out_shape=(jax.ShapeDtypeStruct(...]
  transfers between devices with their start and end apart: 4 -> 4, of which waited for: 1 -> 1; matrix products, arithmetic and copies ran while one was open for 0% -> 0% of each run, Pallas kernels for 30% -> 23%
where the time goes in v6:
time: 53.5 us; the launch traced here: 52.9 us
  Pallas kernels  14.9 us (28%)
  starting transfers between devices  14 us (26%)
  blocking collectives  13.1 us (24%)
  local copies, waits for them, and re-layouts  6.09 us (11%)
  waiting for transfers between devices  2.38 us (4%)
  other arithmetic  1.62 us (3%)
  between operations  0.74 us (1%)
    all_to_all x1, blocking collectives, body(): received = lax.all_to_all(sent, ('dp', 'tensor'), 0, 0, tiled=True)  13.1 us
    pallas_call x1, Pallas kernels, encode_rows(): pl.pallas_call(body, name='encoder', out_shape=jax.ShapeDtypeStruct((dp *...  8.13 us
    all_to_all x1, starting transfers between devices, body(): features = lax.all_to_all(features, ('dp', 'tensor'), 0, 0, tiled=True)  7.9 us
    ppermute x3, starting transfers between devices, body(): lax.ppermute(own, 'tensor', [(i, (i + back) % tensor) for i in range(tens...  6.09 us
    unnamed x22, local copies, waits for them, and re-layouts  6.09 us
    pallas_call x1, Pallas kernels, recurrent(): pl.pallas_call(functools.partial(recurrent_kernel, lambda: lax.axis_index...  3.98 us
    ppermute x3, waiting for transfers between devices, body(): lax.ppermute(own, 'tensor', [(i, (i + back) % tensor) for i in range(tens...  2.37 us
    convert_element_type x1, other arithmetic, body(): own = hidden_state.astype(BF16)  1.62 us
  transfers between devices with their start and end apart: 4, of which 1 were waited for; matrix products, arithmetic and copies ran while one was open for 0% of the time, Pallas kernels for 23%

profile of v6, /device:TPU:0, one launch (start us, length us, event | category | flops | bytes accessed | tf_op | source)
XLA Modules:
  0.0 52.9 jit_solution(6464285160857435463)
XLA Ops:
  0.6 1.6 %convert_element_type.3.refs_0_ = bf16[512,128]{1,0:T(8,128)(2,1)} convert(f32[512,128]{1,0:T(8,128)} %hidden.1) | non-fusion elementwise | flops 65536 | bytes 393216 | tf_op jit(solution)/shard_map/convert_element_type | solution.py:489
  2.2 5.1 %collective-permute-start.2 = (bf16[512,128]{1,0:T(8,128)(2,1)}, bf16[512,128]{1,0:T(8,128)(2,1)}, u32[]{:S(2)}, u32[]{:S(2)}) collective-permute-start(bf16[512,128]{1,0:T(8,128)(2,1)} %convert_element_type.3.refs_0_), channel_id=1, source_target_pairs={{0,3},{1,0},{2,1},{3,2},{4,7},{5,4},{6,5},{7,6},{8,11},{9,8},{10,9... | collective-permute-start | bytes 393224 | tf_op jit(solution)/shard_map/ppermute | solution.py:491
  7.3 0.0 collective-permute-start.1
  7.3 1.0 %collective-permute-start = (bf16[512,128]{1,0:T(8,128)(2,1)}, bf16[512,128]{1,0:T(8,128)(2,1)}, u32[]{:S(2)}, u32[]{:S(2)}) collective-permute-start(bf16[512,128]{1,0:T(8,128)(2,1)} %convert_element_type.3.refs_0_), channel_id=1, source_target_pairs={{0,1},{1,2},{2,3},{3,0},{4,5},{5,6},{6,7},{7,4},{8,9},{9,10},{10,1... | collective-permute-start | bytes 393224 | tf_op jit(solution)/shard_map/ppermute | solution.py:491
  8.3 8.1 %encoder.1 = bf16[32,4,256]{2,1,0:T(4,128)(2,1)} custom-call(s32[4,8]{1,0:T(4,128)} %counts.3, bf16[3,3,4,16]{3,2,1,0:T(4,128)(2,1)} %bitcast.19, bf16[3,3,16,32]{3,2,1,0:T(8,128)(2,1)} %bitcast.18, bf16[3,3,32,32]{3,2,1,0:T(8,128)(2,1)} %bitcast.15, bf16[3,3,32,32]{3,2,1,0:T(8,128)(2,1)} %bitcast.16, bf16[3,3,32,32]{3,2,1,0:T(8,128)(2,1)} %bitcast.17, ...), custom_call_target="tpu_custom_call" | custom-call | flops 20000000000 | bytes 8000000 | tf_op jit(solution)/shard_map/encoder/pallas_call | solution.py:342
  16.5 0.0 collective-permute-done.2.refs_3_
  16.5 2.4 %collective-permute-done.1.refs_2_ = bf16[512,128]{1,0:T(8,128)(2,1)} collective-permute-done((bf16[512,128]{1,0:T(8,128)(2,1)}, bf16[512,128]{1,0:T(8,128)(2,1)}, u32[]{:S(2)}, u32[]{:S(2)}) %collective-permute-start.1) | collective-permute-done | bytes 131104 | tf_op jit(solution)/shard_map/ppermute | solution.py:491
  18.9 0.0 collective-permute-done.refs_1_
  18.9 7.9 %all-to-all-start = ((bf16[32,4,256]{2,1,0:T(4,128)(2,1)}), bf16[32,4,256]{2,1,0:T(4,128)(2,1)S(1)}, u32[]{:S(2)}, u32[]{:S(2)}) async-start(bf16[32,4,256]{2,1,0:T(4,128)(2,1)} %encoder.1), calls=%async_computation | async-start | bytes 131072 | tf_op jit(solution)/shard_map/all_to_all | solution.py:497
  26.8 0.0 copy-start
  26.8 3.4 %copy-done = bf16[4,512,2048]{2,1,0:T(8,128)(2,1)S(1)} copy-done((bf16[4,512,2048]{2,1,0:T(8,128)(2,1)S(1)}, bf16[4,512,2048]{2,1,0:T(8,128)(2,1)}, u32[]{:S(2)}) %copy-start) | copy-done | bytes 8388632
  30.2 0.0 copy-start.5
  30.2 0.7 %copy-done.5 = f32[4,512]{1,0:T(4,128)S(1)} copy-done((f32[4,512]{1,0:T(4,128)S(1)}, f32[4,512]{1,0:T(4,128)}, u32[]{:S(2)}) %copy-start.5) | copy-done | bytes 8216
  30.9 0.0 copy-start.6
  30.9 0.7 %copy-done.6 = s32[4,8]{1,0:T(4,128)S(1)} copy-done((s32[4,8]{1,0:T(4,128)S(1)}, s32[4,8]{1,0:T(4,128)}, u32[]{:S(2)}) %copy-start.6) | copy-done | bytes 152
  31.5 0.0 copy-start.8
  31.5 0.7 %copy-done.8 = s32[1,128]{1,0:T(1,128)S(1)} copy-done((s32[1,128]{1,0:T(1,128)S(1)}, s32[1,128]{1,0:T(1,128)}, u32[]{:S(2)}) %copy-start.8) | copy-done | bytes 536
  32.2 0.0 copy-start.10
  32.2 0.7 %copy-done.10 = s32[1,64]{1,0:T(1,128)S(1)} copy-done((s32[1,64]{1,0:T(1,128)S(1)}, s32[1,64]{1,0:T(1,128)}, u32[]{:S(2)}) %copy-start.10) | copy-done | bytes 280
  32.8 0.0 copy-start.1
  32.9 0.0 copy-start.2
  32.9 0.0 copy-start.3
  32.9 0.0 copy-start.4
  32.9 0.0 copy-start.9
  32.9 4.0 %recurrent.1 = (f32[2048,128]{1,0:T(8,128)S(1)}, bf16[128,128]{1,0:T(8,128)(2,1)S(1)}) custom-call(bf16[4,512,2048]{2,1,0:T(8,128)(2,1)S(1)} %copy-done, f32[4,512]{1,0:T(4,128)S(1)} %copy-done.5, s32[4,8]{1,0:T(4,128)S(1)} %copy-done.6, s32[1,64]{1,0:T(1,128)S(1)} %copy-done.10, s32[1,128]{1,0:T(1,128)S(1)} %copy-done.8, ...), custom_call_target="tpu_custom_call" | custom-call | flops 1073741824 | bytes 8388608 | tf_op jit(solution)/shard_map/recurrent/pallas_call | solution.py:396
  36.9 0.0 copy-start.7
  36.9 0.0 all-to-all-done.features
  36.9 0.0 copy-done.1
  36.9 0.0 copy-done.2
  36.9 0.0 copy-done.3
  36.9 0.0 copy-done.4
  36.9 0.0 copy-done.9
  36.9 1.4 %core.1 = (f32[128,19]{1,0:T(8,128)S(1)}, f32[512,128]{1,0:T(8,128)}, f32[512,128]{1,0:T(8,128)}) custom-call(bf16[32,4,256]{2,1,0:T(4,128)(2,1)S(1)} %all-to-all-done.features, f32[2048,128]{1,0:T(8,128)S(1)} %get-tuple-element.18.sums, bf16[128,128]{1,0:T(8,128)(2,1)S(1)} %get-tuple-element.19.chosen, bf16[4,512,256]{2,1,0:T(8,128)(2,1)S(1)} %copy-done.2, ...), custom_call_target="tpu_custom_call" | custom-call | flops 134217728 | bytes 4000000 | tf_op jit(solution)/shard_map/core/pallas_call | solution.py:435
  38.3 13.1 %all_to_all.16 = f32[32,4,19]{2,1,0:T(4,128)S(1)} all-to-all(f32[32,4,19]{2,1,0:T(4,128)S(1)} %bitcast.12), channel_id=1, replica_groups=mesh['dp'=8,'tensor'=4] {'dp','tensor'}, dimensions={0} | all-to-all | bytes 19456 | tf_op jit(solution)/shard_map/all_to_all | solution.py:503
  51.5 0.0 copy-done.7
  51.5 1.4 %answers.1 = f32[19,32]{1,0:T(8,128)} custom-call(s32[4,8]{1,0:T(4,128)S(1)} %copy-done.7, f32[128,19]{1,0:T(8,128)S(1)} %bitcast.11), custom_call_target="tpu_custom_call" | custom-call | tf_op jit(solution)/shard_map/answers/pallas_call | solution.py:468
Async XLA Ops:
  2.2 14.2 %collective-permute-start.2 = (bf16[512,128]{1,0:T(8,128)(2,1)}, bf16[512,128]{1,0:T(8,128)(2,1)}, u32[]{:S(2)}, u32[]{:S(2)}) collective-permute-start(bf16[512,128]{1,0:T(8,128)(2,1)} %convert_element_type.3.refs_0_), channel_id=1, source_target_pairs={{0,3},{1,0},{2,1},{3,2},{4,7},{5,4},{6,5},{7,6},{8,11},{9,8},{10,9... | collective-permute-start | bytes 393224 | tf_op jit(solution)/shard_map/ppermute | solution.py:491
  7.3 11.5 %collective-permute-start.1 = (bf16[512,128]{1,0:T(8,128)(2,1)}, bf16[512,128]{1,0:T(8,128)(2,1)}, u32[]{:S(2)}, u32[]{:S(2)}) collective-permute-start(bf16[512,128]{1,0:T(8,128)(2,1)} %convert_element_type.3.refs_0_), channel_id=1, source_target_pairs={{0,2},{1,3},{2,0},{3,1},{4,6},{5,7},{6,4},{7,5},{8,10},{9,11},{10,... | collective-permute-start | bytes 393224 | tf_op jit(solution)/shard_map/ppermute | solution.py:491
  7.3 11.5 %collective-permute-start = (bf16[512,128]{1,0:T(8,128)(2,1)}, bf16[512,128]{1,0:T(8,128)(2,1)}, u32[]{:S(2)}, u32[]{:S(2)}) collective-permute-start(bf16[512,128]{1,0:T(8,128)(2,1)} %convert_element_type.3.refs_0_), channel_id=1, source_target_pairs={{0,1},{1,2},{2,3},{3,0},{4,5},{5,6},{6,7},{7,4},{8,9},{9,10},{10,1... | collective-permute-start | bytes 393224 | tf_op jit(solution)/shard_map/ppermute | solution.py:491
  18.9 18.0 %all-to-all-start = ((bf16[32,4,256]{2,1,0:T(4,128)(2,1)}), bf16[32,4,256]{2,1,0:T(4,128)(2,1)S(1)}, u32[]{:S(2)}, u32[]{:S(2)}) async-start(bf16[32,4,256]{2,1,0:T(4,128)(2,1)} %encoder.1), calls=%async_computation | async-start | bytes 131072 | tf_op jit(solution)/shard_map/all_to_all | solution.py:497
  26.8 3.4 %copy-start = (bf16[4,512,2048]{2,1,0:T(8,128)(2,1)S(1)}, bf16[4,512,2048]{2,1,0:T(8,128)(2,1)}, u32[]{:S(2)}) copy-start(bf16[4,512,2048]{2,1,0:T(8,128)(2,1)} %weight.2) | copy-start | bytes 25165828
  30.2 0.7 %copy-start.5 = (f32[4,512]{1,0:T(4,128)S(1)}, f32[4,512]{1,0:T(4,128)}, u32[]{:S(2)}) copy-start(f32[4,512]{1,0:T(4,128)} %bias.1) | copy-start | bytes 24580
  30.9 0.7 %copy-start.6 = (s32[4,8]{1,0:T(4,128)S(1)}, s32[4,8]{1,0:T(4,128)}, u32[]{:S(2)}) copy-start(s32[4,8]{1,0:T(4,128)} %counts.3) | copy-start | bytes 388
  31.5 0.7 %copy-start.8 = (s32[1,128]{1,0:T(1,128)S(1)}, s32[1,128]{1,0:T(1,128)}, u32[]{:S(2)}) copy-start(s32[1,128]{1,0:T(1,128)} %resets.3) | copy-start | bytes 1540
  32.2 0.7 %copy-start.10 = (s32[1,64]{1,0:T(1,128)S(1)}, s32[1,64]{1,0:T(1,128)}, u32[]{:S(2)}) copy-start(s32[1,64]{1,0:T(1,128)} %slots.1) | copy-start | bytes 772
  32.8 4.0 %copy-start.1 = (f32[512,128]{1,0:T(8,128)S(1)}, f32[512,128]{1,0:T(8,128)}, u32[]{:S(2)}) copy-start(f32[512,128]{1,0:T(8,128)} %hidden.1) | copy-start | bytes 786436
  32.9 4.0 %copy-start.2 = (bf16[4,512,256]{2,1,0:T(8,128)(2,1)S(1)}, bf16[4,512,256]{2,1,0:T(8,128)(2,1)}, u32[]{:S(2)}) copy-start(bf16[4,512,256]{2,1,0:T(8,128)(2,1)} %weight.3) | copy-start | bytes 3145732
  32.9 4.1 %copy-start.3 = (f32[512,128]{1,0:T(8,128)S(1)}, f32[512,128]{1,0:T(8,128)}, u32[]{:S(2)}) copy-start(f32[512,128]{1,0:T(8,128)} %cell.1) | copy-start | bytes 786436
  32.9 4.1 %copy-start.4 = (bf16[19,512]{1,0:T(8,128)(2,1)S(1)}, bf16[19,512]{1,0:T(8,128)(2,1)}, u32[]{:S(2)}) copy-start(bf16[19,512]{1,0:T(8,128)(2,1)} %heads.1) | copy-start | bytes 58372
  32.9 4.1 %copy-start.9 = (s32[1,128]{1,0:T(1,128)S(1)}, s32[1,128]{1,0:T(1,128)}, u32[]{:S(2)}) copy-start(s32[1,128]{1,0:T(1,128)} %resets.3) | copy-start | bytes 1540
  36.9 14.6 %copy-start.7 = (s32[4,8]{1,0:T(4,128)S(1)}, s32[4,8]{1,0:T(4,128)}, u32[]{:S(2)}) copy-start(s32[4,8]{1,0:T(4,128)} %counts.3) | copy-start | bytes 388

commit v7 on v6

--- a/solution.py
+++ b/solution.py
@@ -9,7 +9,6 @@
 
 F32, BF16, I32 = jnp.float32, jnp.bfloat16, jnp.int32
 LANES = 128
-VMEM_MOST = 67_043_328
 PACK = 16
 Y1, Y2 = 12, 3
 NN = (((1,), (0,)), ((), ()))
@@ -346,14 +345,24 @@
         in_specs=[HBM] * len(operands),
         out_specs=VMEM,
         scratch_shapes=scratch,
-        compiler_params=pltpu.CompilerParams(vmem_limit_bytes=VMEM_MOST),
+        compiler_params=pltpu.CompilerParams(vmem_limit_bytes=40 << 20),
         cost_estimate=pl.CostEstimate(flops=20_000_000_000, bytes_accessed=8_000_000, transcendentals=0),
-    )(*operands)
+    )(*[pltpu.with_memory_space_constraint(x, pltpu.HBM) for x in operands])
 
 
 def recurrent_kernel(index, dp_index, weight, bias, counts, slots, resets, *refs):
-    *pieces, out, chosen, hidden = refs
+    *pieces, out, chosen, hidden, held, sems = refs
     gates, share, _ = weight.shape
+    slot_count, tall, _ = held.shape
+    chunks = gates * share // tall
+
+    def copy(i):
+        q, low = divmod(i * tall, share)
+        slot = i % slot_count
+        return pltpu.make_async_copy(weight.at[q, pl.ds(low, tall)], held.at[slot], sems.at[slot])
+
+    for i in range(slot_count - 1):
+        copy(i).start()
     tensor, dp = counts.shape
     width, places = pieces[0].shape
     for back, piece in enumerate(pieces):
@@ -385,9 +394,13 @@
     chosen[...] = mm(to_row, of_slot, NT).astype(BF16)
 
     keep = 1.0 - resets[...].astype(F32)
-    for q in range(gates):
-        column = jnp.transpose(jnp.broadcast_to(bias[q : q + 1, :], (places, share)))
-        out[q * share : (q + 1) * share, :] = mm(weight[q], hidden[...]) * keep + column
+    for i in range(chunks):
+        q, low = divmod(i * tall, share)
+        column = jnp.transpose(jnp.broadcast_to(bias[q : q + 1, low : low + tall], (places, tall)))
+        copy(i).wait()
+        if i + slot_count - 1 < chunks:
+            copy(i + slot_count - 1).start()
+        out[i * tall : (i + 1) * tall, :] = mm(held[i % slot_count], hidden[...]) * keep + column
 
 
 def recurrent(weight, bias, counts, slots, resets, pieces, rows):
@@ -400,14 +413,18 @@
             jax.ShapeDtypeStruct((gates * share, places), F32),
             jax.ShapeDtypeStruct((rows, places), BF16),
         ),
-        in_specs=[VMEM] * (5 + len(pieces)),
+        in_specs=[HBM] + [VMEM] * (4 + len(pieces)),
         out_specs=(VMEM, VMEM),
-        scratch_shapes=[pltpu.VMEM((hidden, places), BF16)],
+        scratch_shapes=[
+            pltpu.VMEM((hidden, places), BF16),
+            pltpu.VMEM((4, share // 2, hidden), BF16),
+            pltpu.SemaphoreType.DMA((4,)),
+        ],
         compiler_params=pltpu.CompilerParams(vmem_limit_bytes=24 << 20),
         cost_estimate=pl.CostEstimate(
             flops=2 * gates * share * hidden * places, bytes_accessed=2 * gates * share * hidden, transcendentals=0
         ),
-    )(weight, bias, counts, slots, resets, *pieces)
+    )(pltpu.with_memory_space_constraint(weight, pltpu.HBM), bias, counts, slots, resets, *pieces)
 
 
 def core_kernel(features, sums, chosen, weight, hidden, cell, heads, resets, sent, hidden_out, cell_out):

time: 53.5 us -> 48.2 us (0.901); the launches traced: 52.9 us -> 48.4 us
  Pallas kernels: 14.9 us -> 22.3 us
  local copies, waits for them, and re-layouts: 6.09 us -> 0.04 us
  starting transfers between devices: 14 us -> 11.2 us
  blocking collectives: 13.1 us -> 11 us
  other arithmetic: 1.62 us -> 0.97 us
    pallas_call x1, Pallas kernels: 8.13 us -> 14.3 us  [encode_rows(): pl.pallas_call(body, name='encoder', out_shape=jax.ShapeDtypeStruct((dp *...]
    unnamed x22 -> x16, local copies, waits for them, and re-layouts: 6.09 us -> 0.04 us
    all_to_all x1, starting transfers between devices: 7.9 us -> 5.06 us  [body(): features = lax.all_to_all(features, ('dp', 'tensor'), 0, 0, tiled=True)]
    ppermute x3, waiting for transfers between devices: 2.37 us -> 0.01 us  [body(): lax.ppermute(own, 'tensor', [(i, (i + back) % tensor) for i in range(tens...]
    all_to_all x1, waiting for transfers between devices: 0.01 us -> 2.15 us  [body(): features = lax.all_to_all(features, ('dp', 'tensor'), 0, 0, tiled=True)]
    all_to_all x1, blocking collectives: 13.1 us -> 11 us  [body(): received = lax.all_to_all(sent, ('dp', 'tensor'), 0, 0, tiled=True)]
    pallas_call x1, Pallas kernels: 3.98 us -> 5.25 us  [recurrent(): pl.pallas_call(functools.partial(recurrent_kernel, lambda: lax.axis_index...]
    convert_element_type x1, other arithmetic: 1.62 us -> 0.97 us  [body(): own = hidden_state.astype(BF16)]
  transfers between devices with their start and end apart: 4 -> 4, of which waited for: 1 -> 1; matrix products, arithmetic and copies ran while one was open for 0% -> 0% of each run, Pallas kernels for 23% -> 40%
where the time goes in v7:
time: 48.2 us; the launch traced here: 48.4 us
  Pallas kernels  22.3 us (46%)
  starting transfers between devices  11.2 us (23%)
  blocking collectives  11 us (23%)
  waiting for transfers between devices  2.16 us (4%)
  other arithmetic  0.97 us (2%)
  between operations  0.76 us (2%)
    pallas_call x1, Pallas kernels, encode_rows(): pl.pallas_call(body, name='encoder', out_shape=jax.ShapeDtypeStruct((dp *...  14.3 us
    all_to_all x1, blocking collectives, body(): received = lax.all_to_all(sent, ('dp', 'tensor'), 0, 0, tiled=True)  11 us
    ppermute x3, starting transfers between devices, body(): lax.ppermute(own, 'tensor', [(i, (i + back) % tensor) for i in range(tens...  6.14 us
    pallas_call x1, Pallas kernels, recurrent(): pl.pallas_call(functools.partial(recurrent_kernel, lambda: lax.axis_index...  5.25 us
    all_to_all x1, starting transfers between devices, body(): features = lax.all_to_all(features, ('dp', 'tensor'), 0, 0, tiled=True)  5.06 us
    all_to_all x1, waiting for transfers between devices, body(): features = lax.all_to_all(features, ('dp', 'tensor'), 0, 0, tiled=True)  2.15 us
    pallas_call x1, Pallas kernels, answers(): pl.pallas_call(functools.partial(answers_kernel, counts.shape[0], lambda:...  1.39 us
    pallas_call x1, Pallas kernels, core(): pl.pallas_call(core_kernel, name='core', out_shape=(jax.ShapeDtypeStruct(...  1.38 us
  transfers between devices with their start and end apart: 4, of which 1 were waited for; matrix products, arithmetic and copies ran while one was open for 0% of the time, Pallas kernels for 40%

profile of v7, /device:TPU:0, one launch (start us, length us, event | category | flops | bytes accessed | tf_op | source)
XLA Modules:
  0.0 48.4 jit_solution(9147805315843515007)
XLA Ops:
  0.6 1.0 %convert_element_type.3.refs_0_ = bf16[512,128]{1,0:T(8,128)(2,1)S(1)} convert(f32[512,128]{1,0:T(8,128)} %hidden.1) | non-fusion elementwise | flops 65536 | bytes 393216 | tf_op jit(solution)/shard_map/convert_element_type | solution.py:506
  1.6 5.1 %collective-permute-start.2 = (bf16[512,128]{1,0:T(8,128)(2,1)S(1)}, bf16[512,128]{1,0:T(8,128)(2,1)S(1)}, u32[]{:S(2)}, u32[]{:S(2)}) collective-permute-start(bf16[512,128]{1,0:T(8,128)(2,1)S(1)} %convert_element_type.3.refs_0_), channel_id=1, source_target_pairs={{0,3},{1,0},{2,1},{3,2},{4,7},{5,4},{6,5},{7,6},{8,11},{9,8},{10,9... | collective-permute-start | bytes 393224 | tf_op jit(solution)/shard_map/ppermute | solution.py:508
  6.7 0.0 collective-permute-start.1
  6.7 1.0 %collective-permute-start = (bf16[512,128]{1,0:T(8,128)(2,1)S(1)}, bf16[512,128]{1,0:T(8,128)(2,1)S(1)}, u32[]{:S(2)}, u32[]{:S(2)}) collective-permute-start(bf16[512,128]{1,0:T(8,128)(2,1)S(1)} %convert_element_type.3.refs_0_), channel_id=1, source_target_pairs={{0,1},{1,2},{2,3},{3,0},{4,5},{5,6},{6,7},{7,4},{8,9},{9,10},{10,1... | collective-permute-start | bytes 393224 | tf_op jit(solution)/shard_map/ppermute | solution.py:508
  7.7 0.0 copy-start.4
  7.7 0.0 copy-start.5
  7.7 0.0 copy-start.6
  7.8 0.0 copy-start.7
  7.8 14.3 %encoder.1 = bf16[32,4,256]{2,1,0:T(4,128)(2,1)} custom-call(s32[4,8]{1,0:T(4,128)} %counts.3, bf16[3,3,4,16]{3,2,1,0:T(4,128)(2,1)} %bitcast.19, bf16[3,3,16,32]{3,2,1,0:T(8,128)(2,1)} %bitcast.18, bf16[3,3,32,32]{3,2,1,0:T(8,128)(2,1)} %bitcast.15, bf16[3,3,32,32]{3,2,1,0:T(8,128)(2,1)} %bitcast.16, bf16[3,3,32,32]{3,2,1,0:T(8,128)(2,1)} %bitcast.17, ...), custom_call_target="tpu_custom_call" | custom-call | flops 20000000000 | bytes 8000000 | tf_op jit(solution)/shard_map/encoder/pallas_call | solution.py:341
  22.0 0.0 collective-permute-done.2.refs_3_
  22.0 0.0 collective-permute-done.1.refs_2_
  22.0 0.0 collective-permute-done.refs_1_
  22.1 5.1 %all-to-all-start = ((bf16[32,4,256]{2,1,0:T(4,128)(2,1)}), bf16[32,4,256]{2,1,0:T(4,128)(2,1)S(1)}, u32[]{:S(2)}, u32[]{:S(2)}) async-start(bf16[32,4,256]{2,1,0:T(4,128)(2,1)} %encoder.1), calls=%async_computation | async-start | bytes 131072 | tf_op jit(solution)/shard_map/all_to_all | solution.py:514
  27.1 0.0 copy-done.4
  27.1 0.0 copy-done.5
  27.1 0.0 copy-done.6
  27.2 0.0 copy-done.7
  27.2 0.0 copy-start
  27.2 0.0 copy-start.1
  27.2 0.0 copy-start.2
  27.2 0.0 copy-start.3
  27.2 5.2 %recurrent.1 = (f32[2048,128]{1,0:T(8,128)S(1)}, bf16[128,128]{1,0:T(8,128)(2,1)S(1)}) custom-call(bf16[4,512,2048]{2,1,0:T(8,128)(2,1)} %weight.2, f32[4,512]{1,0:T(4,128)S(1)} %copy-done.4, s32[4,8]{1,0:T(4,128)S(1)} %copy-done.5, s32[1,64]{1,0:T(1,128)S(1)} %copy-done.7, s32[1,128]{1,0:T(1,128)S(1)} %copy-done.6, ...), custom_call_target="tpu_custom_call" | custom-call | flops 1073741824 | bytes 8388608 | tf_op jit(solution)/shard_map/recurrent/pallas_call | solution.py:409
  32.5 2.2 %all-to-all-done.features = bf16[32,4,256]{2,1,0:T(4,128)(2,1)S(1)} async-done(((bf16[32,4,256]{2,1,0:T(4,128)(2,1)}), bf16[32,4,256]{2,1,0:T(4,128)(2,1)S(1)}, u32[]{:S(2)}, u32[]{:S(2)}) %all-to-all-start) | async-done | bytes 65568 | tf_op jit(solution)/shard_map/all_to_all | solution.py:514
  34.6 0.0 copy-done
  34.6 0.0 copy-done.1
  34.6 0.0 copy-done.2
  34.6 0.0 copy-done.3
  34.6 1.4 %core.1 = (f32[128,19]{1,0:T(8,128)S(1)}, f32[512,128]{1,0:T(8,128)}, f32[512,128]{1,0:T(8,128)}) custom-call(bf16[32,4,256]{2,1,0:T(4,128)(2,1)S(1)} %all-to-all-done.features, f32[2048,128]{1,0:T(8,128)S(1)} %get-tuple-element.18.sums, bf16[128,128]{1,0:T(8,128)(2,1)S(1)} %get-tuple-element.19.chosen, bf16[4,512,256]{2,1,0:T(8,128)(2,1)S(1)} %copy-done.1, ...), custom_call_target="tpu_custom_call" | custom-call | flops 134217728 | bytes 4000000 | tf_op jit(solution)/shard_map/core/pallas_call | solution.py:452
  36.0 11.0 %all_to_all.16 = f32[32,4,19]{2,1,0:T(4,128)S(1)} all-to-all(f32[32,4,19]{2,1,0:T(4,128)S(1)} %bitcast.12), channel_id=1, replica_groups=mesh['dp'=8,'tensor'=4] {'dp','tensor'}, dimensions={0} | all-to-all | bytes 19456 | tf_op jit(solution)/shard_map/all_to_all | solution.py:520
  47.0 1.4 %answers.1 = f32[19,32]{1,0:T(8,128)} custom-call(s32[4,8]{1,0:T(4,128)S(1)} %copy-done.5, f32[128,19]{1,0:T(8,128)S(1)} %bitcast.11), custom_call_target="tpu_custom_call" | custom-call | tf_op jit(solution)/shard_map/answers/pallas_call | solution.py:485
Async XLA Ops:
  1.6 20.4 %collective-permute-start.2 = (bf16[512,128]{1,0:T(8,128)(2,1)S(1)}, bf16[512,128]{1,0:T(8,128)(2,1)S(1)}, u32[]{:S(2)}, u32[]{:S(2)}) collective-permute-start(bf16[512,128]{1,0:T(8,128)(2,1)S(1)} %convert_element_type.3.refs_0_), channel_id=1, source_target_pairs={{0,3},{1,0},{2,1},{3,2},{4,7},{5,4},{6,5},{7,6},{8,11},{9,8},{10,9... | collective-permute-start | bytes 393224 | tf_op jit(solution)/shard_map/ppermute | solution.py:508
  6.7 15.3 %collective-permute-start.1 = (bf16[512,128]{1,0:T(8,128)(2,1)S(1)}, bf16[512,128]{1,0:T(8,128)(2,1)S(1)}, u32[]{:S(2)}, u32[]{:S(2)}) collective-permute-start(bf16[512,128]{1,0:T(8,128)(2,1)S(1)} %convert_element_type.3.refs_0_), channel_id=1, source_target_pairs={{0,2},{1,3},{2,0},{3,1},{4,6},{5,7},{6,4},{7,5},{8,10},{9,11},{10,... | collective-permute-start | bytes 393224 | tf_op jit(solution)/shard_map/ppermute | solution.py:508
  6.7 15.3 %collective-permute-start = (bf16[512,128]{1,0:T(8,128)(2,1)S(1)}, bf16[512,128]{1,0:T(8,128)(2,1)S(1)}, u32[]{:S(2)}, u32[]{:S(2)}) collective-permute-start(bf16[512,128]{1,0:T(8,128)(2,1)S(1)} %convert_element_type.3.refs_0_), channel_id=1, source_target_pairs={{0,1},{1,2},{2,3},{3,0},{4,5},{5,6},{6,7},{7,4},{8,9},{9,10},{10,1... | collective-permute-start | bytes 393224 | tf_op jit(solution)/shard_map/ppermute | solution.py:508
  7.7 19.4 %copy-start.4 = (f32[4,512]{1,0:T(4,128)S(1)}, f32[4,512]{1,0:T(4,128)}, u32[]{:S(2)}) copy-start(f32[4,512]{1,0:T(4,128)} %bias.1) | copy-start | bytes 24580
  7.7 19.4 %copy-start.5 = (s32[4,8]{1,0:T(4,128)S(1)}, s32[4,8]{1,0:T(4,128)}, u32[]{:S(2)}) copy-start(s32[4,8]{1,0:T(4,128)} %counts.3) | copy-start | bytes 388
  7.7 19.4 %copy-start.6 = (s32[1,128]{1,0:T(1,128)S(1)}, s32[1,128]{1,0:T(1,128)}, u32[]{:S(2)}) copy-start(s32[1,128]{1,0:T(1,128)} %resets.3) | copy-start | bytes 1540
  7.8 19.4 %copy-start.7 = (s32[1,64]{1,0:T(1,128)S(1)}, s32[1,64]{1,0:T(1,128)}, u32[]{:S(2)}) copy-start(s32[1,64]{1,0:T(1,128)} %slots.1) | copy-start | bytes 772
  22.1 12.6 %all-to-all-start = ((bf16[32,4,256]{2,1,0:T(4,128)(2,1)}), bf16[32,4,256]{2,1,0:T(4,128)(2,1)S(1)}, u32[]{:S(2)}, u32[]{:S(2)}) async-start(bf16[32,4,256]{2,1,0:T(4,128)(2,1)} %encoder.1), calls=%async_computation | async-start | bytes 131072 | tf_op jit(solution)/shard_map/all_to_all | solution.py:514
  27.2 7.5 %copy-start = (f32[512,128]{1,0:T(8,128)S(1)}, f32[512,128]{1,0:T(8,128)}, u32[]{:S(2)}) copy-start(f32[512,128]{1,0:T(8,128)} %hidden.1) | copy-start | bytes 786436
  27.2 7.4 %copy-start.1 = (bf16[4,512,256]{2,1,0:T(8,128)(2,1)S(1)}, bf16[4,512,256]{2,1,0:T(8,128)(2,1)}, u32[]{:S(2)}) copy-start(bf16[4,512,256]{2,1,0:T(8,128)(2,1)} %weight.3) | copy-start | bytes 3145732
  27.2 7.4 %copy-start.2 = (f32[512,128]{1,0:T(8,128)S(1)}, f32[512,128]{1,0:T(8,128)}, u32[]{:S(2)}) copy-start(f32[512,128]{1,0:T(8,128)} %cell.1) | copy-start | bytes 786436
  27.2 7.4 %copy-start.3 = (bf16[19,512]{1,0:T(8,128)(2,1)S(1)}, bf16[19,512]{1,0:T(8,128)(2,1)}, u32[]{:S(2)}) copy-start(bf16[19,512]{1,0:T(8,128)(2,1)} %heads.1) | copy-start | bytes 58372

commit v8 on v7

--- a/solution.py
+++ b/solution.py
@@ -15,7 +15,6 @@
 NT = (((1,), (1,)), ((), ()))
 TN = (((0,), (0,)), ((), ()))
 VMEM = pl.BlockSpec(memory_space=pltpu.VMEM)
-SMEM = pl.BlockSpec(memory_space=pltpu.SMEM)
 HBM = pl.BlockSpec(memory_space=pltpu.HBM)
 
 
@@ -67,8 +66,15 @@
     far, out, near = refs[:8], refs[8], refs[9:17]
     p1, p2, p3, t1, t2, t3, t4, t5, g1, s1, g2, s2, g3, s3, x4, x5, p4, flat, sems = refs[17:]
     counts, w1, w2, w3, r1, r2, frames, proj = near
-    copies = [pltpu.make_async_copy(a, b, sems.at[i]) for i, (a, b) in enumerate(zip(far, near))]
-    for copy in copies:
+    pairs = list(zip(far, near))
+    first = [pltpu.make_async_copy(a, b, sems.at[i]) for i, (a, b) in enumerate(pairs[:6])]
+    arriving = []
+    for low in range(0, z.cap, z.n3):
+        part = pl.ds(low, min(z.n3, z.cap - low))
+        sem = sems.at[len(first) + len(arriving)]
+        arriving.append(pltpu.make_async_copy(far[6].at[part], frames.at[part], sem))
+    final = pltpu.make_async_copy(far[7], proj, sems.at[len(first) + len(arriving)])
+    for copy in first + arriving + [final]:
         copy.start()
 
     def place(ref, x, width, live, where):
@@ -110,10 +116,10 @@
             ref[q, : z.c2] = jnp.zeros((z.c2, z.wide), BF16)
             low = ref.shape[1] - z.c2 - z.w3 * z.c2
             ref[q, z.c2 + z.w3 * z.c2 :] = jnp.zeros((low, z.wide), BF16)
-    for copy in copies[:6]:
+    for copy in first:
         copy.wait()
     own = counts[tensor_index(), dp_index()]
-    pairs = lax.div(own + (z.n3 - 1), z.n3)
+    steps = lax.div(own + (z.n3 - 1), z.n3)
     s3[...] = jnp.zeros(s3.shape, BF16)
 
     def banded(weights, target, rows, cin, cout, window, first, dims):
@@ -230,6 +236,8 @@
         pool_rows(blocks(), z.c2, z.w2, 1, write)
 
     def convolve(p, _):
+        for k, copy in enumerate(arriving):
+            pl.when(p == k)(copy.wait)
         for half in range(2):
             for slot in (2 * half, 2 * half + 1):
                 mix_one(4 * p + slot, slot)
@@ -241,8 +249,9 @@
         conv_three(p)
         return 0
 
-    copies[6].wait()
-    lax.fori_loop(0, pairs, convolve, 0)
+    lax.fori_loop(0, steps, convolve, 0)
+    for k, copy in enumerate(arriving):
+        pl.when(k >= steps)(copy.wait)
     total = None
     for p in range(z.pairs):
         part = mm(s3[p], p4[p])
@@ -277,7 +286,7 @@
             flat[pl.ds(y * z.w3 + x, c, stride=z.w3 * z.w3), :] = encoded[
                 y * c : (y + 1) * c, x * z.cap : (x + 1) * z.cap
             ]
-    copies[7].wait()
+    final.wait()
     features = jnp.maximum(mm(flat[...].astype(BF16), proj[...], TN), 0.0).astype(BF16)
 
     start = jnp.int32(0)
@@ -332,7 +341,7 @@
         tall,
         pltpu.VMEM((z.pairs, 2 * LANES, z.wide), BF16),
         pltpu.VMEM((n * z.w3, z.cap), F32),
-        pltpu.SemaphoreType.DMA((len(operands),)),
+        pltpu.SemaphoreType.DMA((len(operands) - 1 + z.pairs,)),
     ]
     body = functools.partial(
         encoder_kernel, z, dp, tensor,
@@ -351,7 +360,7 @@
 
 
 def recurrent_kernel(index, dp_index, weight, bias, counts, slots, resets, *refs):
-    *pieces, out, chosen, hidden, held, sems = refs
+    *pieces, out, chosen, back, hidden, held, sems = refs
     gates, share, _ = weight.shape
     slot_count, tall, _ = held.shape
     chunks = gates * share // tall
@@ -365,8 +374,8 @@
         copy(i).start()
     tensor, dp = counts.shape
     width, places = pieces[0].shape
-    for back, piece in enumerate(pieces):
-        low = pl.multiple_of(((index() - back) & (tensor - 1)) * width, width)
+    for behind, piece in enumerate(pieces):
+        low = pl.multiple_of(((index() - behind) & (tensor - 1)) * width, width)
         hidden[pl.ds(low, width), :] = piece[...]
 
     rows, count = chosen.shape[0], slots.shape[1]
@@ -393,6 +402,15 @@
     of_slot = one_hot(iota((places, count), 0) == slots[...])
     chosen[...] = mm(to_row, of_slot, NT).astype(BF16)
 
+    here = (iota((tensor, dp), 0) == index()) & (iota((tensor, dp), 1) == mine)
+
+    def at_home(table):
+        return jnp.sum(jnp.where(here, table, 0.0), axis=(0, 1), keepdims=True).astype(I32)
+
+    arrival = ((sender - at_home(starts)) & (dp - 1)) + level * dp
+    live = (iota(back.shape, 1) == arrival) & (arrival < at_home(tallies))
+    back[...] = jnp.where(live, 1.0, 0.0)
+
     keep = 1.0 - resets[...].astype(F32)
     for i in range(chunks):
         q, low = divmod(i * tall, share)
@@ -403,7 +421,7 @@
         out[i * tall : (i + 1) * tall, :] = mm(held[i % slot_count], hidden[...]) * keep + column
 
 
-def recurrent(weight, bias, counts, slots, resets, pieces, rows):
+def recurrent(weight, bias, counts, slots, resets, pieces, rows, cap):
     gates, share, hidden = weight.shape
     places = pieces[0].shape[1]
     return pl.pallas_call(
@@ -412,13 +430,14 @@
         out_shape=(
             jax.ShapeDtypeStruct((gates * share, places), F32),
             jax.ShapeDtypeStruct((rows, places), BF16),
+            jax.ShapeDtypeStruct((rows, cap), F32),
         ),
         in_specs=[HBM] + [VMEM] * (4 + len(pieces)),
-        out_specs=(VMEM, VMEM),
+        out_specs=(VMEM, VMEM, VMEM),
         scratch_shapes=[
             pltpu.VMEM((hidden, places), BF16),
-            pltpu.VMEM((4, share // 2, hidden), BF16),
-            pltpu.SemaphoreType.DMA((4,)),
+            pltpu.VMEM((6, share // 2, hidden), BF16),
+            pltpu.SemaphoreType.DMA((6,)),
         ],
         compiler_params=pltpu.CompilerParams(vmem_limit_bytes=24 << 20),
         cost_estimate=pl.CostEstimate(
@@ -466,35 +485,19 @@
     )(features, sums, chosen, weight, hidden, cell, heads, resets)
 
 
-def answers_kernel(tensor, dp_index, tensor_index, counts, received, out):
-    dp = counts.shape[1]
-    rows, cap = received.shape[0], out.shape[1]
-    depth = cap // dp
-    start = jnp.int32(0)
-    for a in range(dp):
-        start = start + jnp.where(a < dp_index(), counts[tensor_index(), a], 0)
-    own = counts[tensor_index(), dp_index()]
-    line = iota((rows, cap), 0)
-    giver, level = line >> log2(tensor * depth), line & (depth - 1)
-    arrival = ((giver - start) & (dp - 1)) + level * dp
-    place = jnp.where((iota((rows, cap), 1) == arrival) & (arrival < own), 1.0, 0.0)
-    out[...] = mm(received[...], place, TN, precision=lax.Precision.HIGHEST)
-
-
-def answers(counts, received, cap):
+def answers_kernel(received, back, out):
+    out[...] = mm(received[...], back[...], TN, precision=lax.Precision.HIGHEST)
+
+
+def answers(received, back):
     return pl.pallas_call(
-        functools.partial(
-            answers_kernel,
-            counts.shape[0],
-            lambda: lax.axis_index("dp"),
-            lambda: lax.axis_index("tensor"),
-        ),
+        answers_kernel,
         name="answers",
-        out_shape=jax.ShapeDtypeStruct((received.shape[1], cap), F32),
-        in_specs=[SMEM, VMEM],
+        out_shape=jax.ShapeDtypeStruct((received.shape[1], back.shape[1]), F32),
+        in_specs=[VMEM, VMEM],
         out_specs=VMEM,
         compiler_params=pltpu.CompilerParams(vmem_limit_bytes=8 << 20),
-    )(counts, received)
+    )(received, back)
 
 
 def body(
@@ -513,12 +516,14 @@
     features, pieces = lax.optimization_barrier((features, pieces))
     features = lax.all_to_all(features, ("dp", "tensor"), 0, 0, tiled=True)
     rows = features.shape[0] * features.shape[1]
-    sums, chosen = recurrent(recur_weight, gate_bias, counts, slot_ids, reset_flags, pieces, rows)
+    sums, chosen, back = recurrent(
+        recur_weight, gate_bias, counts, slot_ids, reset_flags, pieces, rows, frames.shape[0]
+    )
     sent, hidden_after, cell_after = core(
         features, sums, chosen, input_weight, hidden_state, cell_state, head_weight, reset_flags
     )
     received = lax.all_to_all(sent, ("dp", "tensor"), 0, 0, tiled=True)
-    return answers(counts, received, frames.shape[0]), hidden_after, cell_after
+    return answers(received, back), hidden_after, cell_after
 
 
 def solution(mesh):

time: 48.2 us -> 46.7 us (0.969)
  Pallas kernels: 22.3 us -> 15.1 us
  starting transfers between devices: 11.2 us -> 14.9 us
  waiting for transfers between devices: 2.16 us -> 4.67 us
    pallas_call x1, Pallas kernels: 14.3 us -> 7.77 us  [encode_rows(): pl.pallas_call(body, name='encoder', out_shape=jax.ShapeDtypeStruct((dp *...]
    all_to_all x1, starting transfers between devices: 5.06 us -> 8.8 us  [body(): features = lax.all_to_all(features, ('dp', 'tensor'), 0, 0, tiled=True)]
    ppermute x3, waiting for transfers between devices: 0.01 us -> 2.4 us  [body(): lax.ppermute(own, 'tensor', [(i, (i + back) % tensor) for i in range(tens...]
    pallas_call x1, Pallas kernels: 1.39 us -> 0.82 us  [answers(): pl.pallas_call(answers_kernel, name='answers', out_shape=jax.ShapeDtypeSt...]
  transfers between devices with their start and end apart: 4 -> 4, of which waited for: 1 -> 2; matrix products, arithmetic and copies ran while one was open for 0% -> 0% of each run, Pallas kernels for 40% -> 27%
where the time goes in v8:
time: 46.7 us; the launch traced here: 47.4 us
  Pallas kernels  15.1 us (32%)
  starting transfers between devices  14.9 us (32%)
  blocking collectives  10.9 us (23%)
  waiting for transfers between devices  4.67 us (10%)
  other arithmetic  0.97 us (2%)
  between operations  0.75 us (2%)
    all_to_all x1, blocking collectives, body(): received = lax.all_to_all(sent, ('dp', 'tensor'), 0, 0, tiled=True)  10.9 us
    all_to_all x1, starting transfers between devices, body(): features = lax.all_to_all(features, ('dp', 'tensor'), 0, 0, tiled=True)  8.8 us
    pallas_call x1, Pallas kernels, encode_rows(): pl.pallas_call(body, name='encoder', out_shape=jax.ShapeDtypeStruct((dp *...  7.77 us
    ppermute x3, starting transfers between devices, body(): lax.ppermute(own, 'tensor', [(i, (i + back) % tensor) for i in range(tens...  6.14 us
    pallas_call x1, Pallas kernels, recurrent(): pl.pallas_call(functools.partial(recurrent_kernel, lambda: lax.axis_index...  5.13 us
    ppermute x3, waiting for transfers between devices, body(): lax.ppermute(own, 'tensor', [(i, (i + back) % tensor) for i in range(tens...  2.4 us
    all_to_all x1, waiting for transfers between devices, body(): features = lax.all_to_all(features, ('dp', 'tensor'), 0, 0, tiled=True)  2.27 us
    pallas_call x1, Pallas kernels, core(): pl.pallas_call(core_kernel, name='core', out_shape=(jax.ShapeDtypeStruct(...  1.38 us
  transfers between devices with their start and end apart: 4, of which 2 were waited for; matrix products, arithmetic and copies ran while one was open for 0% of the time, Pallas kernels for 27%

profile of v8, /device:TPU:0, one launch (start us, length us, event | category | flops | bytes accessed | tf_op | source)
XLA Modules:
  0.0 47.4 jit_solution(1852341943817578875)
XLA Ops:
  0.6 1.0 %convert_element_type.3.refs_0_ = bf16[512,128]{1,0:T(8,128)(2,1)S(1)} convert(f32[512,128]{1,0:T(8,128)} %hidden.1) | non-fusion elementwise | flops 65536 | bytes 393216 | tf_op jit(solution)/shard_map/convert_element_type | solution.py:509
  1.6 5.1 %collective-permute-start.2 = (bf16[512,128]{1,0:T(8,128)(2,1)S(1)}, bf16[512,128]{1,0:T(8,128)(2,1)S(1)}, u32[]{:S(2)}, u32[]{:S(2)}) collective-permute-start(bf16[512,128]{1,0:T(8,128)(2,1)S(1)} %convert_element_type.3.refs_0_), channel_id=1, source_target_pairs={{0,3},{1,0},{2,1},{3,2},{4,7},{5,4},{6,5},{7,6},{8,11},{9,8},{10,9... | collective-permute-start | bytes 393224 | tf_op jit(solution)/shard_map/ppermute | solution.py:511
  6.7 0.0 collective-permute-start.1
  6.7 1.0 %collective-permute-start = (bf16[512,128]{1,0:T(8,128)(2,1)S(1)}, bf16[512,128]{1,0:T(8,128)(2,1)S(1)}, u32[]{:S(2)}, u32[]{:S(2)}) collective-permute-start(bf16[512,128]{1,0:T(8,128)(2,1)S(1)} %convert_element_type.3.refs_0_), channel_id=1, source_target_pairs={{0,1},{1,2},{2,3},{3,0},{4,5},{5,6},{6,7},{7,4},{8,9},{9,10},{10,1... | collective-permute-start | bytes 393224 | tf_op jit(solution)/shard_map/ppermute | solution.py:511
  7.7 0.0 copy-start.4
  7.7 0.0 copy-start.5
  7.7 0.0 copy-start.6
  7.8 0.0 copy-start.7
  7.8 7.8 %encoder.1 = bf16[32,4,256]{2,1,0:T(4,128)(2,1)} custom-call(s32[4,8]{1,0:T(4,128)} %counts.1, bf16[3,3,4,16]{3,2,1,0:T(4,128)(2,1)} %bitcast.19, bf16[3,3,16,32]{3,2,1,0:T(8,128)(2,1)} %bitcast.18, bf16[3,3,32,32]{3,2,1,0:T(8,128)(2,1)} %bitcast.15, bf16[3,3,32,32]{3,2,1,0:T(8,128)(2,1)} %bitcast.16, bf16[3,3,32,32]{3,2,1,0:T(8,128)(2,1)} %bitcast.17, ...), custom_call_target="tpu_custom_call" | custom-call | flops 20000000000 | bytes 8000000 | tf_op jit(solution)/shard_map/encoder/pallas_call | solution.py:350
  15.5 0.0 collective-permute-done.2.refs_3_
  15.5 2.4 %collective-permute-done.1.refs_2_ = bf16[512,128]{1,0:T(8,128)(2,1)S(1)} collective-permute-done((bf16[512,128]{1,0:T(8,128)(2,1)S(1)}, bf16[512,128]{1,0:T(8,128)(2,1)S(1)}, u32[]{:S(2)}, u32[]{:S(2)}) %collective-permute-start.1) | collective-permute-done | bytes 131104 | tf_op jit(solution)/shard_map/ppermute | solution.py:511
  17.9 0.0 collective-permute-done.refs_1_
  17.9 8.8 %all-to-all-start = ((bf16[32,4,256]{2,1,0:T(4,128)(2,1)}), bf16[32,4,256]{2,1,0:T(4,128)(2,1)S(1)}, u32[]{:S(2)}, u32[]{:S(2)}) async-start(bf16[32,4,256]{2,1,0:T(4,128)(2,1)} %encoder.1), calls=%async_computation | async-start | bytes 131072 | tf_op jit(solution)/shard_map/all_to_all | solution.py:517
  26.8 0.0 copy-done.4
  26.8 0.0 copy-done.5
  26.8 0.0 copy-done.6
  26.8 0.0 copy-done.7
  26.8 0.0 copy-start
  26.8 0.0 copy-start.1
  26.8 0.0 copy-start.2
  26.8 0.0 copy-start.3
  26.8 5.1 %recurrent.1 = (f32[2048,128]{1,0:T(8,128)S(1)}, bf16[128,128]{1,0:T(8,128)(2,1)S(1)}, f32[128,32]{1,0:T(8,128)S(1)}) custom-call(bf16[4,512,2048]{2,1,0:T(8,128)(2,1)} %weight.2, f32[4,512]{1,0:T(4,128)S(1)} %copy-done.4, s32[4,8]{1,0:T(4,128)S(1)} %copy-done.5, s32[1,64]{1,0:T(1,128)S(1)} %copy-done.7, s32[1,128]{1,0:T(1,128)S(1)} %copy-done.6, ...), custom_call_target="tpu_custom_call" | custom-call | flops 1073741824 | bytes 8388608 | tf_op jit(solution)/shard_map/recurrent/pallas_call | solution.py:427
  32.0 2.3 %all-to-all-done.features = bf16[32,4,256]{2,1,0:T(4,128)(2,1)S(1)} async-done(((bf16[32,4,256]{2,1,0:T(4,128)(2,1)}), bf16[32,4,256]{2,1,0:T(4,128)(2,1)S(1)}, u32[]{:S(2)}, u32[]{:S(2)}) %all-to-all-start) | async-done | bytes 65568 | tf_op jit(solution)/shard_map/all_to_all | solution.py:517
  34.2 0.0 copy-done
  34.3 0.0 copy-done.1
  34.3 0.0 copy-done.2
  34.3 0.0 copy-done.3
  34.3 1.4 %core.1 = (f32[128,19]{1,0:T(8,128)S(1)}, f32[512,128]{1,0:T(8,128)}, f32[512,128]{1,0:T(8,128)}) custom-call(bf16[32,4,256]{2,1,0:T(4,128)(2,1)S(1)} %all-to-all-done.features, f32[2048,128]{1,0:T(8,128)S(1)} %get-tuple-element.19.sums, bf16[128,128]{1,0:T(8,128)(2,1)S(1)} %get-tuple-element.20.chosen, bf16[4,512,256]{2,1,0:T(8,128)(2,1)S(1)} %copy-done.1, ...), custom_call_target="tpu_custom_call" | custom-call | flops 134217728 | bytes 4000000 | tf_op jit(solution)/shard_map/core/pallas_call | solution.py:471
  35.6 10.9 %all_to_all.16 = f32[32,4,19]{2,1,0:T(4,128)S(1)} all-to-all(f32[32,4,19]{2,1,0:T(4,128)S(1)} %bitcast.12), channel_id=1, replica_groups=mesh['dp'=8,'tensor'=4] {'dp','tensor'}, dimensions={0} | all-to-all | bytes 19456 | tf_op jit(solution)/shard_map/all_to_all | solution.py:525
  46.5 0.8 %answers.1 = f32[19,32]{1,0:T(8,128)} custom-call(f32[128,19]{1,0:T(8,128)S(1)} %bitcast.11, f32[128,32]{1,0:T(8,128)S(1)} %get-tuple-element.22.back), custom_call_target="tpu_custom_call" | custom-call | tf_op jit(solution)/shard_map/answers/pallas_call | solution.py:493
Async XLA Ops:
  1.6 13.9 %collective-permute-start.2 = (bf16[512,128]{1,0:T(8,128)(2,1)S(1)}, bf16[512,128]{1,0:T(8,128)(2,1)S(1)}, u32[]{:S(2)}, u32[]{:S(2)}) collective-permute-start(bf16[512,128]{1,0:T(8,128)(2,1)S(1)} %convert_element_type.3.refs_0_), channel_id=1, source_target_pairs={{0,3},{1,0},{2,1},{3,2},{4,7},{5,4},{6,5},{7,6},{8,11},{9,8},{10,9... | collective-permute-start | bytes 393224 | tf_op jit(solution)/shard_map/ppermute | solution.py:511
  6.7 11.2 %collective-permute-start.1 = (bf16[512,128]{1,0:T(8,128)(2,1)S(1)}, bf16[512,128]{1,0:T(8,128)(2,1)S(1)}, u32[]{:S(2)}, u32[]{:S(2)}) collective-permute-start(bf16[512,128]{1,0:T(8,128)(2,1)S(1)} %convert_element_type.3.refs_0_), channel_id=1, source_target_pairs={{0,2},{1,3},{2,0},{3,1},{4,6},{5,7},{6,4},{7,5},{8,10},{9,11},{10,... | collective-permute-start | bytes 393224 | tf_op jit(solution)/shard_map/ppermute | solution.py:511
  6.7 11.2 %collective-permute-start = (bf16[512,128]{1,0:T(8,128)(2,1)S(1)}, bf16[512,128]{1,0:T(8,128)(2,1)S(1)}, u32[]{:S(2)}, u32[]{:S(2)}) collective-permute-start(bf16[512,128]{1,0:T(8,128)(2,1)S(1)} %convert_element_type.3.refs_0_), channel_id=1, source_target_pairs={{0,1},{1,2},{2,3},{3,0},{4,5},{5,6},{6,7},{7,4},{8,9},{9,10},{10,1... | collective-permute-start | bytes 393224 | tf_op jit(solution)/shard_map/ppermute | solution.py:511
  7.7 19.0 %copy-start.4 = (f32[4,512]{1,0:T(4,128)S(1)}, f32[4,512]{1,0:T(4,128)}, u32[]{:S(2)}) copy-start(f32[4,512]{1,0:T(4,128)} %bias.1) | copy-start | bytes 24580
  7.7 19.0 %copy-start.5 = (s32[4,8]{1,0:T(4,128)S(1)}, s32[4,8]{1,0:T(4,128)}, u32[]{:S(2)}) copy-start(s32[4,8]{1,0:T(4,128)} %counts.1) | copy-start | bytes 388
  7.7 19.0 %copy-start.6 = (s32[1,128]{1,0:T(1,128)S(1)}, s32[1,128]{1,0:T(1,128)}, u32[]{:S(2)}) copy-start(s32[1,128]{1,0:T(1,128)} %resets.3) | copy-start | bytes 1540
  7.8 19.0 %copy-start.7 = (s32[1,64]{1,0:T(1,128)S(1)}, s32[1,64]{1,0:T(1,128)}, u32[]{:S(2)}) copy-start(s32[1,64]{1,0:T(1,128)} %slots.1) | copy-start | bytes 772
  17.9 16.3 %all-to-all-start = ((bf16[32,4,256]{2,1,0:T(4,128)(2,1)}), bf16[32,4,256]{2,1,0:T(4,128)(2,1)S(1)}, u32[]{:S(2)}, u32[]{:S(2)}) async-start(bf16[32,4,256]{2,1,0:T(4,128)(2,1)} %encoder.1), calls=%async_computation | async-start | bytes 131072 | tf_op jit(solution)/shard_map/all_to_all | solution.py:517
  26.8 7.5 %copy-start = (f32[512,128]{1,0:T(8,128)S(1)}, f32[512,128]{1,0:T(8,128)}, u32[]{:S(2)}) copy-start(f32[512,128]{1,0:T(8,128)} %hidden.1) | copy-start | bytes 786436
  26.8 7.4 %copy-start.1 = (bf16[4,512,256]{2,1,0:T(8,128)(2,1)S(1)}, bf16[4,512,256]{2,1,0:T(8,128)(2,1)}, u32[]{:S(2)}) copy-start(bf16[4,512,256]{2,1,0:T(8,128)(2,1)} %weight.3) | copy-start | bytes 3145732
  26.8 7.4 %copy-start.2 = (f32[512,128]{1,0:T(8,128)S(1)}, f32[512,128]{1,0:T(8,128)}, u32[]{:S(2)}) copy-start(f32[512,128]{1,0:T(8,128)} %cell.1) | copy-start | bytes 786436
  26.8 7.4 %copy-start.3 = (bf16[19,512]{1,0:T(8,128)(2,1)S(1)}, bf16[19,512]{1,0:T(8,128)(2,1)}, u32[]{:S(2)}) copy-start(bf16[19,512]{1,0:T(8,128)(2,1)} %heads.1) | copy-start | bytes 58372
